TPU v7x, 32 devices: a whole 2x2x4 slice. The times are simulated.
32 devices in a mesh: tm: 8 (over z, y), space: 4 (over x, core).
Axes of the slice: x: 2, y: 2, z: 4, core: 2. Of those that a mesh axis runs over, the one named last changes fastest.
Arguments:
- increments: float32 [8, 3, 512, 1024], P('tm', None, 'space'), may hold values from -6 to 6
- start_state: float32 [3, 512, 1024], P(None, 'space'), may hold values from -6 to 6
- depth: float32 [512, 1024], P('space'), may hold values from 0.5 to 1.5
- error_weight: float32 [3, 512, 1024], P(None, 'space'), may hold values from 0.25 to 1
- obs_index: int32 [8, 4096], P('tm'), may hold values from 0 to 1572863
- obs_count: int32 [8], P('tm'), may hold values from 1024 to 4096, as said below
- obs_value: float32 [8, 4096], P('tm'), may hold values from -6 to 6
- obs_weight: float32 [8, 4096], P('tm'), may hold values from 0.5 to 2
Outputs:
- analysis: float32 [8, 3, 512, 1024], P('tm', None, 'space')
- costs: float32 [2, 8], P(None, 'tm')
Inputs may be any that keep to these rules, and one draw needn't show every extreme that they name: Only the first obs_count entries of a subwindow's observation rows are live; some subwindow has all 4096 live.
All inputs are finite; a program needn't handle non-finite values.
Results may differ from a plain program's by a relative error of at most 0.0001.
Values sent between devices are 32-bit elements; how exact they have to be, the bound alone decides.
No kernel may reach another device: no remote copies, remote signals or barrier semaphores. Data moves between devices by JAX's collectives and lax.ppermute only.
A program may use at most 128 MiB of HBM per device.

v0:
```python
import math

import jax
import jax.numpy as jnp
from jax import lax
from jax.experimental import pallas as pl
from jax.experimental.pallas import tpu as pltpu
from jax.sharding import PartitionSpec as P

STEPS = 6
ITERS = 2
COURANT = 0.35
CORIOLIS_MAX = 0.2
STEP_SIZE = 0.2

SUB = 8
LANE = 128
NEAR = 16
FAR = 24
GROUPS = 4
HALF = 0.5 * COURANT


def tile_rows(i):
    return pl.ds(SUB * i, SUB)


def wide(tile, width):
    return jnp.concatenate([tile] * (width // LANE), axis=1)


def raw_lon(x):
    width = x.shape[1]
    return pltpu.roll(x, width - 1, 1) - pltpu.roll(x, 1, 1)


class LatDiff:
    def __init__(self, count, width):
        row = lax.broadcasted_iota(jnp.int32, (SUB, width), 0)
        self.first, self.last = row == 0, row == SUB - 1
        self.count, self.up, self.down = count, {}, {}

    def put(self, i, x):
        self.up[i] = pltpu.roll(x, SUB - 1, 0)
        self.down[i] = pltpu.roll(x, 1, 0)

    def at(self, i):
        above = self.up[min(i + 1, self.count - 1)]
        below = self.down[max(i - 1, 0)]
        return jnp.where(self.last, above, self.up[i]) - jnp.where(
            self.first, below, self.down[i]
        )


def sweep(state, depth, rate, off, halo, edge_ref, forward):
    count = state.shape[1] // SUB
    width = state.shape[2]
    north, south = halo // SUB - 1, count - halo // SUB

    def one(_, carry):
        first, second = LatDiff(count, width), LatDiff(count, width)

        def coef(i):
            return depth[pl.ds(off + SUB * i, SUB), :]

        def rot(i):
            return wide(rate[pl.ds(off + SUB * i, SUB), :], width)

        def masked(i, x):
            if i == north:
                return x * edge_ref[0]
            if i == south:
                return x * edge_ref[1]
            return x

        def prepare(i):
            v = state[1, tile_rows(i), :]
            first.put(i, coef(i) * v if forward else v)

        def stage_a(i):
            if i + 1 < count:
                prepare(i + 1)
            if forward:
                flow = coef(i) * state[0, tile_rows(i), :]
                new = state[2, tile_rows(i), :] - (raw_lon(flow) + first.at(i))
            else:
                mix = state[0, tile_rows(i), :] - rot(i) * state[1, tile_rows(i), :]
                state[0, tile_rows(i), :] = mix
                new = state[2, tile_rows(i), :] + (raw_lon(mix) + first.at(i))
            new = masked(i, new)
            state[2, tile_rows(i), :] = new
            second.put(i, new)

        def stage_b(i):
            new = state[2, tile_rows(i), :]
            u, v = state[0, tile_rows(i), :], state[1, tile_rows(i), :]
            if forward:
                u = u + rot(i) * v - raw_lon(new)
                v = v - rot(i) * u - second.at(i)
                state[0, tile_rows(i), :] = u
                state[1, tile_rows(i), :] = v
            else:
                state[0, tile_rows(i), :] = u + coef(i) * raw_lon(new)
                state[1, tile_rows(i), :] = v + rot(i) * u + coef(i) * second.at(i)

        prepare(0)
        for i in range(count):
            stage_a(i)
            if i > 0:
                stage_b(i - 1)
        stage_b(count - 1)
        return carry

    lax.fori_loop(0, STEPS, one, 0)


def gap_kernel(
    own_lo,
    flags,
    own_e,
    own_m,
    mid_e,
    mid_m,
    far_e,
    far_m,
    from_north,
    from_south,
    start,
    depth,
    rate,
    weight,
    obs_a,
    obs_b,
    lam_out,
    part_out,
    cost_out,
    lo,
    mid,
    kept,
    hi,
    depth_v,
    rate_v,
    weight_v,
    a_v,
    b_v,
    sems,
):
    rows = kept.shape[1]
    inner = rows - 2 * FAR
    width = kept.shape[2]

    def assemble(dst, halo, e, m, at, slot):
        pieces = [
            (from_north.at[:, pl.ds(at, halo), :], 0, halo),
            (e.at[:, pl.ds(0, FAR), :], halo, FAR),
            (m, halo + FAR, inner),
            (e.at[:, pl.ds(FAR, FAR), :], halo + FAR + inner, FAR),
            (from_south.at[:, pl.ds(at, halo), :], halo + rows, halo),
        ]
        return [
            pltpu.make_async_copy(src, dst.at[:, pl.ds(where, size), :], sems.at[slot + n])
            for n, (src, where, size) in enumerate(pieces)
        ]

    own_at, mid_at, far_at = 0, NEAR, NEAR + FAR
    is_own_lo = own_lo[0] == 1
    c_depth = pltpu.make_async_copy(depth, depth_v, sems.at[0])
    c_rate = pltpu.make_async_copy(rate, rate_v, sems.at[1])
    c_mid = assemble(mid, FAR, mid_e, mid_m, mid_at, 2)
    lo_own = assemble(lo, NEAR, own_e, own_m, own_at, 7)
    lo_far = assemble(lo, NEAR, far_e, far_m, far_at, 7)
    hi_own = assemble(hi, NEAR, own_e, own_m, own_at, 12)
    hi_far = assemble(hi, NEAR, far_e, far_m, far_at, 12)
    c_kept = [
        pltpu.make_async_copy(mid_e.at[:, pl.ds(0, FAR), :], kept.at[:, pl.ds(0, FAR), :], sems.at[17]),
        pltpu.make_async_copy(mid_m, kept.at[:, pl.ds(FAR, inner), :], sems.at[18]),
        pltpu.make_async_copy(
            mid_e.at[:, pl.ds(FAR, FAR), :], kept.at[:, pl.ds(FAR + inner, FAR), :], sems.at[19]
        ),
    ]
    c_weight = pltpu.make_async_copy(weight, weight_v, sems.at[20])
    c_a = pltpu.make_async_copy(obs_a, a_v, sems.at[21])
    c_b = pltpu.make_async_copy(obs_b, b_v, sems.at[22])
    c_depth.start()
    c_rate.start()
    for c in c_mid:
        c.start()

    @pl.when(is_own_lo)
    def _():
        for c in lo_own + hi_far:
            c.start()

    @pl.when(jnp.logical_not(is_own_lo))
    def _():
        for c in lo_far + hi_own:
            c.start()

    for c in c_kept + [c_weight, c_a, c_b]:
        c.start()

    c_depth.wait()
    c_rate.wait()
    for c in c_mid:
        c.wait()

    def scale_third(ref, factor):
        for i in range(ref.shape[1] // SUB):
            ref[2, tile_rows(i), :] = ref[2, tile_rows(i), :] * factor

    scale_third(mid, HALF)
    sweep(mid, depth_v, rate_v, 0, FAR, flags, True)
    for c in lo_own:
        c.wait()

    scale_third(lo, HALF)
    sweep(lo, depth_v, rate_v, FAR - NEAR, NEAR, flags, True)
    for c in hi_own + [c_weight]:
        c.wait()

    for part in range(3):
        back_scale = 1.0 / HALF if part == 2 else 1.0
        for i in range(lam_out.shape[1] // SUB):
            end = mid[part, pl.ds(FAR - NEAR + SUB * i, SUB), :] * back_scale
            lam = weight_v[part, tile_rows(i), :] * (hi[part, tile_rows(i), :] - end)
            lam_out[part, tile_rows(i), :] = lam * (flags[2] * back_scale)

    for c in c_kept + [c_a, c_b]:
        c.wait()

    @pl.when(flags[3] > 0.5)
    def _():
        c = pltpu.make_async_copy(start, lo.at[:, pl.ds(NEAR, rows), :], sems.at[0])
        c.start()
        c.wait()
        for i in range(rows // SUB):
            at = pl.ds(NEAR + SUB * i, SUB)
            lo[2, at, :] = lo[2, at, :] * HALF

    model = jnp.zeros((SUB, width), jnp.float32)
    fit = jnp.zeros((SUB, width), jnp.float32)
    for part in range(3):
        back_scale = 1.0 / HALF if part == 2 else 1.0
        for i in range(rows // SUB):
            here = kept[part, tile_rows(i), :]
            near = pl.ds(NEAR + SUB * i, SUB)
            gap = here - lo[part, near, :] * back_scale
            lam = weight_v[part, near, :] * gap
            pull = a_v[part, tile_rows(i), :] * here
            model = model + lam * gap
            fit = fit + here * (pull - 2.0 * b_v[part, tile_rows(i), :])
            part_out[part, tile_rows(i), :] = here - STEP_SIZE * (
                lam + (pull - b_v[part, tile_rows(i), :])
            )
    total = model + fit
    folded = total[:, :LANE]
    for n in range(1, width // LANE):
        folded = folded + total[:, n * LANE : (n + 1) * LANE]
    cost_out[...] = folded


def step_kernel(flags, lam, part, depth, rate, edge_out, mid_out, work):
    rows, width = part.shape[1], part.shape[2]
    work[...] = lam[...]
    sweep(work, depth, rate, FAR - NEAR, NEAR, flags, False)
    for c in range(3):
        scale = STEP_SIZE * (HALF if c == 2 else 1.0)
        for i in range(rows // SUB):
            new = part[c, tile_rows(i), :] + scale * work[c, pl.ds(NEAR + SUB * i, SUB), :]
            if SUB * i < FAR:
                edge_out[c, tile_rows(i), :] = new
            elif SUB * i < rows - FAR:
                mid_out[c, pl.ds(SUB * i - FAR, SUB), :] = new
            else:
                edge_out[c, pl.ds(SUB * i - rows + 2 * FAR, SUB), :] = new


def final_kernel(flags, lam, part, depth, rate, out, work):
    rows = part.shape[1]
    work[...] = lam[...]
    sweep(work, depth, rate, FAR - NEAR, NEAR, flags, False)
    for c in range(3):
        scale = STEP_SIZE * (HALF if c == 2 else 1.0)
        for i in range(rows // SUB):
            out[c, tile_rows(i), :] = (
                part[c, tile_rows(i), :] + scale * work[c, pl.ds(NEAR + SUB * i, SUB), :]
            )


def deposit_kernel(code, load, value, a_out, b_out, *acc):
    a_acc, b_acc = acc[:GROUPS], acc[GROUPS:]
    chunks = a_out.shape[1] // LANE
    zero = jnp.zeros((SUB, LANE), jnp.float32)
    rows = a_out.shape[0]

    def clear(r, c):
        for ref in acc:
            for n in range(SUB):
                ref[pl.ds(pl.multiple_of((r * SUB + n) * SUB, SUB), SUB), :] = zero
        return c

    lax.fori_loop(0, rows // SUB, clear, 0)
    column = lax.broadcasted_iota(jnp.int32, (SUB, LANE), 0) * LANE + lax.broadcasted_iota(
        jnp.int32, (SUB, LANE), 1
    )
    shift = (chunks * LANE).bit_length() - 1

    def body(n, c):
        for g in range(GROUPS):
            i = n * GROUPS + g
            word = code[i]
            at = pl.ds(pl.multiple_of((word >> shift) * SUB, SUB), SUB)
            hit = column == (word & (chunks * LANE - 1))
            a_acc[g][at, :] = a_acc[g][at, :] + jnp.where(hit, load[i], 0.0)
            b_acc[g][at, :] = b_acc[g][at, :] + jnp.where(hit, value[i], 0.0)
        return c

    lax.fori_loop(0, code.shape[0] // GROUPS, body, 0, unroll=4)

    def gather(t, c):
        at = pl.ds(pl.multiple_of(t * SUB, SUB), SUB)
        for s in range(chunks):
            def total(refs):
                picked = [ref[pl.ds(t * SUB * SUB + s, SUB, stride=SUB), :] for ref in refs]
                return (picked[0] + picked[1]) + (picked[2] + picked[3])

            a_out[at, pl.ds(s * LANE, LANE)] = total(a_acc)
            b_out[at, pl.ds(s * LANE, LANE)] = total(b_acc)
        return c

    lax.fori_loop(0, rows // SUB, gather, 0)


def per_device(
    increments, start_state, depth, error_weight, obs_index, obs_count, obs_value, obs_weight
):
    _, comps, rows, lon = increments.shape
    bands = lax.axis_size("space")
    windows = lax.axis_size("tm")
    band = lax.axis_index("space")
    me = lax.axis_index("tm")
    even = me % 2 == 0
    total_rows = rows * bands
    first_row = band * rows
    f32 = jnp.float32
    any_space = pl.BlockSpec(memory_space=pl.ANY)
    smem = pl.BlockSpec(memory_space=pltpu.SMEM)
    vmem = pl.BlockSpec(memory_space=pltpu.VMEM)

    swap = [(i, i ^ 1) for i in range(windows)]
    inward = [(i, i - 2) for i in range(2, windows) if i % 2 == 0] + [
        (i, i + 2) for i in range(windows - 2) if i % 2 == 1
    ]
    outward = [(b, a) for a, b in inward]
    southward = [(i, i + 1) for i in range(bands - 1)]
    northward = [(b, a) for a, b in southward]

    index = obs_index[0]
    plane = total_rows * lon
    component = index // plane
    remainder = index % plane
    local = remainder // lon - first_row
    kept = (local >= 0) & (local < rows) & (jnp.arange(index.shape[0]) < obs_count[0])
    code = jnp.where(kept, (component * rows + local) * lon + remainder % lon, comps * rows * lon)
    load = jnp.where(kept, obs_weight[0], 0.0)
    pulled = load * obs_value[0]
    own_list = jnp.stack([code.astype(f32), load, pulled])
    own_const = jnp.sum(pulled * obs_value[0])
    other_list = lax.ppermute(own_list, "tm", swap)

    deposit = pl.pallas_call(
        deposit_kernel,
        in_specs=[smem] * 3,
        out_specs=[vmem] * 2,
        out_shape=[jax.ShapeDtypeStruct((comps * rows, lon), f32)] * 2,
        scratch_shapes=[pltpu.VMEM(((comps * rows + SUB) * SUB, LANE), f32)] * (2 * GROUPS),
        cost_estimate=pl.CostEstimate(flops=40_000_000, bytes_accessed=0, transcendentals=0),
        name="deposit",
    )

    def deposited(words, scale, value):
        a, b = deposit(words, scale, value)
        return a.reshape(comps, rows, lon), b.reshape(comps, rows, lon)

    def beside(block, size):
        return block[:, rows - size :], block[:, :size]

    weight_s, weight_n = beside(error_weight, NEAR)
    depth_s, depth_n = beside(depth[None], FAR)
    flat = lambda w, d: jnp.concatenate([w.reshape(-1, lon), d[0]], 0)
    const_n = lax.ppermute(flat(weight_s, depth_s), "space", southward)
    const_s = lax.ppermute(flat(weight_n, depth_n), "space", northward)
    split = comps * NEAR
    shaped = lambda c: c[:split].reshape(comps, NEAR, lon)
    weight_wide = jnp.concatenate([shaped(const_n), error_weight, shaped(const_s)], 1)
    depth_wide = (HALF * HALF) * jnp.concatenate([const_n[split:], depth, const_s[split:]], 0)
    latitude = (
        (first_row - FAR + jnp.arange(rows + 2 * FAR)).astype(f32) + 0.5
    ) / total_rows * math.pi - math.pi / 2
    rate_wide = jnp.broadcast_to(
        (CORIOLIS_MAX * jnp.sin(latitude))[:, None], (rows + 2 * FAR, LANE)
    )

    near_rows, far_rows = rows + 2 * NEAR, rows + 2 * FAR
    gap_call = pl.pallas_call(
        gap_kernel,
        in_specs=[smem, smem] + [any_space] * 14,
        out_specs=[vmem] * 3,
        out_shape=[
            jax.ShapeDtypeStruct((comps, near_rows, lon), f32),
            jax.ShapeDtypeStruct((comps, rows, lon), f32),
            jax.ShapeDtypeStruct((SUB, LANE), f32),
        ],
        scratch_shapes=[
            pltpu.VMEM((comps, near_rows, lon), f32),
            pltpu.VMEM((comps, far_rows, lon), f32),
            pltpu.VMEM((comps, rows, lon), f32),
            pltpu.VMEM((comps, near_rows, lon), f32),
            pltpu.VMEM((far_rows, lon), f32),
            pltpu.VMEM((far_rows, LANE), f32),
            pltpu.VMEM((comps, near_rows, lon), f32),
            pltpu.VMEM((comps, rows, lon), f32),
            pltpu.VMEM((comps, rows, lon), f32),
            pltpu.SemaphoreType.DMA((23,)),
        ],
        cost_estimate=pl.CostEstimate(flops=30_000_000, bytes_accessed=0, transcendentals=0),
        name="gaps",
    )
    step_cost = pl.CostEstimate(flops=15_000_000, bytes_accessed=0, transcendentals=0)
    step_call = pl.pallas_call(
        step_kernel,
        in_specs=[smem] + [vmem] * 4,
        out_specs=[vmem] * 2,
        out_shape=[
            jax.ShapeDtypeStruct((comps, 2 * FAR, lon), f32),
            jax.ShapeDtypeStruct((comps, rows - 2 * FAR, lon), f32),
        ],
        scratch_shapes=[pltpu.VMEM((comps, near_rows, lon), f32)],
        cost_estimate=step_cost,
        name="step",
    )
    final_call = pl.pallas_call(
        final_kernel,
        in_specs=[smem] + [vmem] * 4,
        out_specs=vmem,
        out_shape=jax.ShapeDtypeStruct((comps, rows, lon), f32),
        scratch_shapes=[pltpu.VMEM((comps, near_rows, lon), f32)],
        cost_estimate=step_cost,
        name="final",
    )

    own = increments[0]
    edge = jnp.concatenate([own[:, :FAR], own[:, rows - FAR :]], 1)
    inner = own[:, FAR : rows - FAR]
    costs = []
    for turn in range(ITERS):
        away = turn % 2 == 0
        target = (me ^ 1) if away else me
        shift = inward if away else outward
        mid_e = lax.ppermute(edge, "tm", swap)
        far_e = lax.ppermute(edge, "tm", shift)
        mid_m = lax.ppermute(inner, "tm", swap)
        far_m = lax.ppermute(inner, "tm", shift)
        words, scale, value = other_list if away else own_list
        obs_a, obs_b = deposited(words.astype(jnp.int32), scale, value)
        from_north = lax.ppermute(
            jnp.concatenate(
                [edge[:, 2 * FAR - NEAR :], mid_e[:, FAR:], far_e[:, 2 * FAR - NEAR :]], 1
            ),
            "space",
            southward,
        )
        from_south = lax.ppermute(
            jnp.concatenate([edge[:, :NEAR], mid_e[:, :FAR], far_e[:, :NEAR]], 1),
            "space",
            northward,
        )
        own_lo = (even if away else ~even).astype(jnp.int32).reshape(1)
        flags = jnp.stack(
            [band > 0, band < bands - 1, target < windows - 1, target == 0]
        ).astype(f32)
        lam, part, cost = gap_call(
            own_lo,
            flags,
            edge,
            inner,
            mid_e,
            mid_m,
            far_e,
            far_m,
            from_north,
            from_south,
            start_state,
            depth_wide,
            rate_wide,
            weight_wide,
            obs_a,
            obs_b,
        )
        cost = jnp.sum(cost)
        costs.append(lax.ppermute(cost, "tm", swap) if away else cost)
        if turn < ITERS - 1:
            edge, inner = step_call(flags, lam, part, depth_wide, rate_wide)
        else:
            state = final_call(flags, lam, part, depth_wide, rate_wide)
    sums = (jnp.stack(costs) + own_const).reshape(1, ITERS)
    sums = jnp.pad(sums, ((0, 0), (0, LANE - ITERS)))
    spread = sums
    for turn in range(1, bands):
        ring = [(i, (i + turn) % bands) for i in range(bands)]
        spread = spread + lax.ppermute(sums, "space", ring)
    cells = comps * total_rows * lon
    return state[None], (0.5 / cells) * spread[0, :ITERS, None]


def solution(mesh):
    placed = (
        P("tm", None, "space", None),
        P(None, "space", None),
        P("space", None),
        P(None, "space", None),
        P("tm", None),
        P("tm"),
        P("tm", None),
        P("tm", None),
    )
    return jax.shard_map(
        per_device,
        mesh=mesh,
        in_specs=placed,
        out_specs=(P("tm", None, "space", None), P(None, "tm")),
        check_vma=False,
    )
```

profile of v0, /device:TPU:0, one launch (start us, length us, event | category | flops | bytes accessed | tf_op | source)
XLA Modules:
  0.0 185.6 jit_solution(5073219754317508738)
XLA Ops:
  2.0 3.1 %collective-permute-start = (f32[3,48,1024]{2,1,0:T(8,128)S(1)}, f32[3,48,1024]{2,1,0:T(8,128)}, u32[]{:S(2)}, u32[]{:S(2)}) collective-permute-start(f32[3,48,1024]{2,1,0:T(8,128)S(1)} %pad_maximum_fusion.5.own_e), channel_id=1, source_target_pairs={{0,4},{4,0},{8,12},{12,8},{16,20},{20,16},{24,28},{28,24},{1,5},{5... | collective-permute-start | bytes 1769480 | tf_op jit(solution)/shard_map/ppermute | solution.py:460
  6.4 3.6 %collective-permute-start.1 = (f32[3,80,1024]{2,1,0:T(8,128)S(1)}, f32[3,80,1024]{2,1,0:T(8,128)}, u32[]{:S(2)}, u32[]{:S(2)}) collective-permute-start(f32[3,80,1024]{2,1,0:T(8,128)S(1)} %slice.100.own_m), channel_id=1, source_target_pairs={{0,4},{4,0},{8,12},{12,8},{16,20},{20,16},{24,28},{28,24},{1,5},{5... | collective-permute-start | bytes 2949128 | tf_op jit(solution)/shard_map/ppermute | solution.py:462
  13.0 2.7 %collective-permute-start.8 = (f32[3,4096]{1,0:T(4,128)}, f32[3,4096]{1,0:T(4,128)}, u32[]{:S(2)}, u32[]{:S(2)}) collective-permute-start(f32[3,4096]{1,0:T(4,128)} %pad_maximum_fusion.8), channel_id=1, source_target_pairs={{0,4},{4,0},{8,12},{12,8},{16,20},{20,16},{24,28},{28,24},{1,5},{5... | collective-permute-start | bytes 147464 | tf_op jit(solution)/shard_map/ppermute | solution.py:369
  16.8 1.6 slice_bitcast_fusion.1
  20.0 1.6 pad_maximum_fusion.7
  29.0 11.9 %collective-permute-done.8 = f32[3,4096]{1,0:T(4,128)} collective-permute-done((f32[3,4096]{1,0:T(4,128)}, f32[3,4096]{1,0:T(4,128)}, u32[]{:S(2)}, u32[]{:S(2)}) %collective-permute-start.8) | collective-permute-done | bytes 49184 | tf_op jit(solution)/shard_map/ppermute | solution.py:369
  40.9 2.1 %collective-permute-start.4 = (f32[3,56,1024]{2,1,0:T(8,128)}, f32[3,56,1024]{2,1,0:T(8,128)}, u32[]{:S(2)}, u32[]{:S(2)}) collective-permute-start(f32[3,56,1024]{2,1,0:T(8,128)} %pad_maximum_fusion.1), channel_id=1, source_target_pairs={{0,1},{1,2},{2,3},{4,5},{5,6},{6,7},{8,9},{9,10},{10,11},{12,13},{... | collective-permute-start | bytes 2064392 | tf_op jit(solution)/shard_map/ppermute | solution.py:466
  44.3 1.6 fusion.27
  45.9 17.8 %deposit.2 = (f32[384,1024]{1,0:T(8,128)}, f32[384,1024]{1,0:T(8,128)}) custom-call(s32[4096]{0:T(1024)} %bitcast.57, f32[4096]{0:T(1024)} %bitcast.56, f32[4096]{0:T(1024)} %bitcast.55), custom_call_target="tpu_custom_call" | custom-call | flops 40000000 | tf_op jit(solution)/shard_map/deposit/pallas_call | solution.py:382
  68.8 18.4 %gaps.2 = (f32[3,160,1024]{2,1,0:T(8,128)}, f32[3,128,1024]{2,1,0:T(8,128)}, f32[8,128]{1,0:T(8,128)}) custom-call(s32[1]{0:T(128)} %bitcast.7.own_lo, f32[4]{0:T(128)} %add_convert_fusion.1.flags, f32[3,48,1024]{2,1,0:T(8,128)} %copy-done.3, f32[3,80,1024]{2,1,0:T(8,128)} %copy-done, f32[3,48,1024]{2,1,0:T(8,128)} %collective-permute-done.mid_e, ...), custom_call_target="tpu_custom_call" | custom-call | flops 30000000 | tf_op jit(solution)/shard_map/gaps/pallas_call | solution.py:482
  87.2 10.2 %step.1 = (f32[3,48,1024]{2,1,0:T(8,128)}, f32[3,80,1024]{2,1,0:T(8,128)}) custom-call(f32[4]{0:T(128)} %add_convert_fusion.1.flags, f32[3,160,1024]{2,1,0:T(8,128)} %get-tuple-element.16.lam, f32[3,128,1024]{2,1,0:T(8,128)} %get-tuple-element.17.part, f32[176,1024]{1,0:T(8,128)} %maximum_multiply_fusion.depth, f32[176,128]{1,0:T(8,128)} %broadcast_in_dim.25.rate), custom_call_target="tpu_custom_call" | custom-call | flops 15000000 | tf_op jit(solution)/shard_map/step/pallas_call | solution.py:503
  97.4 3.2 %collective-permute-start.9 = (f32[3,48,1024]{2,1,0:T(8,128)}, f32[3,48,1024]{2,1,0:T(8,128)S(1)}, u32[]{:S(2)}, u32[]{:S(2)}) collective-permute-start(f32[3,48,1024]{2,1,0:T(8,128)} %get-tuple-element.18.own_e), channel_id=1, source_target_pairs={{0,4},{4,0},{8,12},{12,8},{16,20},{20,16},{24,28},{28,24},{1,5},{5... | collective-permute-start | bytes 1769480 | tf_op jit(solution)/shard_map/ppermute | solution.py:460
  100.6 2.1 %collective-permute-start.11 = (f32[3,48,1024]{2,1,0:T(8,128)}, f32[3,48,1024]{2,1,0:T(8,128)S(1)}, u32[]{:S(2)}, u32[]{:S(2)}) collective-permute-start(f32[3,48,1024]{2,1,0:T(8,128)} %get-tuple-element.18.own_e), channel_id=1, source_target_pairs={{0,8},{8,16},{16,24},{12,4},{20,12},{28,20},{1,9},{9,17},{17,25},{... | collective-permute-start | bytes 1769480 | tf_op jit(solution)/shard_map/ppermute | solution.py:461
  102.7 3.8 %collective-permute-start.12 = (f32[3,80,1024]{2,1,0:T(8,128)}, f32[3,80,1024]{2,1,0:T(8,128)S(1)}, u32[]{:S(2)}, u32[]{:S(2)}) collective-permute-start(f32[3,80,1024]{2,1,0:T(8,128)} %get-tuple-element.19.own_m), channel_id=1, source_target_pairs={{0,8},{8,16},{16,24},{12,4},{20,12},{28,20},{1,9},{9,17},{17,25},{... | collective-permute-start | bytes 2949128 | tf_op jit(solution)/shard_map/ppermute | solution.py:463
  107.6 6.0 %collective-permute-done.9.mid_e = f32[3,48,1024]{2,1,0:T(8,128)S(1)} collective-permute-done((f32[3,48,1024]{2,1,0:T(8,128)}, f32[3,48,1024]{2,1,0:T(8,128)S(1)}, u32[]{:S(2)}, u32[]{:S(2)}) %collective-permute-start.9) | collective-permute-done | bytes 589856 | tf_op jit(solution)/shard_map/ppermute | solution.py:460
  113.7 2.2 %collective-permute-done.11.far_e = f32[3,48,1024]{2,1,0:T(8,128)S(1)} collective-permute-done((f32[3,48,1024]{2,1,0:T(8,128)}, f32[3,48,1024]{2,1,0:T(8,128)S(1)}, u32[]{:S(2)}, u32[]{:S(2)}) %collective-permute-start.11) | collective-permute-done | bytes 589856 | tf_op jit(solution)/shard_map/ppermute | solution.py:461
  117.4 5.1 %collective-permute-start.13 = (f32[3,56,1024]{2,1,0:T(8,128)S(1)}, f32[3,56,1024]{2,1,0:T(8,128)}, u32[]{:S(2)}, u32[]{:S(2)}) collective-permute-start(f32[3,56,1024]{2,1,0:T(8,128)S(1)} %pad_maximum_fusion.3), channel_id=1, source_target_pairs={{0,1},{1,2},{2,3},{4,5},{5,6},{6,7},{8,9},{9,10},{10,11},{12,13},{... | collective-permute-start | bytes 2064392 | tf_op jit(solution)/shard_map/ppermute | solution.py:466
  124.4 17.8 %deposit.3 = (f32[384,1024]{1,0:T(8,128)}, f32[384,1024]{1,0:T(8,128)}) custom-call(s32[4096]{0:T(1024)} %fusion.9.code, f32[4096]{0:T(1024)} %get-tuple-element.28.load, f32[4096]{0:T(1024)} %get-tuple-element.27.value), custom_call_target="tpu_custom_call" | custom-call | flops 40000000 | tf_op jit(solution)/shard_map/deposit/pallas_call | solution.py:382
  143.5 2.5 %collective-permute-start.15 = (f32[]{:T(128)}, f32[]{:T(128)}, u32[]{:S(2)}, u32[]{:S(2)}) collective-permute-start(f32[]{:T(128)} %reduce_sum.27), channel_id=1, source_target_pairs={{0,4},{4,0},{8,12},{12,8},{16,20},{20,16},{24,28},{28,24},{1,5},{5... | collective-permute-start | bytes 20 | tf_op jit(solution)/shard_map/ppermute | solution.py:501
  147.4 19.9 %gaps.3 = (f32[3,160,1024]{2,1,0:T(8,128)}, f32[3,128,1024]{2,1,0:T(8,128)}, f32[8,128]{1,0:T(8,128)}) custom-call(s32[1]{0:T(128)} %bitcast.4.own_lo, f32[4]{0:T(128)} %add_convert_fusion.flags, f32[3,48,1024]{2,1,0:T(8,128)} %get-tuple-element.18.own_e, f32[3,80,1024]{2,1,0:T(8,128)} %get-tuple-element.19.own_m, f32[3,48,1024]{2,1,0:T(8,128)} %copy-done.4, ...), custom_call_target="tpu_custom_call" | custom-call | flops 30000000 | tf_op jit(solution)/shard_map/gaps/pallas_call | solution.py:482
  168.5 1.9 %maximum_add_fusion = f32[1,2]{1,0:T(1,128)S(1)} fusion(f32[1,1]{1,0:T(1,128)} %bitcast.29, f32[1,1]{1,0:T(1,128)} %bitcast.28, f32[]{:T(128)} %get-tuple-element.26), kind=kLoop, calls=%fused_computation.61 | loop fusion | flops 4 | bytes 20 | tf_op jit(solution)/shard_map/add | solution.py:506
  170.5 1.5 collective-permute-start.16
  172.0 1.6 collective-permute-start.17
  174.9 10.1 %final.1 = f32[3,128,1024]{2,1,0:T(8,128)} custom-call(f32[4]{0:T(128)} %add_convert_fusion.flags, f32[3,160,1024]{2,1,0:T(8,128)} %get-tuple-element.22.lam, f32[3,128,1024]{2,1,0:T(8,128)} %get-tuple-element.23.part, f32[176,1024]{1,0:T(8,128)} %maximum_multiply_fusion.depth, f32[176,128]{1,0:T(8,128)} %broadcast_in_dim.25.rate), custom_call_target="tpu_custom_call" | custom-call | flops 15000000 | tf_op jit(solution)/shard_map/final/pallas_call | solution.py:505
  (92 shorter events, 31.6 us)
Async XLA Ops:
  1.9 14.9 %copy-start.3 = (f32[3,48,1024]{2,1,0:T(8,128)}, f32[3,48,1024]{2,1,0:T(8,128)S(1)}, u32[]{:S(2)}) copy-start(f32[3,48,1024]{2,1,0:T(8,128)S(1)} %pad_maximum_fusion.5.own_e) | copy-start | bytes 1769476
  2.0 20.4 %collective-permute-start = (f32[3,48,1024]{2,1,0:T(8,128)S(1)}, f32[3,48,1024]{2,1,0:T(8,128)}, u32[]{:S(2)}, u32[]{:S(2)}) collective-permute-start(f32[3,48,1024]{2,1,0:T(8,128)S(1)} %pad_maximum_fusion.5.own_e), channel_id=1, source_target_pairs={{0,4},{4,0},{8,12},{12,8},{16,20},{20,16},{24,28},{28,24},{1,5},{5... | collective-permute-start | bytes 1769480 | tf_op jit(solution)/shard_map/ppermute | solution.py:460
  5.0 19.8 %collective-permute-start.2 = (f32[3,48,1024]{2,1,0:T(8,128)S(1)}, f32[3,48,1024]{2,1,0:T(8,128)}, u32[]{:S(2)}, u32[]{:S(2)}) collective-permute-start(f32[3,48,1024]{2,1,0:T(8,128)S(1)} %pad_maximum_fusion.5.own_e), channel_id=1, source_target_pairs={{8,0},{16,8},{24,16},{4,12},{12,20},{20,28},{9,1},{17,9},{25,17},{... | collective-permute-start | bytes 1769480 | tf_op jit(solution)/shard_map/ppermute | solution.py:461
  6.4 15.9 %copy-start = (f32[3,80,1024]{2,1,0:T(8,128)}, f32[3,80,1024]{2,1,0:T(8,128)S(1)}, u32[]{:S(2)}) copy-start(f32[3,80,1024]{2,1,0:T(8,128)S(1)} %slice.100.own_m) | copy-start | bytes 2949124
  6.4 61.6 %collective-permute-start.1 = (f32[3,80,1024]{2,1,0:T(8,128)S(1)}, f32[3,80,1024]{2,1,0:T(8,128)}, u32[]{:S(2)}, u32[]{:S(2)}) collective-permute-start(f32[3,80,1024]{2,1,0:T(8,128)S(1)} %slice.100.own_m), channel_id=1, source_target_pairs={{0,4},{4,0},{8,12},{12,8},{16,20},{20,16},{24,28},{28,24},{1,5},{5... | collective-permute-start | bytes 2949128 | tf_op jit(solution)/shard_map/ppermute | solution.py:462
  10.0 58.0 %collective-permute-start.3 = (f32[3,80,1024]{2,1,0:T(8,128)S(1)}, f32[3,80,1024]{2,1,0:T(8,128)}, u32[]{:S(2)}, u32[]{:S(2)}) collective-permute-start(f32[3,80,1024]{2,1,0:T(8,128)S(1)} %slice.100.own_m), channel_id=1, source_target_pairs={{8,0},{16,8},{24,16},{4,12},{12,20},{20,28},{9,1},{17,9},{25,17},{... | collective-permute-start | bytes 2949128 | tf_op jit(solution)/shard_map/ppermute | solution.py:463
  13.0 27.9 %collective-permute-start.8 = (f32[3,4096]{1,0:T(4,128)}, f32[3,4096]{1,0:T(4,128)}, u32[]{:S(2)}, u32[]{:S(2)}) collective-permute-start(f32[3,4096]{1,0:T(4,128)} %pad_maximum_fusion.8), channel_id=1, source_target_pairs={{0,4},{4,0},{8,12},{12,8},{16,20},{20,16},{24,28},{28,24},{1,5},{5... | collective-permute-start | bytes 147464 | tf_op jit(solution)/shard_map/ppermute | solution.py:369
  22.4 20.7 %collective-permute-start.6 = (f32[72,1024]{1,0:T(8,128)S(1)}, f32[72,1024]{1,0:T(8,128)S(1)}, u32[]{:S(2)}, u32[]{:S(2)}) collective-permute-start(f32[72,1024]{1,0:T(8,128)S(1)} %pad_maximum_fusion.6), channel_id=1, source_target_pairs={{0,1},{1,2},{2,3},{4,5},{5,6},{6,7},{8,9},{9,10},{10,11},{12,13},{... | collective-permute-start | bytes 884744 | tf_op jit(solution)/shard_map/ppermute | solution.py:391
  24.8 39.0 %collective-permute-start.7 = (f32[72,1024]{1,0:T(8,128)}, f32[72,1024]{1,0:T(8,128)}, u32[]{:S(2)}, u32[]{:S(2)}) collective-permute-start(f32[72,1024]{1,0:T(8,128)} %pad_maximum_fusion.7), channel_id=1, source_target_pairs={{1,0},{2,1},{3,2},{5,4},{6,5},{7,6},{9,8},{10,9},{11,10},{13,12},{... | collective-permute-start | bytes 884744 | tf_op jit(solution)/shard_map/ppermute | solution.py:392
  28.1 37.5 %copy-start.6 = (f32[128,1024]{1,0:T(8,128)S(1)}, f32[128,1024]{1,0:T(8,128)}, u32[]{:S(2)}) copy-start(f32[128,1024]{1,0:T(8,128)} %param.10) | copy-start | bytes 1572868
  29.0 37.6 %copy-start.2 = (f32[3,128,1024]{2,1,0:T(8,128)S(1)}, f32[3,128,1024]{2,1,0:T(8,128)}, u32[]{:S(2)}) copy-start(f32[3,128,1024]{2,1,0:T(8,128)} %param.11) | copy-start | bytes 4718596
  40.9 27.1 %collective-permute-start.4 = (f32[3,56,1024]{2,1,0:T(8,128)}, f32[3,56,1024]{2,1,0:T(8,128)}, u32[]{:S(2)}, u32[]{:S(2)}) collective-permute-start(f32[3,56,1024]{2,1,0:T(8,128)} %pad_maximum_fusion.1), channel_id=1, source_target_pairs={{0,1},{1,2},{2,3},{4,5},{5,6},{6,7},{8,9},{9,10},{10,11},{12,13},{... | collective-permute-start | bytes 2064392 | tf_op jit(solution)/shard_map/ppermute | solution.py:466
  43.0 25.0 %collective-permute-start.5 = (f32[3,56,1024]{2,1,0:T(8,128)}, f32[3,56,1024]{2,1,0:T(8,128)}, u32[]{:S(2)}, u32[]{:S(2)}) collective-permute-start(f32[3,56,1024]{2,1,0:T(8,128)} %pad_maximum_fusion.2), channel_id=1, source_target_pairs={{1,0},{2,1},{3,2},{5,4},{6,5},{7,6},{9,8},{10,9},{11,10},{13,12},{... | collective-permute-start | bytes 2064392 | tf_op jit(solution)/shard_map/ppermute | solution.py:473
  97.4 16.2 %collective-permute-start.9 = (f32[3,48,1024]{2,1,0:T(8,128)}, f32[3,48,1024]{2,1,0:T(8,128)S(1)}, u32[]{:S(2)}, u32[]{:S(2)}) collective-permute-start(f32[3,48,1024]{2,1,0:T(8,128)} %get-tuple-element.18.own_e), channel_id=1, source_target_pairs={{0,4},{4,0},{8,12},{12,8},{16,20},{20,16},{24,28},{28,24},{1,5},{5... | collective-permute-start | bytes 1769480 | tf_op jit(solution)/shard_map/ppermute | solution.py:460
  100.6 15.3 %collective-permute-start.11 = (f32[3,48,1024]{2,1,0:T(8,128)}, f32[3,48,1024]{2,1,0:T(8,128)S(1)}, u32[]{:S(2)}, u32[]{:S(2)}) collective-permute-start(f32[3,48,1024]{2,1,0:T(8,128)} %get-tuple-element.18.own_e), channel_id=1, source_target_pairs={{0,8},{8,16},{16,24},{12,4},{20,12},{28,20},{1,9},{9,17},{17,25},{... | collective-permute-start | bytes 1769480 | tf_op jit(solution)/shard_map/ppermute | solution.py:461
  102.6 43.4 %collective-permute-start.10 = (f32[3,80,1024]{2,1,0:T(8,128)}, f32[3,80,1024]{2,1,0:T(8,128)S(1)}, u32[]{:S(2)}, u32[]{:S(2)}) collective-permute-start(f32[3,80,1024]{2,1,0:T(8,128)} %get-tuple-element.19.own_m), channel_id=1, source_target_pairs={{0,4},{4,0},{8,12},{12,8},{16,20},{20,16},{24,28},{28,24},{1,5},{5... | collective-permute-start | bytes 2949128 | tf_op jit(solution)/shard_map/ppermute | solution.py:462
  102.7 43.3 %collective-permute-start.12 = (f32[3,80,1024]{2,1,0:T(8,128)}, f32[3,80,1024]{2,1,0:T(8,128)S(1)}, u32[]{:S(2)}, u32[]{:S(2)}) collective-permute-start(f32[3,80,1024]{2,1,0:T(8,128)} %get-tuple-element.19.own_m), channel_id=1, source_target_pairs={{0,8},{8,16},{16,24},{12,4},{20,12},{28,20},{1,9},{9,17},{17,25},{... | collective-permute-start | bytes 2949128 | tf_op jit(solution)/shard_map/ppermute | solution.py:463
  115.9 27.0 %copy-start.14 = (f32[8,128]{1,0:T(8,128)S(1)}, f32[8,128]{1,0:T(8,128)}, u32[]{:S(2)}) copy-start(f32[8,128]{1,0:T(8,128)} %get-tuple-element.24) | copy-start | bytes 12292
  115.9 30.1 %collective-permute-start.14 = (f32[3,56,1024]{2,1,0:T(8,128)S(1)}, f32[3,56,1024]{2,1,0:T(8,128)}, u32[]{:S(2)}, u32[]{:S(2)}) collective-permute-start(f32[3,56,1024]{2,1,0:T(8,128)S(1)} %pad_maximum_fusion.4), channel_id=1, source_target_pairs={{1,0},{2,1},{3,2},{5,4},{6,5},{7,6},{9,8},{10,9},{11,10},{13,12},{... | collective-permute-start | bytes 2064392 | tf_op jit(solution)/shard_map/ppermute | solution.py:473
  117.4 28.6 %collective-permute-start.13 = (f32[3,56,1024]{2,1,0:T(8,128)S(1)}, f32[3,56,1024]{2,1,0:T(8,128)}, u32[]{:S(2)}, u32[]{:S(2)}) collective-permute-start(f32[3,56,1024]{2,1,0:T(8,128)S(1)} %pad_maximum_fusion.3), channel_id=1, source_target_pairs={{0,1},{1,2},{2,3},{4,5},{5,6},{6,7},{8,9},{9,10},{10,11},{12,13},{... | collective-permute-start | bytes 2064392 | tf_op jit(solution)/shard_map/ppermute | solution.py:466
  143.5 25.0 %collective-permute-start.15 = (f32[]{:T(128)}, f32[]{:T(128)}, u32[]{:S(2)}, u32[]{:S(2)}) collective-permute-start(f32[]{:T(128)} %reduce_sum.27), channel_id=1, source_target_pairs={{0,4},{4,0},{8,12},{12,8},{16,20},{20,16},{24,28},{28,24},{1,5},{5... | collective-permute-start | bytes 20 | tf_op jit(solution)/shard_map/ppermute | solution.py:501
  170.5 14.6 %collective-permute-start.16 = (f32[1,128]{1,0:T(1,128)S(1)}, f32[1,128]{1,0:T(1,128)S(1)}, u32[]{:S(2)}, u32[]{:S(2)}) collective-permute-start(f32[1,128]{1,0:T(1,128)S(1)} %pad.4), channel_id=1, source_target_pairs={{0,1},{1,2},{2,3},{3,0},{4,5},{5,6},{6,7},{7,4},{8,9},{9,10},{10,1... | collective-permute-start | bytes 1544 | tf_op jit(solution)/shard_map/ppermute | solution.py:511
  172.0 13.1 %collective-permute-start.17 = (f32[1,128]{1,0:T(1,128)S(1)}, f32[1,128]{1,0:T(1,128)S(1)}, u32[]{:S(2)}, u32[]{:S(2)}) collective-permute-start(f32[1,128]{1,0:T(1,128)S(1)} %pad.4), channel_id=1, source_target_pairs={{0,2},{1,3},{2,0},{3,1},{4,6},{5,7},{6,4},{7,5},{8,10},{9,11},{10,... | collective-permute-start | bytes 1544 | tf_op jit(solution)/shard_map/ppermute | solution.py:511
  173.5 11.5 %collective-permute-start.18 = (f32[1,128]{1,0:T(1,128)S(1)}, f32[1,128]{1,0:T(1,128)S(1)}, u32[]{:S(2)}, u32[]{:S(2)}) collective-permute-start(f32[1,128]{1,0:T(1,128)S(1)} %pad.4), channel_id=1, source_target_pairs={{0,3},{1,0},{2,1},{3,2},{4,7},{5,4},{6,5},{7,6},{8,11},{9,8},{10,9... | collective-permute-start | bytes 1544 | tf_op jit(solution)/shard_map/ppermute | solution.py:511
  (11 other events, 59.0 us)
where the time goes:
time: 187 us; the launch traced here: 186 us
  Pallas kernels  94.1 us (50%)
  starting transfers between devices  40.5 us (22%)
  waiting for transfers between devices  20.2 us (11%)
  other arithmetic  17.8 us (10%)
  local copies, waits for them, and re-layouts  11.3 us (6%)
    pallas_call x2, Pallas kernels, per_device(): gap_call(own_lo, flags, edge, inner, mid_e, mid_m, far_e, far_m, from_nor...  38.3 us
    pallas_call x2, Pallas kernels, deposited(): a, b = deposit(words, scale, value)  35.5 us
    ppermute x1, waiting for transfers between devices, per_device(): other_list = lax.ppermute(own_list, 'tm', swap)  11.9 us
    pallas_call x1, Pallas kernels, per_device(): edge, inner = step_call(flags, lam, part, depth_wide, rate_wide)  10.2 us
    pallas_call x1, Pallas kernels, per_device(): state = final_call(flags, lam, part, depth_wide, rate_wide)  10.1 us
    ppermute x2, starting transfers between devices, per_device(): lax.ppermute(jnp.concatenate([edge[:, 2 * FAR - NEAR:], mid_e[:, FAR:], f...  7.19 us
    ppermute x2, starting transfers between devices, per_device(): mid_e = lax.ppermute(edge, 'tm', swap)  6.25 us
    ppermute x2, waiting for transfers between devices, per_device(): mid_e = lax.ppermute(edge, 'tm', swap)  6.03 us
  transfers between devices with their start and end apart: 19, of which 3 were waited for; matrix products, arithmetic and copies ran while one was open for 13% of the time, Pallas kernels for 35%

commit v1 on v0

v1 whole, which is shorter than its diff:
```python
import math

import jax
import jax.numpy as jnp
from jax import lax
from jax.experimental import pallas as pl
from jax.experimental.pallas import tpu as pltpu
from jax.sharding import PartitionSpec as P

STEPS = 6
ITERS = 2
COURANT = 0.35
CORIOLIS_MAX = 0.2
STEP_SIZE = 0.2

SUB = 8
LANE = 128
NEAR = 2 * STEPS
FAR = 4 * STEPS
GROUPS = 4
HALF = 0.5 * COURANT
LEAD = 24


def turned(x):
    return pltpu.roll(x, LANE - 1, 1), pltpu.roll(x, 1, 1)


def raw_lon(pair, first, last):
    ahead, behind = pair
    size = ahead.shape[0]
    ahead = jnp.where(last, pltpu.roll(ahead, size - 1, 0), ahead)
    behind = jnp.where(first, pltpu.roll(behind, 1, 0), behind)
    return ahead - behind


def sweep(state, depth, rate, off, halo, edge_ref, forward):
    count = rate.shape[0] - 2 * off
    size = state.shape[1] // count
    north, south = halo - 1, count - halo

    def one(_, carry):
        lane = lax.broadcasted_iota(jnp.int32, (size, LANE), 1)
        first, last = lane == 0, lane == LANE - 1
        flows, tops, pairs_a, pairs_b = {}, {}, {}, {}

        def at(r):
            return pl.ds(size * r, size)

        def coef(r):
            return depth[pl.ds(size * (off + r), size), :]

        def rot(r):
            return rate[pl.ds(off + r, 1), :]

        def masked(r, x):
            if r == north:
                return x * edge_ref[0]
            if r == south:
                return x * edge_ref[1]
            return x

        def prepare(r):
            v = state[1, at(r), :]
            flows[r] = coef(r) * v if forward else v

        def lat(values, r):
            return values[min(r + 1, count - 1)] - values[max(r - 1, 0)]

        def open_a(r):
            if forward:
                pairs_a[r] = turned(coef(r) * state[0, at(r), :])
            else:
                mix = state[0, at(r), :] - rot(r) * state[1, at(r), :]
                state[0, at(r), :] = mix
                pairs_a[r] = turned(mix)

        def close_a(r):
            if r + 1 < count:
                prepare(r + 1)
            slope = raw_lon(pairs_a.pop(r), first, last) + lat(flows, r)
            old = state[2, at(r), :]
            tops[r] = masked(r, old - slope if forward else old + slope)
            state[2, at(r), :] = tops[r]
            pairs_b[r] = turned(tops[r])

        def close_b(r):
            u, v = state[0, at(r), :], state[1, at(r), :]
            slope = raw_lon(pairs_b.pop(r), first, last)
            if r + 1 < count:
                above = state[2, at(r + 1), :]
            else:
                above = tops[r]
            rise = above - state[2, at(max(r - 1, 0)), :]
            if forward:
                u = u + rot(r) * v - slope
                state[0, at(r), :] = u
                state[1, at(r), :] = v - rot(r) * u - rise
            else:
                state[0, at(r), :] = u + coef(r) * slope
                state[1, at(r), :] = v + rot(r) * u + coef(r) * rise

        prepare(0)
        for r in range(-LEAD, count + LEAD):
            if 0 <= r + LEAD < count:
                open_a(r + LEAD)
            if 0 <= r < count:
                close_a(r)
            if 0 <= r - LEAD < count:
                close_b(r - LEAD)
        return carry

    lax.fori_loop(0, STEPS, one, 0)


def over(count, block, body):
    def step(n, carry):
        body(pl.multiple_of(n * block, SUB))
        return carry

    lax.fori_loop(0, count // block, step, 0)


def gap_kernel(
    own_lo,
    flags,
    own_e,
    own_m,
    mid_e,
    mid_m,
    far_e,
    far_m,
    from_north,
    from_south,
    start,
    depth,
    rate,
    weight,
    obs_a,
    obs_b,
    lam_out,
    part_out,
    cost_out,
    lo,
    mid,
    kept,
    hi,
    depth_v,
    rate_v,
    weight_v,
    a_v,
    b_v,
    sems,
):
    size = depth_v.shape[0] // rate_v.shape[0]
    near, far = NEAR * size, FAR * size
    band = kept.shape[1]
    inner = band - 2 * far

    def assemble(dst, halo, e, m, at, slot):
        pieces = [
            (from_north.at[:, pl.ds(at, halo), :], 0, halo),
            (e.at[:, pl.ds(0, far), :], halo, far),
            (m, halo + far, inner),
            (e.at[:, pl.ds(far, far), :], halo + far + inner, far),
            (from_south.at[:, pl.ds(at, halo), :], halo + band, halo),
        ]
        return [
            pltpu.make_async_copy(src, dst.at[:, pl.ds(where, length), :], sems.at[slot + n])
            for n, (src, where, length) in enumerate(pieces)
        ]

    own_at, mid_at, far_at = 0, near, near + far
    is_own_lo = own_lo[0] == 1
    c_depth = pltpu.make_async_copy(depth, depth_v, sems.at[0])
    c_rate = pltpu.make_async_copy(rate, rate_v, sems.at[1])
    c_mid = assemble(mid, far, mid_e, mid_m, mid_at, 2)
    lo_own = assemble(lo, near, own_e, own_m, own_at, 7)
    lo_far = assemble(lo, near, far_e, far_m, far_at, 7)
    hi_own = assemble(hi, near, own_e, own_m, own_at, 12)
    hi_far = assemble(hi, near, far_e, far_m, far_at, 12)
    c_kept = [
        pltpu.make_async_copy(
            mid_e.at[:, pl.ds(0, far), :], kept.at[:, pl.ds(0, far), :], sems.at[17]
        ),
        pltpu.make_async_copy(mid_m, kept.at[:, pl.ds(far, inner), :], sems.at[18]),
        pltpu.make_async_copy(
            mid_e.at[:, pl.ds(far, far), :], kept.at[:, pl.ds(far + inner, far), :], sems.at[19]
        ),
    ]
    c_weight = pltpu.make_async_copy(weight, weight_v, sems.at[20])
    c_a = pltpu.make_async_copy(obs_a, a_v, sems.at[21])
    c_b = pltpu.make_async_copy(obs_b, b_v, sems.at[22])
    c_depth.start()
    c_rate.start()
    for c in c_mid:
        c.start()

    @pl.when(is_own_lo)
    def _():
        for c in lo_own + hi_far:
            c.start()

    @pl.when(jnp.logical_not(is_own_lo))
    def _():
        for c in lo_far + hi_own:
            c.start()

    for c in c_kept + [c_weight, c_a, c_b]:
        c.start()

    c_depth.wait()
    c_rate.wait()
    for c in c_mid:
        c.wait()

    block = 8 * size

    def scale_third(ref, where, length):
        def body(n):
            at = pl.ds(where + n, block)
            ref[2, at, :] = ref[2, at, :] * HALF

        over(length, block, body)

    scale_third(mid, 0, mid.shape[1])
    sweep(mid, depth_v, rate_v, 0, FAR, flags, True)
    for c in lo_own:
        c.wait()

    scale_third(lo, 0, lo.shape[1])
    sweep(lo, depth_v, rate_v, FAR - NEAR, NEAR, flags, True)
    for c in hi_own + [c_weight]:
        c.wait()

    for part in range(3):
        back_scale = 1.0 / HALF if part == 2 else 1.0

        def body(n):
            at = pl.ds(n, block)
            end = mid[part, pl.ds(far - near + n, block), :] * back_scale
            lam = weight_v[part, at, :] * (hi[part, at, :] - end)
            lam_out[part, at, :] = lam * (flags[2] * back_scale)

        over(hi.shape[1], block, body)

    for c in c_kept + [c_a, c_b]:
        c.wait()

    @pl.when(flags[3] > 0.5)
    def _():
        c = pltpu.make_async_copy(start, lo.at[:, pl.ds(near, band), :], sems.at[0])
        c.start()
        c.wait()
        scale_third(lo, near, band)

    cost_out[...] = jnp.zeros_like(cost_out)
    for part in range(3):
        back_scale = 1.0 / HALF if part == 2 else 1.0

        def body(n):
            at, shifted = pl.ds(n, block), pl.ds(near + n, block)
            here = kept[part, at, :]
            gap = here - lo[part, shifted, :] * back_scale
            lam = weight_v[part, shifted, :] * gap
            pull = a_v[part, at, :] * here
            part_out[part, at, :] = here - STEP_SIZE * (lam + (pull - b_v[part, at, :]))
            cost_out[...] += lam * gap + here * (pull - 2.0 * b_v[part, at, :])

        over(band, block, body)


def step_kernel(flags, lam, part, depth, rate, edge_out, mid_out, work):
    band = part.shape[1]
    size = depth.shape[0] // rate.shape[0]
    near, far = NEAR * size, FAR * size
    block = 8 * size
    work[...] = lam[...]
    sweep(work, depth, rate, FAR - NEAR, NEAR, flags, False)
    for c in range(3):
        scale = STEP_SIZE * (HALF if c == 2 else 1.0)

        def new(where):
            return part[c, pl.ds(where, block), :] + scale * work[c, pl.ds(near + where, block), :]

        def upper(n):
            edge_out[c, pl.ds(n, block), :] = new(n)
            edge_out[c, pl.ds(far + n, block), :] = new(band - far + n)

        def middle(n):
            mid_out[c, pl.ds(n, block), :] = new(far + n)

        over(far, block, upper)
        over(band - 2 * far, block, middle)


def final_kernel(flags, lam, part, depth, rate, out, work):
    size = depth.shape[0] // rate.shape[0]
    near = NEAR * size
    work[...] = lam[...]
    sweep(work, depth, rate, FAR - NEAR, NEAR, flags, False)
    for c in range(3):
        scale = STEP_SIZE * (HALF if c == 2 else 1.0)

        def body(t, carry):
            base = t * (SUB * size)
            for s in range(size):
                here = part[c, pl.ds(base + s, SUB, stride=size), :]
                back = work[c, pl.ds(near + base + s, SUB, stride=size), :]
                out[c, pl.ds(pl.multiple_of(t * SUB, SUB), SUB), pl.ds(s * LANE, LANE)] = (
                    here + scale * back
                )
            return carry

        lax.fori_loop(0, out.shape[1] // SUB, body, 0)


def deposit_kernel(code, load, value, a_out, b_out, *acc):
    a_acc, b_acc = acc[:GROUPS], acc[GROUPS:]
    size = acc[0].shape[0] - a_out.shape[0]
    block = 8 * size
    zero = jnp.zeros((block, LANE), jnp.float32)

    def clear(n):
        for ref in acc:
            ref[pl.ds(n, block), :] = zero

    over(a_out.shape[0], block, clear)
    column = lax.broadcasted_iota(jnp.int32, (size, LANE), 0) * LANE + lax.broadcasted_iota(
        jnp.int32, (size, LANE), 1
    )
    shift = (size * LANE).bit_length() - 1

    def body(n, carry):
        for g in range(GROUPS):
            i = n * GROUPS + g
            word = code[i]
            at = pl.ds(pl.multiple_of((word >> shift) * size, size), size)
            hit = column == (word & (size * LANE - 1))
            a_acc[g][at, :] = a_acc[g][at, :] + jnp.where(hit, load[i], 0.0)
            b_acc[g][at, :] = b_acc[g][at, :] + jnp.where(hit, value[i], 0.0)
        return carry

    lax.fori_loop(0, code.shape[0] // GROUPS, body, 0, unroll=4)

    def total(n):
        at = pl.ds(n, block)
        for out, refs in ((a_out, a_acc), (b_out, b_acc)):
            out[at, :] = (refs[0][at, :] + refs[1][at, :]) + (refs[2][at, :] + refs[3][at, :])

    over(a_out.shape[0], block, total)


def per_device(
    increments, start_state, depth, error_weight, obs_index, obs_count, obs_value, obs_weight
):
    _, comps, rows, lon = increments.shape
    bands = lax.axis_size("space")
    windows = lax.axis_size("tm")
    band = lax.axis_index("space")
    me = lax.axis_index("tm")
    even = me % 2 == 0
    total_rows = rows * bands
    first_row = band * rows
    size = lon // LANE
    f32 = jnp.float32
    any_space = pl.BlockSpec(memory_space=pl.ANY)
    smem = pl.BlockSpec(memory_space=pltpu.SMEM)
    vmem = pl.BlockSpec(memory_space=pltpu.VMEM)

    def folded(x):
        return x.reshape(x.shape[:-2] + (x.shape[-2] * size, LANE))

    swap = [(i, i ^ 1) for i in range(windows)]
    inward = [(i, i - 2) for i in range(2, windows) if i % 2 == 0] + [
        (i, i + 2) for i in range(windows - 2) if i % 2 == 1
    ]
    outward = [(b, a) for a, b in inward]
    southward = [(i, i + 1) for i in range(bands - 1)]
    northward = [(b, a) for a, b in southward]
    near, far = NEAR * size, FAR * size
    band_size = rows * size

    own = folded(increments[0])
    edge = jnp.concatenate([own[:, :far], own[:, band_size - far :]], 1)
    inner = own[:, far : band_size - far]

    index = obs_index[0]
    plane = total_rows * lon
    component = index // plane
    remainder = index % plane
    local = remainder // lon - first_row
    kept = (local >= 0) & (local < rows) & (jnp.arange(index.shape[0]) < obs_count[0])
    code = jnp.where(kept, (component * rows + local) * lon + remainder % lon, comps * rows * lon)
    load = jnp.where(kept, obs_weight[0], 0.0)
    pulled = load * obs_value[0]
    own_list = jnp.stack([code.astype(f32), load, pulled])
    own_const = jnp.sum(pulled * obs_value[0])
    other_list = lax.ppermute(own_list, "tm", swap)

    deposit = pl.pallas_call(
        deposit_kernel,
        in_specs=[smem] * 3,
        out_specs=[vmem] * 2,
        out_shape=[jax.ShapeDtypeStruct((comps * band_size, LANE), f32)] * 2,
        scratch_shapes=[pltpu.VMEM((comps * band_size + size, LANE), f32)] * (2 * GROUPS),
        cost_estimate=pl.CostEstimate(flops=40_000_000, bytes_accessed=0, transcendentals=0),
        name="deposit",
    )

    def deposited(words):
        a, b = deposit(words[0].astype(jnp.int32), words[1], words[2])
        return a.reshape(comps, band_size, LANE), b.reshape(comps, band_size, LANE)

    const = jnp.concatenate([folded(error_weight).reshape(-1, LANE), folded(depth)], 0)
    pieces = [const[c * band_size : (c + 1) * band_size] for c in range(comps + 1)]
    sizes = [near] * comps + [far]
    const_n = lax.ppermute(
        jnp.concatenate([p[band_size - n :] for p, n in zip(pieces, sizes)]), "space", southward
    )
    const_s = lax.ppermute(
        jnp.concatenate([p[:n] for p, n in zip(pieces, sizes)]), "space", northward
    )
    split = comps * near
    shaped = lambda c: c[:split].reshape(comps, near, LANE)
    weight_wide = jnp.concatenate([shaped(const_n), folded(error_weight), shaped(const_s)], 1)
    depth_wide = (HALF * HALF) * jnp.concatenate([const_n[split:], pieces[-1], const_s[split:]], 0)
    latitude = (
        (first_row - FAR + jnp.arange(rows + 2 * FAR)).astype(f32) + 0.5
    ) / total_rows * math.pi - math.pi / 2
    rate_wide = jnp.broadcast_to(
        (CORIOLIS_MAX * jnp.sin(latitude))[:, None], (rows + 2 * FAR, LANE)
    )
    start = folded(start_state)

    near_size, far_size = band_size + 2 * near, band_size + 2 * far
    gap_call = pl.pallas_call(
        gap_kernel,
        in_specs=[smem, smem] + [any_space] * 14,
        out_specs=[vmem] * 3,
        out_shape=[
            jax.ShapeDtypeStruct((comps, near_size, LANE), f32),
            jax.ShapeDtypeStruct((comps, band_size, LANE), f32),
            jax.ShapeDtypeStruct((8 * size, LANE), f32),
        ],
        scratch_shapes=[
            pltpu.VMEM((comps, near_size, LANE), f32),
            pltpu.VMEM((comps, far_size, LANE), f32),
            pltpu.VMEM((comps, band_size, LANE), f32),
            pltpu.VMEM((comps, near_size, LANE), f32),
            pltpu.VMEM((far_size, LANE), f32),
            pltpu.VMEM((rows + 2 * FAR, LANE), f32),
            pltpu.VMEM((comps, near_size, LANE), f32),
            pltpu.VMEM((comps, band_size, LANE), f32),
            pltpu.VMEM((comps, band_size, LANE), f32),
            pltpu.SemaphoreType.DMA((23,)),
        ],
        cost_estimate=pl.CostEstimate(flops=30_000_000, bytes_accessed=0, transcendentals=0),
        name="gaps",
    )
    step_cost = pl.CostEstimate(flops=15_000_000, bytes_accessed=0, transcendentals=0)
    step_call = pl.pallas_call(
        step_kernel,
        in_specs=[smem] + [vmem] * 4,
        out_specs=[vmem] * 2,
        out_shape=[
            jax.ShapeDtypeStruct((comps, 2 * far, LANE), f32),
            jax.ShapeDtypeStruct((comps, band_size - 2 * far, LANE), f32),
        ],
        scratch_shapes=[pltpu.VMEM((comps, near_size, LANE), f32)],
        cost_estimate=step_cost,
        name="step",
    )
    final_call = pl.pallas_call(
        final_kernel,
        in_specs=[smem] + [vmem] * 4,
        out_specs=vmem,
        out_shape=jax.ShapeDtypeStruct((comps, rows, lon), f32),
        scratch_shapes=[pltpu.VMEM((comps, near_size, LANE), f32)],
        cost_estimate=step_cost,
        name="final",
    )

    costs = []
    own_obs = deposited(own_list)
    for turn in range(ITERS):
        away = turn % 2 == 0
        target = (me ^ 1) if away else me
        shift = inward if away else outward
        mid_e = lax.ppermute(edge, "tm", swap)
        far_e = lax.ppermute(edge, "tm", shift)
        mid_m = lax.ppermute(inner, "tm", swap)
        far_m = lax.ppermute(inner, "tm", shift)
        if turn == 0:
            own_obs, mid_e, other_list = lax.optimization_barrier((own_obs, mid_e, other_list))
            other_obs = deposited(other_list)
        obs_a, obs_b = other_obs if away else own_obs
        from_north = lax.ppermute(
            jnp.concatenate(
                [edge[:, 2 * far - near :], mid_e[:, far:], far_e[:, 2 * far - near :]], 1
            ),
            "space",
            southward,
        )
        from_south = lax.ppermute(
            jnp.concatenate([edge[:, :near], mid_e[:, :far], far_e[:, :near]], 1),
            "space",
            northward,
        )
        own_lo = (even if away else ~even).astype(jnp.int32).reshape(1)
        flags = jnp.stack(
            [band > 0, band < bands - 1, target < windows - 1, target == 0]
        ).astype(f32)
        lam, part, cost = gap_call(
            own_lo,
            flags,
            edge,
            inner,
            mid_e,
            mid_m,
            far_e,
            far_m,
            from_north,
            from_south,
            start,
            depth_wide,
            rate_wide,
            weight_wide,
            obs_a,
            obs_b,
        )
        cost = jnp.sum(cost)
        costs.append(lax.ppermute(cost, "tm", swap) if away else cost)
        if turn < ITERS - 1:
            edge, inner = step_call(flags, lam, part, depth_wide, rate_wide)
        else:
            state = final_call(flags, lam, part, depth_wide, rate_wide)
    sums = (jnp.stack(costs) + own_const).reshape(1, ITERS)
    sums = jnp.pad(sums, ((0, 0), (0, LANE - ITERS)))
    spread = sums
    for turn in range(1, bands):
        ring = [(i, (i + turn) % bands) for i in range(bands)]
        spread = spread + lax.ppermute(sums, "space", ring)
    cells = comps * total_rows * lon
    return state[None], (0.5 / cells) * spread[0, :ITERS, None]


def solution(mesh):
    placed = (
        P("tm", None, "space", None),
        P(None, "space", None),
        P("space", None),
        P(None, "space", None),
        P("tm", None),
        P("tm"),
        P("tm", None),
        P("tm", None),
    )
    return jax.shard_map(
        per_device,
        mesh=mesh,
        in_specs=placed,
        out_specs=(P("tm", None, "space", None), P(None, "tm")),
        check_vma=False,
    )
```

time: 187 us -> 196 us (1.048)
  waiting for transfers between devices: 20.2 us -> 36 us
  Pallas kernels: 94.1 us -> 86 us
  local copies, waits for them, and re-layouts: 11.3 us -> 19 us
  starting transfers between devices: 40.5 us -> 37.2 us
  other arithmetic: 17.8 us -> 15.3 us
    ppermute x2, waiting for transfers between devices: 0.01 us -> 9.97 us  [per_device(): far_m = lax.ppermute(inner, 'tm', shift)]
    reshape x0 -> x3, local copies, waits for them, and re-layouts: none -> 5.99 us  [folded(): return x.reshape(x.shape[:-2] + (x.shape[-2] * size, LANE))]
    ppermute x1, waiting for transfers between devices: 11.9 us -> 17.4 us  [per_device(): other_list = lax.ppermute(own_list, 'tm', swap)]
    pallas_call x2, Pallas kernels: 38.3 us -> 33.5 us  [per_device(): gap_call(own_lo, flags, edge, inner, mid_e, mid_m, far_e, far_m, from_nor...]
    ppermute x2, starting transfers between devices: 6.25 us -> 9.11 us  [per_device(): mid_e = lax.ppermute(edge, 'tm', swap)]
    ppermute x1, starting transfers between devices: 2.73 us -> 0.08 us  [per_device(): other_list = lax.ppermute(own_list, 'tm', swap)]
    pallas_call x2, Pallas kernels: 35.5 us -> 33.1 us  [deposited(): a, b = deposit(words[0].astype(jnp.int32), words[1], words[2])]
    slice x11 -> x20, local copies, waits for them, and re-layouts: 6.61 us -> 7.25 us  [the longest x6 2.05 us: per_device(): p[band_size - n:]]
  transfers between devices with their start and end apart: 19 -> 19, of which waited for: 3 -> 4; matrix products, arithmetic and copies ran while one was open for 13% -> 14% of each run, Pallas kernels for 35% -> 31%
where the time goes in v1:
time: 196 us; the launch traced here: 195 us
  Pallas kernels  86 us (44%)
  starting transfers between devices  37.2 us (19%)
  waiting for transfers between devices  36 us (18%)
  local copies, waits for them, and re-layouts  19 us (10%)
  other arithmetic  15.3 us (8%)
    pallas_call x2, Pallas kernels, per_device(): gap_call(own_lo, flags, edge, inner, mid_e, mid_m, far_e, far_m, from_nor...  33.5 us
    pallas_call x2, Pallas kernels, deposited(): a, b = deposit(words[0].astype(jnp.int32), words[1], words[2])  33.1 us
    ppermute x1, waiting for transfers between devices, per_device(): other_list = lax.ppermute(own_list, 'tm', swap)  17.4 us
    ppermute x2, waiting for transfers between devices, per_device(): far_m = lax.ppermute(inner, 'tm', shift)  9.97 us
    pallas_call x1, Pallas kernels, per_device(): state = final_call(flags, lam, part, depth_wide, rate_wide)  9.88 us
    pallas_call x1, Pallas kernels, per_device(): edge, inner = step_call(flags, lam, part, depth_wide, rate_wide)  9.43 us
    ppermute x2, starting transfers between devices, per_device(): mid_e = lax.ppermute(edge, 'tm', swap)  9.11 us
    ppermute x2, waiting for transfers between devices, per_device(): mid_e = lax.ppermute(edge, 'tm', swap)  7.5 us
  transfers between devices with their start and end apart: 19, of which 4 were waited for; matrix products, arithmetic and copies ran while one was open for 14% of the time, Pallas kernels for 31%

profile of v1, /device:TPU:0, one launch (start us, length us, event | category | flops | bytes accessed | tf_op | source)
XLA Modules:
  0.0 195.3 jit_solution(17514292746784492739)
XLA Ops:
  0.6 1.5 reshape_squeeze.3
  3.6 6.0 %collective-permute-start = (f32[3,384,128]{2,1,0:T(8,128)S(1)}, f32[3,384,128]{2,1,0:T(8,128)}, u32[]{:S(2)}, u32[]{:S(2)}) collective-permute-start(f32[3,384,128]{2,1,0:T(8,128)S(1)} %pad_maximum_fusion.1.own_e), channel_id=1, source_target_pairs={{0,4},{4,0},{8,12},{12,8},{16,20},{20,16},{24,28},{28,24},{1,5},{5... | collective-permute-start | bytes 1769480 | tf_op jit(solution)/shard_map/ppermute | solution.py:490
  14.5 3.7 %collective-permute-start.7 = (f32[480,128]{1,0:T(8,128)}, f32[480,128]{1,0:T(8,128)}, u32[]{:S(2)}, u32[]{:S(2)}) collective-permute-start(f32[480,128]{1,0:T(8,128)} %pad_maximum_fusion.6), channel_id=1, source_target_pairs={{0,1},{1,2},{2,3},{4,5},{5,6},{6,7},{8,9},{9,10},{10,11},{12,13},{... | collective-permute-start | bytes 737288 | tf_op jit(solution)/shard_map/ppermute | solution.py:418
  23.3 1.9 reshape.125
  25.3 1.5 reshape.127
  26.8 2.5 %reshape.124.start = f32[3,1024,128]{2,1,0:T(8,128)} reshape(f32[3,128,1024]{2,1,0:T(8,128)} %param.9) | data formatting | bytes 3145728 | tf_op jit(solution)/shard_map/reshape | solution.py:372
  29.3 16.5 %deposit.2 = (f32[3072,128]{1,0:T(8,128)}, f32[3072,128]{1,0:T(8,128)}) custom-call(s32[4096]{0:T(1024)} %fusion.9.code, f32[4096]{0:T(1024)} %get-tuple-element.36.load, f32[4096]{0:T(1024)} %get-tuple-element.35.value), custom_call_target="tpu_custom_call" | custom-call | flops 40000000 | tf_op jit(solution)/shard_map/deposit/pallas_call | solution.py:412
  45.9 2.4 %collective-permute-start.2 = (f32[3,640,128]{2,1,0:T(8,128)S(1)}, f32[3,640,128]{2,1,0:T(8,128)}, u32[]{:S(2)}, u32[]{:S(2)}) collective-permute-start(f32[3,640,128]{2,1,0:T(8,128)S(1)} %slice.172.own_m), channel_id=1, source_target_pairs={{0,4},{4,0},{8,12},{12,8},{16,20},{20,16},{24,28},{28,24},{1,5},{5... | collective-permute-start | bytes 2949128 | tf_op jit(solution)/shard_map/ppermute | solution.py:492
  50.2 1.4 pad_maximum_fusion.weight
  54.4 17.4 %collective-permute-done.1 = f32[3,4096]{1,0:T(4,128)S(1)} collective-permute-done((f32[3,4096]{1,0:T(4,128)S(1)}, f32[3,4096]{1,0:T(4,128)S(1)}, u32[]{:S(2)}, u32[]{:S(2)}) %collective-permute-start.1) | collective-permute-done | bytes 49184 | tf_op jit(solution)/shard_map/ppermute | solution.py:399
  73.9 1.5 collective-permute-start.5
  78.2 16.6 %deposit.3 = (f32[3072,128]{1,0:T(8,128)}, f32[3072,128]{1,0:T(8,128)}) custom-call(s32[4096]{0:T(1024)} %bitcast.45, f32[4096]{0:T(1024)} %bitcast.44, f32[4096]{0:T(1024)} %bitcast.43), custom_call_target="tpu_custom_call" | custom-call | flops 40000000 | tf_op jit(solution)/shard_map/deposit/pallas_call | solution.py:412
  95.9 16.0 %gaps.2 = (f32[3,1216,128]{2,1,0:T(8,128)}, f32[3,1024,128]{2,1,0:T(8,128)}, f32[64,128]{1,0:T(8,128)}) custom-call(s32[1]{0:T(128)} %bitcast.7.own_lo, f32[4]{0:T(128)} %add_convert_fusion.1.flags, f32[3,384,128]{2,1,0:T(8,128)} %copy-done.1, f32[3,640,128]{2,1,0:T(8,128)} %copy-done, f32[3,384,128]{2,1,0:T(8,128)} %collective-permute-done.mid_e, ...), custom_call_target="tpu_custom_call" | custom-call | flops 30000000 | tf_op jit(solution)/shard_map/gaps/pallas_call | solution.py:514
  111.8 9.4 %step.1 = (f32[3,384,128]{2,1,0:T(8,128)}, f32[3,640,128]{2,1,0:T(8,128)}) custom-call(f32[4]{0:T(128)} %add_convert_fusion.1.flags, f32[3,1216,128]{2,1,0:T(8,128)} %get-tuple-element.24.lam, f32[3,1024,128]{2,1,0:T(8,128)} %get-tuple-element.25.part, f32[1408,128]{1,0:T(8,128)} %maximum_multiply_fusion.depth, f32[176,128]{1,0:T(8,128)} %broadcast_in_dim.25.rate), custom_call_target="tpu_custom_call" | custom-call | flops 15000000 | tf_op jit(solution)/shard_map/step/pallas_call | solution.py:535
  121.3 3.1 %collective-permute-start.9 = (f32[3,384,128]{2,1,0:T(8,128)}, f32[3,384,128]{2,1,0:T(8,128)S(1)}, u32[]{:S(2)}, u32[]{:S(2)}) collective-permute-start(f32[3,384,128]{2,1,0:T(8,128)} %get-tuple-element.26.own_e), channel_id=1, source_target_pairs={{0,4},{4,0},{8,12},{12,8},{16,20},{20,16},{24,28},{28,24},{1,5},{5... | collective-permute-start | bytes 1769480 | tf_op jit(solution)/shard_map/ppermute | solution.py:490
  125.7 3.4 %collective-permute-start.12 = (f32[3,640,128]{2,1,0:T(8,128)}, f32[3,640,128]{2,1,0:T(8,128)S(1)}, u32[]{:S(2)}, u32[]{:S(2)}) collective-permute-start(f32[3,640,128]{2,1,0:T(8,128)} %get-tuple-element.27.own_m), channel_id=1, source_target_pairs={{0,8},{8,16},{16,24},{12,4},{20,12},{28,20},{1,9},{9,17},{17,25},{... | collective-permute-start | bytes 2949128 | tf_op jit(solution)/shard_map/ppermute | solution.py:493
  130.2 7.5 %collective-permute-done.9.mid_e = f32[3,384,128]{2,1,0:T(8,128)S(1)} collective-permute-done((f32[3,384,128]{2,1,0:T(8,128)}, f32[3,384,128]{2,1,0:T(8,128)S(1)}, u32[]{:S(2)}, u32[]{:S(2)}) %collective-permute-start.9) | collective-permute-done | bytes 589856 | tf_op jit(solution)/shard_map/ppermute | solution.py:490
  139.8 3.7 %collective-permute-start.13 = (f32[3,384,128]{2,1,0:T(8,128)}, f32[3,384,128]{2,1,0:T(8,128)S(1)}, u32[]{:S(2)}, u32[]{:S(2)}) collective-permute-start(f32[3,384,128]{2,1,0:T(8,128)} %pad_maximum_fusion.4), channel_id=1, source_target_pairs={{0,1},{1,2},{2,3},{4,5},{5,6},{6,7},{8,9},{9,10},{10,11},{12,13},{... | collective-permute-start | bytes 1769480 | tf_op jit(solution)/shard_map/ppermute | solution.py:498
  147.0 3.0 %collective-permute-start.15 = (f32[]{:T(128)}, f32[]{:T(128)}, u32[]{:S(2)}, u32[]{:S(2)}) collective-permute-start(f32[]{:T(128)} %reduce_sum.27), channel_id=1, source_target_pairs={{0,4},{4,0},{8,12},{12,8},{16,20},{20,16},{24,28},{28,24},{1,5},{5... | collective-permute-start | bytes 20 | tf_op jit(solution)/shard_map/ppermute | solution.py:533
  150.0 10.0 %collective-permute-done.12.far_m = f32[3,640,128]{2,1,0:T(8,128)S(1)} collective-permute-done((f32[3,640,128]{2,1,0:T(8,128)}, f32[3,640,128]{2,1,0:T(8,128)S(1)}, u32[]{:S(2)}, u32[]{:S(2)}) %collective-permute-start.12) | collective-permute-done | bytes 983072 | tf_op jit(solution)/shard_map/ppermute | solution.py:493
  161.4 17.6 %gaps.3 = (f32[3,1216,128]{2,1,0:T(8,128)}, f32[3,1024,128]{2,1,0:T(8,128)}, f32[64,128]{1,0:T(8,128)}) custom-call(s32[1]{0:T(128)} %bitcast.4.own_lo, f32[4]{0:T(128)} %add_convert_fusion.flags, f32[3,384,128]{2,1,0:T(8,128)} %get-tuple-element.26.own_e, f32[3,640,128]{2,1,0:T(8,128)} %get-tuple-element.27.own_m, f32[3,384,128]{2,1,0:T(8,128)} %copy-done.2, ...), custom_call_target="tpu_custom_call" | custom-call | flops 30000000 | tf_op jit(solution)/shard_map/gaps/pallas_call | solution.py:514
  180.3 2.0 %maximum_add_fusion = f32[1,2]{1,0:T(1,128)S(1)} fusion(f32[1,1]{1,0:T(1,128)} %bitcast.23, f32[1,1]{1,0:T(1,128)} %bitcast.22, f32[]{:T(128)} %get-tuple-element.34), kind=kLoop, calls=%fused_computation.59 | loop fusion | flops 4 | bytes 20 | tf_op jit(solution)/shard_map/add | solution.py:538
  182.3 2.0 %collective-permute-start.17 = (f32[1,128]{1,0:T(1,128)S(1)}, f32[1,128]{1,0:T(1,128)S(1)}, u32[]{:S(2)}, u32[]{:S(2)}) collective-permute-start(f32[1,128]{1,0:T(1,128)S(1)} %pad.4), channel_id=1, source_target_pairs={{0,2},{1,3},{2,0},{3,1},{4,6},{5,7},{6,4},{7,5},{8,10},{9,11},{10,... | collective-permute-start | bytes 1544 | tf_op jit(solution)/shard_map/ppermute | solution.py:543
  184.8 9.9 %final.1 = f32[3,128,1024]{2,1,0:T(8,128)} custom-call(f32[4]{0:T(128)} %add_convert_fusion.flags, f32[3,1216,128]{2,1,0:T(8,128)} %get-tuple-element.30.lam, f32[3,1024,128]{2,1,0:T(8,128)} %get-tuple-element.31.part, f32[1408,128]{1,0:T(8,128)} %maximum_multiply_fusion.depth, f32[176,128]{1,0:T(8,128)} %broadcast_in_dim.25.rate), custom_call_target="tpu_custom_call" | custom-call | flops 15000000 | tf_op jit(solution)/shard_map/final/pallas_call | solution.py:537
  (100 shorter events, 33.1 us)
Async XLA Ops:
  2.2 12.3 %copy-start.1 = (f32[3,384,128]{2,1,0:T(8,128)}, f32[3,384,128]{2,1,0:T(8,128)S(1)}, u32[]{:S(2)}) copy-start(f32[3,384,128]{2,1,0:T(8,128)S(1)} %pad_maximum_fusion.1.own_e) | copy-start | bytes 1769476
  2.3 70.6 %collective-permute-start.3 = (f32[3,384,128]{2,1,0:T(8,128)S(1)}, f32[3,384,128]{2,1,0:T(8,128)}, u32[]{:S(2)}, u32[]{:S(2)}) collective-permute-start(f32[3,384,128]{2,1,0:T(8,128)S(1)} %pad_maximum_fusion.1.own_e), channel_id=1, source_target_pairs={{8,0},{16,8},{24,16},{4,12},{12,20},{20,28},{9,1},{17,9},{25,17},{... | collective-permute-start | bytes 1769480 | tf_op jit(solution)/shard_map/ppermute | solution.py:491
  3.6 68.2 %collective-permute-start = (f32[3,384,128]{2,1,0:T(8,128)S(1)}, f32[3,384,128]{2,1,0:T(8,128)}, u32[]{:S(2)}, u32[]{:S(2)}) collective-permute-start(f32[3,384,128]{2,1,0:T(8,128)S(1)} %pad_maximum_fusion.1.own_e), channel_id=1, source_target_pairs={{0,4},{4,0},{8,12},{12,8},{16,20},{20,16},{24,28},{28,24},{1,5},{5... | collective-permute-start | bytes 1769480 | tf_op jit(solution)/shard_map/ppermute | solution.py:490
  12.4 33.5 %collective-permute-start.8 = (f32[480,128]{1,0:T(8,128)}, f32[480,128]{1,0:T(8,128)}, u32[]{:S(2)}, u32[]{:S(2)}) collective-permute-start(f32[480,128]{1,0:T(8,128)} %pad_maximum_fusion.7), channel_id=1, source_target_pairs={{1,0},{2,1},{3,2},{5,4},{6,5},{7,6},{9,8},{10,9},{11,10},{13,12},{... | collective-permute-start | bytes 737288 | tf_op jit(solution)/shard_map/ppermute | solution.py:421
  13.8 6.9 %copy-start.11 = (f32[1,4096]{1,0:T(1,128)S(1)}, f32[1,4096]{1,0:T(1,128)}, u32[]{:S(2)}) copy-start(f32[1,4096]{1,0:T(1,128)} %param.14) | copy-start | bytes 49156
  14.5 34.7 %collective-permute-start.7 = (f32[480,128]{1,0:T(8,128)}, f32[480,128]{1,0:T(8,128)}, u32[]{:S(2)}, u32[]{:S(2)}) collective-permute-start(f32[480,128]{1,0:T(8,128)} %pad_maximum_fusion.6), channel_id=1, source_target_pairs={{0,1},{1,2},{2,3},{4,5},{5,6},{6,7},{8,9},{9,10},{10,11},{12,13},{... | collective-permute-start | bytes 737288 | tf_op jit(solution)/shard_map/ppermute | solution.py:418
  18.3 27.6 %copy-start = (f32[3,640,128]{2,1,0:T(8,128)}, f32[3,640,128]{2,1,0:T(8,128)S(1)}, u32[]{:S(2)}) copy-start(f32[3,640,128]{2,1,0:T(8,128)S(1)} %slice.172.own_m) | copy-start | bytes 2949124
  18.3 76.4 %collective-permute-start.4 = (f32[3,640,128]{2,1,0:T(8,128)S(1)}, f32[3,640,128]{2,1,0:T(8,128)}, u32[]{:S(2)}, u32[]{:S(2)}) collective-permute-start(f32[3,640,128]{2,1,0:T(8,128)S(1)} %slice.172.own_m), channel_id=1, source_target_pairs={{8,0},{16,8},{24,16},{4,12},{12,20},{20,28},{9,1},{17,9},{25,17},{... | collective-permute-start | bytes 2949128 | tf_op jit(solution)/shard_map/ppermute | solution.py:493
  45.9 48.9 %collective-permute-start.2 = (f32[3,640,128]{2,1,0:T(8,128)S(1)}, f32[3,640,128]{2,1,0:T(8,128)}, u32[]{:S(2)}, u32[]{:S(2)}) collective-permute-start(f32[3,640,128]{2,1,0:T(8,128)S(1)} %slice.172.own_m), channel_id=1, source_target_pairs={{0,4},{4,0},{8,12},{12,8},{16,20},{20,16},{24,28},{28,24},{1,5},{5... | collective-permute-start | bytes 2949128 | tf_op jit(solution)/shard_map/ppermute | solution.py:492
  49.2 22.5 %collective-permute-start.1 = (f32[3,4096]{1,0:T(4,128)S(1)}, f32[3,4096]{1,0:T(4,128)S(1)}, u32[]{:S(2)}, u32[]{:S(2)}) collective-permute-start(f32[3,4096]{1,0:T(4,128)S(1)} %pad_maximum_fusion.8), channel_id=1, source_target_pairs={{0,4},{4,0},{8,12},{12,8},{16,20},{20,16},{24,28},{28,24},{1,5},{5... | collective-permute-start | bytes 147464 | tf_op jit(solution)/shard_map/ppermute | solution.py:399
  73.9 20.9 %collective-permute-start.5 = (f32[3,384,128]{2,1,0:T(8,128)S(1)}, f32[3,384,128]{2,1,0:T(8,128)S(1)}, u32[]{:S(2)}, u32[]{:S(2)}) collective-permute-start(f32[3,384,128]{2,1,0:T(8,128)S(1)} %pad_maximum_fusion.2), channel_id=1, source_target_pairs={{0,1},{1,2},{2,3},{4,5},{5,6},{6,7},{8,9},{9,10},{10,11},{12,13},{... | collective-permute-start | bytes 1769480 | tf_op jit(solution)/shard_map/ppermute | solution.py:498
  76.2 18.5 %collective-permute-start.6 = (f32[3,384,128]{2,1,0:T(8,128)}, f32[3,384,128]{2,1,0:T(8,128)S(1)}, u32[]{:S(2)}, u32[]{:S(2)}) collective-permute-start(f32[3,384,128]{2,1,0:T(8,128)} %pad_maximum_fusion.3), channel_id=1, source_target_pairs={{1,0},{2,1},{3,2},{5,4},{6,5},{7,6},{9,8},{10,9},{11,10},{13,12},{... | collective-permute-start | bytes 1769480 | tf_op jit(solution)/shard_map/ppermute | solution.py:505
  121.3 16.4 %collective-permute-start.9 = (f32[3,384,128]{2,1,0:T(8,128)}, f32[3,384,128]{2,1,0:T(8,128)S(1)}, u32[]{:S(2)}, u32[]{:S(2)}) collective-permute-start(f32[3,384,128]{2,1,0:T(8,128)} %get-tuple-element.26.own_e), channel_id=1, source_target_pairs={{0,4},{4,0},{8,12},{12,8},{16,20},{20,16},{24,28},{28,24},{1,5},{5... | collective-permute-start | bytes 1769480 | tf_op jit(solution)/shard_map/ppermute | solution.py:490
  124.4 14.5 %collective-permute-start.11 = (f32[3,384,128]{2,1,0:T(8,128)}, f32[3,384,128]{2,1,0:T(8,128)S(1)}, u32[]{:S(2)}, u32[]{:S(2)}) collective-permute-start(f32[3,384,128]{2,1,0:T(8,128)} %get-tuple-element.26.own_e), channel_id=1, source_target_pairs={{0,8},{8,16},{16,24},{12,4},{20,12},{28,20},{1,9},{9,17},{17,25},{... | collective-permute-start | bytes 1769480 | tf_op jit(solution)/shard_map/ppermute | solution.py:491
  125.7 34.2 %collective-permute-start.12 = (f32[3,640,128]{2,1,0:T(8,128)}, f32[3,640,128]{2,1,0:T(8,128)S(1)}, u32[]{:S(2)}, u32[]{:S(2)}) collective-permute-start(f32[3,640,128]{2,1,0:T(8,128)} %get-tuple-element.27.own_m), channel_id=1, source_target_pairs={{0,8},{8,16},{16,24},{12,4},{20,12},{28,20},{1,9},{9,17},{17,25},{... | collective-permute-start | bytes 2949128 | tf_op jit(solution)/shard_map/ppermute | solution.py:493
  129.1 30.9 %collective-permute-start.10 = (f32[3,640,128]{2,1,0:T(8,128)}, f32[3,640,128]{2,1,0:T(8,128)S(1)}, u32[]{:S(2)}, u32[]{:S(2)}) collective-permute-start(f32[3,640,128]{2,1,0:T(8,128)} %get-tuple-element.27.own_m), channel_id=1, source_target_pairs={{0,4},{4,0},{8,12},{12,8},{16,20},{20,16},{24,28},{28,24},{1,5},{5... | collective-permute-start | bytes 2949128 | tf_op jit(solution)/shard_map/ppermute | solution.py:492
  137.7 8.6 %copy-start.13 = (f32[64,128]{1,0:T(8,128)S(1)}, f32[64,128]{1,0:T(8,128)}, u32[]{:S(2)}) copy-start(f32[64,128]{1,0:T(8,128)} %get-tuple-element.32) | copy-start | bytes 98308
  138.9 21.1 %copy-start.4 = (f32[3,384,128]{2,1,0:T(8,128)}, f32[3,384,128]{2,1,0:T(8,128)S(1)}, u32[]{:S(2)}) copy-start(f32[3,384,128]{2,1,0:T(8,128)S(1)} %collective-permute-done.11.far_e) | copy-start | bytes 1769476
  139.8 20.1 %collective-permute-start.13 = (f32[3,384,128]{2,1,0:T(8,128)}, f32[3,384,128]{2,1,0:T(8,128)S(1)}, u32[]{:S(2)}, u32[]{:S(2)}) collective-permute-start(f32[3,384,128]{2,1,0:T(8,128)} %pad_maximum_fusion.4), channel_id=1, source_target_pairs={{0,1},{1,2},{2,3},{4,5},{5,6},{6,7},{8,9},{9,10},{10,11},{12,13},{... | collective-permute-start | bytes 1769480 | tf_op jit(solution)/shard_map/ppermute | solution.py:498
  144.4 15.6 %collective-permute-start.14 = (f32[3,384,128]{2,1,0:T(8,128)}, f32[3,384,128]{2,1,0:T(8,128)}, u32[]{:S(2)}, u32[]{:S(2)}) collective-permute-start(f32[3,384,128]{2,1,0:T(8,128)} %pad_maximum_fusion.5), channel_id=1, source_target_pairs={{1,0},{2,1},{3,2},{5,4},{6,5},{7,6},{9,8},{10,9},{11,10},{13,12},{... | collective-permute-start | bytes 1769480 | tf_op jit(solution)/shard_map/ppermute | solution.py:505
  147.0 33.3 %collective-permute-start.15 = (f32[]{:T(128)}, f32[]{:T(128)}, u32[]{:S(2)}, u32[]{:S(2)}) collective-permute-start(f32[]{:T(128)} %reduce_sum.27), channel_id=1, source_target_pairs={{0,4},{4,0},{8,12},{12,8},{16,20},{20,16},{24,28},{28,24},{1,5},{5... | collective-permute-start | bytes 20 | tf_op jit(solution)/shard_map/ppermute | solution.py:533
  182.3 12.4 %collective-permute-start.17 = (f32[1,128]{1,0:T(1,128)S(1)}, f32[1,128]{1,0:T(1,128)S(1)}, u32[]{:S(2)}, u32[]{:S(2)}) collective-permute-start(f32[1,128]{1,0:T(1,128)S(1)} %pad.4), channel_id=1, source_target_pairs={{0,2},{1,3},{2,0},{3,1},{4,6},{5,7},{6,4},{7,5},{8,10},{9,11},{10,... | collective-permute-start | bytes 1544 | tf_op jit(solution)/shard_map/ppermute | solution.py:543
  184.3 10.4 %collective-permute-start.18 = (f32[1,128]{1,0:T(1,128)S(1)}, f32[1,128]{1,0:T(1,128)S(1)}, u32[]{:S(2)}, u32[]{:S(2)}) collective-permute-start(f32[1,128]{1,0:T(1,128)S(1)} %pad.4), channel_id=1, source_target_pairs={{0,3},{1,0},{2,1},{3,2},{4,7},{5,4},{6,5},{7,6},{8,11},{9,8},{10,9... | collective-permute-start | bytes 1544 | tf_op jit(solution)/shard_map/ppermute | solution.py:543
  184.6 10.2 %collective-permute-start.16 = (f32[1,128]{1,0:T(1,128)S(1)}, f32[1,128]{1,0:T(1,128)S(1)}, u32[]{:S(2)}, u32[]{:S(2)}) collective-permute-start(f32[1,128]{1,0:T(1,128)S(1)} %pad.4), channel_id=1, source_target_pairs={{0,1},{1,2},{2,3},{3,0},{4,5},{5,6},{6,7},{7,4},{8,9},{9,10},{10,1... | collective-permute-start | bytes 1544 | tf_op jit(solution)/shard_map/ppermute | solution.py:543
  (9 other events, 29.0 us)

commit v2 on v1

--- a/solution.py
+++ b/solution.py
@@ -1,3 +1,4 @@
+import functools
 import math
 
 import jax
@@ -7,6 +8,7 @@
 from jax.experimental.pallas import tpu as pltpu
 from jax.sharding import PartitionSpec as P
 
+
 STEPS = 6
 ITERS = 2
 COURANT = 0.35
@@ -18,6 +20,7 @@
 NEAR = 2 * STEPS
 FAR = 4 * STEPS
 GROUPS = 4
+DEALS = 4
 HALF = 0.5 * COURANT
 LEAD = 24
 
@@ -118,10 +121,12 @@
         body(pl.multiple_of(n * block, SUB))
         return carry
 
-    lax.fori_loop(0, count // block, step, 0)
-
-
-def gap_kernel(
+    trips = count // block
+    lax.fori_loop(0, trips, step, 0, unroll=2 if trips % 2 == 0 else 1)
+
+
+def round_kernel(
+    finish,
     own_lo,
     flags,
     own_e,
@@ -138,20 +143,10 @@
     weight,
     obs_a,
     obs_b,
-    lam_out,
-    part_out,
-    cost_out,
-    lo,
-    mid,
-    kept,
-    hi,
-    depth_v,
-    rate_v,
-    weight_v,
-    a_v,
-    b_v,
-    sems,
+    *refs,
 ):
+    outs, cost_out = refs[:finish], refs[finish]
+    lo, mid, kept, hi, depth_v, rate_v, weight_v, a_v, b_v, cost_v, sems = refs[finish + 1 :]
     size = depth_v.shape[0] // rate_v.shape[0]
     near, far = NEAR * size, FAR * size
     band = kept.shape[1]
@@ -240,7 +235,7 @@
             at = pl.ds(n, block)
             end = mid[part, pl.ds(far - near + n, block), :] * back_scale
             lam = weight_v[part, at, :] * (hi[part, at, :] - end)
-            lam_out[part, at, :] = lam * (flags[2] * back_scale)
+            hi[part, at, :] = lam * (flags[2] * back_scale)
 
         over(hi.shape[1], block, body)
 
@@ -254,7 +249,7 @@
         c.wait()
         scale_third(lo, near, band)
 
-    cost_out[...] = jnp.zeros_like(cost_out)
+    cost_v[...] = jnp.zeros_like(cost_v)
     for part in range(3):
         back_scale = 1.0 / HALF if part == 2 else 1.0
 
@@ -264,58 +259,47 @@
             gap = here - lo[part, shifted, :] * back_scale
             lam = weight_v[part, shifted, :] * gap
             pull = a_v[part, at, :] * here
-            part_out[part, at, :] = here - STEP_SIZE * (lam + (pull - b_v[part, at, :]))
-            cost_out[...] += lam * gap + here * (pull - 2.0 * b_v[part, at, :])
+            kept[part, at, :] = here - STEP_SIZE * (lam + (pull - b_v[part, at, :]))
+            cost_v[...] += lam * gap + here * (pull - 2.0 * b_v[part, at, :])
 
         over(band, block, body)
 
-
-def step_kernel(flags, lam, part, depth, rate, edge_out, mid_out, work):
-    band = part.shape[1]
-    size = depth.shape[0] // rate.shape[0]
-    near, far = NEAR * size, FAR * size
-    block = 8 * size
-    work[...] = lam[...]
-    sweep(work, depth, rate, FAR - NEAR, NEAR, flags, False)
-    for c in range(3):
-        scale = STEP_SIZE * (HALF if c == 2 else 1.0)
+    total = cost_v[pl.ds(0, SUB), :]
+    for n in range(1, cost_v.shape[0] // SUB):
+        total = total + cost_v[pl.ds(SUB * n, SUB), :]
+    cost_out[...] = total
+
+    sweep(hi, depth_v, rate_v, FAR - NEAR, NEAR, flags, False)
+    for part in range(3):
+        scale = STEP_SIZE * (HALF if part == 2 else 1.0)
 
         def new(where):
-            return part[c, pl.ds(where, block), :] + scale * work[c, pl.ds(near + where, block), :]
+            return kept[part, pl.ds(where, block), :] + scale * hi[part, pl.ds(near + where, block), :]
 
         def upper(n):
-            edge_out[c, pl.ds(n, block), :] = new(n)
-            edge_out[c, pl.ds(far + n, block), :] = new(band - far + n)
+            outs[0][part, pl.ds(n, block), :] = new(n)
+            outs[0][part, pl.ds(far + n, block), :] = new(band - far + n)
 
         def middle(n):
-            mid_out[c, pl.ds(n, block), :] = new(far + n)
-
-        over(far, block, upper)
-        over(band - 2 * far, block, middle)
-
-
-def final_kernel(flags, lam, part, depth, rate, out, work):
-    size = depth.shape[0] // rate.shape[0]
-    near = NEAR * size
-    work[...] = lam[...]
-    sweep(work, depth, rate, FAR - NEAR, NEAR, flags, False)
-    for c in range(3):
-        scale = STEP_SIZE * (HALF if c == 2 else 1.0)
-
-        def body(t, carry):
+            outs[1][part, pl.ds(n, block), :] = new(far + n)
+
+        def last(t, carry):
             base = t * (SUB * size)
             for s in range(size):
-                here = part[c, pl.ds(base + s, SUB, stride=size), :]
-                back = work[c, pl.ds(near + base + s, SUB, stride=size), :]
-                out[c, pl.ds(pl.multiple_of(t * SUB, SUB), SUB), pl.ds(s * LANE, LANE)] = (
-                    here + scale * back
-                )
+                here = kept[part, pl.ds(base + s, SUB, stride=size), :]
+                back = hi[part, pl.ds(near + base + s, SUB, stride=size), :]
+                at = pl.ds(pl.multiple_of(t * SUB, SUB), SUB)
+                outs[0][part, at, pl.ds(s * LANE, LANE)] = here + scale * back
             return carry
 
-        lax.fori_loop(0, out.shape[1] // SUB, body, 0)
-
-
-def deposit_kernel(code, load, value, a_out, b_out, *acc):
+        if finish == 2:
+            over(far, block, upper)
+            over(inner, block, middle)
+        else:
+            lax.fori_loop(0, outs[0].shape[1] // SUB, last, 0)
+
+
+def deposit_kernel(code, load, value, a_out, b_out, picked, *acc):
     a_acc, b_acc = acc[:GROUPS], acc[GROUPS:]
     size = acc[0].shape[0] - a_out.shape[0]
     block = 8 * size
@@ -330,18 +314,32 @@
         jnp.int32, (size, LANE), 1
     )
     shift = (size * LANE).bit_length() - 1
+    spare = (a_out.shape[0] // size) << shift
+    entries = code.shape[0] - GROUPS * DEALS
+
+    def pick(n, found):
+        for k in range(GROUPS * DEALS):
+            i = n * (GROUPS * DEALS) + k
+            picked[found] = i
+            found = found + (code[i] < spare).astype(jnp.int32)
+        return found
+
+    found = lax.fori_loop(0, entries // (GROUPS * DEALS), pick, 0)
+    for k in range(GROUPS * DEALS):
+        picked[found + k] = entries
 
     def body(n, carry):
-        for g in range(GROUPS):
-            i = n * GROUPS + g
-            word = code[i]
-            at = pl.ds(pl.multiple_of((word >> shift) * size, size), size)
-            hit = column == (word & (size * LANE - 1))
-            a_acc[g][at, :] = a_acc[g][at, :] + jnp.where(hit, load[i], 0.0)
-            b_acc[g][at, :] = b_acc[g][at, :] + jnp.where(hit, value[i], 0.0)
+        for k in range(DEALS):
+            for g in range(GROUPS):
+                i = picked[n * (GROUPS * DEALS) + (k * GROUPS + g)]
+                word = code[i]
+                at = pl.ds(pl.multiple_of((word >> shift) * size, size), size)
+                hit = column == (word & (size * LANE - 1))
+                a_acc[g][at, :] = a_acc[g][at, :] + jnp.where(hit, load[i], 0.0)
+                b_acc[g][at, :] = b_acc[g][at, :] + jnp.where(hit, value[i], 0.0)
         return carry
 
-    lax.fori_loop(0, code.shape[0] // GROUPS, body, 0, unroll=4)
+    lax.fori_loop(0, (found + GROUPS * DEALS - 1) // (GROUPS * DEALS), body, 0)
 
     def total(n):
         at = pl.ds(n, block)
@@ -398,25 +396,47 @@
     own_const = jnp.sum(pulled * obs_value[0])
     other_list = lax.ppermute(own_list, "tm", swap)
 
-    deposit = pl.pallas_call(
+    def kernel(body, in_specs, out_specs, outs, scratch, flops):
+        held = sum(math.prod(o.shape) for o in outs)
+        held += sum(math.prod(c.shape) for c in scratch if c.dtype == f32)
+        return pl.pallas_call(
+            body,
+            in_specs=in_specs,
+            out_specs=out_specs,
+            out_shape=outs,
+            scratch_shapes=scratch,
+            cost_estimate=pl.CostEstimate(flops=flops, bytes_accessed=0, transcendentals=0),
+            compiler_params=pltpu.CompilerParams(vmem_limit_bytes=4 * held + (4 << 20)),
+        )
+
+    extra = GROUPS * DEALS
+    deposit = kernel(
         deposit_kernel,
-        in_specs=[smem] * 3,
-        out_specs=[vmem] * 2,
-        out_shape=[jax.ShapeDtypeStruct((comps * band_size, LANE), f32)] * 2,
-        scratch_shapes=[pltpu.VMEM((comps * band_size + size, LANE), f32)] * (2 * GROUPS),
-        cost_estimate=pl.CostEstimate(flops=40_000_000, bytes_accessed=0, transcendentals=0),
-        name="deposit",
+        [smem] * 3,
+        [vmem] * 2,
+        [jax.ShapeDtypeStruct((comps * band_size, LANE), f32)] * 2,
+        [pltpu.SMEM((index.shape[0] + extra,), jnp.int32)]
+        + [pltpu.VMEM((comps * band_size + size, LANE), f32)] * (2 * GROUPS),
+        20_000_000,
     )
 
     def deposited(words):
-        a, b = deposit(words[0].astype(jnp.int32), words[1], words[2])
+        spare = jnp.full((extra,), comps * rows * lon, jnp.int32)
+        none = jnp.zeros((extra,), f32)
+        a, b = deposit(
+            jnp.concatenate([words[0].astype(jnp.int32), spare]),
+            jnp.concatenate([words[1], none]),
+            jnp.concatenate([words[2], none]),
+        )
         return a.reshape(comps, band_size, LANE), b.reshape(comps, band_size, LANE)
 
     const = jnp.concatenate([folded(error_weight).reshape(-1, LANE), folded(depth)], 0)
     pieces = [const[c * band_size : (c + 1) * band_size] for c in range(comps + 1)]
     sizes = [near] * comps + [far]
     const_n = lax.ppermute(
-        jnp.concatenate([p[band_size - n :] for p, n in zip(pieces, sizes)]), "space", southward
+        jnp.concatenate([p[band_size - n :] for p, n in zip(pieces, sizes)]),
+        "space",
+        southward,
     )
     const_s = lax.ppermute(
         jnp.concatenate([p[:n] for p, n in zip(pieces, sizes)]), "space", northward
@@ -434,55 +454,37 @@
     start = folded(start_state)
 
     near_size, far_size = band_size + 2 * near, band_size + 2 * far
-    gap_call = pl.pallas_call(
-        gap_kernel,
-        in_specs=[smem, smem] + [any_space] * 14,
-        out_specs=[vmem] * 3,
-        out_shape=[
-            jax.ShapeDtypeStruct((comps, near_size, LANE), f32),
-            jax.ShapeDtypeStruct((comps, band_size, LANE), f32),
-            jax.ShapeDtypeStruct((8 * size, LANE), f32),
-        ],
-        scratch_shapes=[
-            pltpu.VMEM((comps, near_size, LANE), f32),
-            pltpu.VMEM((comps, far_size, LANE), f32),
-            pltpu.VMEM((comps, band_size, LANE), f32),
-            pltpu.VMEM((comps, near_size, LANE), f32),
-            pltpu.VMEM((far_size, LANE), f32),
-            pltpu.VMEM((rows + 2 * FAR, LANE), f32),
-            pltpu.VMEM((comps, near_size, LANE), f32),
-            pltpu.VMEM((comps, band_size, LANE), f32),
-            pltpu.VMEM((comps, band_size, LANE), f32),
-            pltpu.SemaphoreType.DMA((23,)),
-        ],
-        cost_estimate=pl.CostEstimate(flops=30_000_000, bytes_accessed=0, transcendentals=0),
-        name="gaps",
-    )
-    step_cost = pl.CostEstimate(flops=15_000_000, bytes_accessed=0, transcendentals=0)
-    step_call = pl.pallas_call(
-        step_kernel,
-        in_specs=[smem] + [vmem] * 4,
-        out_specs=[vmem] * 2,
-        out_shape=[
-            jax.ShapeDtypeStruct((comps, 2 * far, LANE), f32),
-            jax.ShapeDtypeStruct((comps, band_size - 2 * far, LANE), f32),
-        ],
-        scratch_shapes=[pltpu.VMEM((comps, near_size, LANE), f32)],
-        cost_estimate=step_cost,
-        name="step",
-    )
-    final_call = pl.pallas_call(
-        final_kernel,
-        in_specs=[smem] + [vmem] * 4,
-        out_specs=vmem,
-        out_shape=jax.ShapeDtypeStruct((comps, rows, lon), f32),
-        scratch_shapes=[pltpu.VMEM((comps, near_size, LANE), f32)],
-        cost_estimate=step_cost,
-        name="final",
-    )
-
-    costs = []
-    own_obs = deposited(own_list)
+    tile = jax.ShapeDtypeStruct((SUB, LANE), f32)
+
+    def round_call(finish, outs):
+        return kernel(
+            functools.partial(round_kernel, finish),
+            [smem, smem] + [any_space] * 14,
+            [vmem] * (finish + 1),
+            outs + [tile],
+            [
+                pltpu.VMEM((comps, near_size, LANE), f32),
+                pltpu.VMEM((comps, far_size, LANE), f32),
+                pltpu.VMEM((comps, band_size, LANE), f32),
+                pltpu.VMEM((comps, near_size, LANE), f32),
+                pltpu.VMEM((far_size, LANE), f32),
+                pltpu.VMEM((rows + 2 * FAR, LANE), f32),
+                pltpu.VMEM((comps, near_size, LANE), f32),
+                pltpu.VMEM((comps, band_size, LANE), f32),
+                pltpu.VMEM((comps, band_size, LANE), f32),
+                pltpu.VMEM((8 * size, LANE), f32),
+                pltpu.SemaphoreType.DMA((23,)),
+            ],
+            45_000_000,
+        )
+
+    def ring_sum(x):
+        total = x
+        for turn in range(1, bands):
+            ring = [(i, (i + turn) % bands) for i in range(bands)]
+            total = total + lax.ppermute(x, "space", ring)
+        return total
+
     for turn in range(ITERS):
         away = turn % 2 == 0
         target = (me ^ 1) if away else me
@@ -491,10 +493,7 @@
         far_e = lax.ppermute(edge, "tm", shift)
         mid_m = lax.ppermute(inner, "tm", swap)
         far_m = lax.ppermute(inner, "tm", shift)
-        if turn == 0:
-            own_obs, mid_e, other_list = lax.optimization_barrier((own_obs, mid_e, other_list))
-            other_obs = deposited(other_list)
-        obs_a, obs_b = other_obs if away else own_obs
+        obs_a, obs_b = deposited(other_list if away else own_list)
         from_north = lax.ppermute(
             jnp.concatenate(
                 [edge[:, 2 * far - near :], mid_e[:, far:], far_e[:, 2 * far - near :]], 1
@@ -511,7 +510,14 @@
         flags = jnp.stack(
             [band > 0, band < bands - 1, target < windows - 1, target == 0]
         ).astype(f32)
-        lam, part, cost = gap_call(
+        if turn < ITERS - 1:
+            outs = [
+                jax.ShapeDtypeStruct((comps, 2 * far, LANE), f32),
+                jax.ShapeDtypeStruct((comps, band_size - 2 * far, LANE), f32),
+            ]
+        else:
+            outs = [jax.ShapeDtypeStruct((comps, rows, lon), f32)]
+        *state, cost = round_call(len(outs), outs)(
             own_lo,
             flags,
             edge,
@@ -529,20 +535,16 @@
             obs_a,
             obs_b,
         )
-        cost = jnp.sum(cost)
-        costs.append(lax.ppermute(cost, "tm", swap) if away else cost)
-        if turn < ITERS - 1:
-            edge, inner = step_call(flags, lam, part, depth_wide, rate_wide)
-        else:
-            state = final_call(flags, lam, part, depth_wide, rate_wide)
-    sums = (jnp.stack(costs) + own_const).reshape(1, ITERS)
-    sums = jnp.pad(sums, ((0, 0), (0, LANE - ITERS)))
-    spread = sums
-    for turn in range(1, bands):
-        ring = [(i, (i + turn) % bands) for i in range(bands)]
-        spread = spread + lax.ppermute(sums, "space", ring)
+        if turn == 0:
+            edge, inner = state
+            edge, own_list = lax.optimization_barrier((edge, own_list))
+            cost = lax.ppermute(cost, "tm", swap)
+            fixed = jnp.full((SUB, LANE), own_const / (SUB * LANE))
+            early = ring_sum(jnp.stack([cost + fixed, fixed]))
     cells = comps * total_rows * lon
-    return state[None], (0.5 / cells) * spread[0, :ITERS, None]
+    late = ring_sum(cost) + early[1]
+    costs = (0.5 / cells) * jnp.stack([jnp.sum(early[0]), jnp.sum(late)])
+    return state[0][None], costs[:, None]
 
 
 def solution(mesh):
@@ -556,6 +558,7 @@
         P("tm", None),
         P("tm", None),
     )
+
     return jax.shard_map(
         per_device,
         mesh=mesh,

time: 196 us -> 166 us (0.85)
  waiting for transfers between devices: 36 us -> 12.9 us
  Pallas kernels: 86 us -> 69.5 us
  local copies, waits for them, and re-layouts: 19 us -> 27.8 us
  other arithmetic: 15.3 us -> 9.8 us
  starting transfers between devices: 37.2 us -> 41.8 us
    ppermute x1, waiting for transfers between devices: 17.4 us -> 0.54 us  [per_device(): other_list = lax.ppermute(own_list, 'tm', swap)]
    pallas_call x6 -> x4, Pallas kernels: 86 us -> 69.5 us  [the longest x2 41.6 us: per_device(): round_call(len(outs), outs)]
    ppermute x4 -> x7, waiting for transfers between devices: 0.01 us -> 12.3 us  [the longest x1 10 us: per_device(): cost = lax.ppermute(cost, 'tm', swap)]
    ppermute x2, waiting for transfers between devices: 9.97 us -> 0.01 us  [per_device(): far_m = lax.ppermute(inner, 'tm', shift)]
    ppermute x2, waiting for transfers between devices: 7.5 us -> 0.01 us  [per_device(): mid_e = lax.ppermute(edge, 'tm', swap)]
    slice x6, local copies, waits for them, and re-layouts: 2.05 us -> 9.3 us  [per_device(): p[band_size - n:]]
    ppermute x4 -> x7, starting transfers between devices: 5.55 us -> 10.4 us  [the longest x6 8.38 us: ring_sum(): total = total + lax.ppermute(x, 'space', ring)]
    ppermute x2, starting transfers between devices: 2.61 us -> 6.95 us  [per_device(): far_e = lax.ppermute(edge, 'tm', shift)]
  transfers between devices with their start and end apart: 19 -> 22, of which waited for: 4 -> 4; matrix products, arithmetic and copies ran while one was open for 14% -> 19% of each run, Pallas kernels for 31% -> 17%
where the time goes in v2:
time: 166 us; the launch traced here: 164 us
  Pallas kernels  69.5 us (42%)
  starting transfers between devices  41.8 us (25%)
  local copies, waits for them, and re-layouts  27.8 us (17%)
  waiting for transfers between devices  12.9 us (8%)
  other arithmetic  9.8 us (6%)
  between operations  2.58 us (2%)
    pallas_call x2, Pallas kernels, per_device(): round_call(len(outs), outs)  41.6 us
    pallas_call x2, Pallas kernels, deposited(): deposit(jnp.concatenate([words[0].astype(jnp.int32), spare]), jnp.concate...  27.9 us
    ppermute x1, waiting for transfers between devices, per_device(): cost = lax.ppermute(cost, 'tm', swap)  10 us
    slice x6, local copies, waits for them, and re-layouts, per_device(): p[band_size - n:]  9.3 us
    ppermute x6, starting transfers between devices, ring_sum(): total = total + lax.ppermute(x, 'space', ring)  8.38 us
    ppermute x2, starting transfers between devices, per_device(): far_e = lax.ppermute(edge, 'tm', shift)  6.95 us
    reshape x3, local copies, waits for them, and re-layouts, folded(): return x.reshape(x.shape[:-2] + (x.shape[-2] * size, LANE))  6.06 us
    ppermute x2, starting transfers between devices, per_device(): mid_e = lax.ppermute(edge, 'tm', swap)  5.3 us
  transfers between devices with their start and end apart: 22, of which 4 were waited for; matrix products, arithmetic and copies ran while one was open for 19% of the time, Pallas kernels for 17%

profile of v2, /device:TPU:0, one launch (start us, length us, event | category | flops | bytes accessed | tf_op | source)
XLA Modules:
  0.0 164.4 jit_solution(4556431629909868529)
XLA Ops:
  3.7 5.3 %collective-permute-start = (f32[3,384,128]{2,1,0:T(8,128)S(1)}, f32[3,384,128]{2,1,0:T(8,128)S(1)}, u32[]{:S(2)}, u32[]{:S(2)}) collective-permute-start(f32[3,384,128]{2,1,0:T(8,128)S(1)} %pad_maximum_fusion.1.own_e), channel_id=1, source_target_pairs={{0,4},{4,0},{8,12},{12,8},{16,20},{20,16},{24,28},{28,24},{1,5},{5... | collective-permute-start | bytes 1769480 | tf_op jit(solution)/shard_map/ppermute | solution.py:492
  11.3 3.1 %collective-permute-start.1 = (f32[3,640,128]{2,1,0:T(8,128)}, f32[3,640,128]{2,1,0:T(8,128)}, u32[]{:S(2)}, u32[]{:S(2)}) collective-permute-start(f32[3,640,128]{2,1,0:T(8,128)} %slice.188.own_m), channel_id=1, source_target_pairs={{0,4},{4,0},{8,12},{12,8},{16,20},{20,16},{24,28},{28,24},{1,5},{5... | collective-permute-start | bytes 2949128 | tf_op jit(solution)/shard_map/ppermute | solution.py:494
  16.2 1.6 fusion.22
  17.8 1.7 %fusion.14 = (f32[1,12,1024]{2,1,0:T(8,128)}, f32[1,12,1024]{2,1,0:T(8,128)}, f32[1,12,1024]{2,1,0:T(8,128)}, f32[1,12,1024]{2,1,0:T(8,128)}, f32[1,12,1024]{2,1,0:T(8,128)}, /*index=5*/f32[1,12,1024]{2,1,0:T(8,128)S(1)}) fusion(f32[3,128,1024]{2,1,0:T(8,128)} %param.11), kind=kLoop, calls=%fused_computation.56 | loop fusion | bytes 589824 | tf_op jit(solution)/shard_map/slice | solution.py:437
  19.6 1.6 slice.159
  25.6 1.6 pad_maximum_fusion.6
  27.3 2.0 %reshape.109 = f32[1024,128]{1,0:T(8,128)} reshape(f32[128,1024]{1,0:T(8,128)} %param.10) | data formatting | bytes 1048576 | tf_op jit(solution)/shard_map/reshape | solution.py:370
  29.2 2.6 %reshape.111 = f32[3,1024,128]{2,1,0:T(8,128)} reshape(f32[3,128,1024]{2,1,0:T(8,128)} %param.11) | data formatting | bytes 3145728 | tf_op jit(solution)/shard_map/reshape | solution.py:370
  36.0 1.5 reshape.108.start
  40.9 3.0 %collective-permute-start.6 = (f32[480,128]{1,0:T(8,128)S(1)}, f32[480,128]{1,0:T(8,128)S(1)}, u32[]{:S(2)}, u32[]{:S(2)}) collective-permute-start(f32[480,128]{1,0:T(8,128)S(1)} %copy-done.14), channel_id=1, source_target_pairs={{0,1},{1,2},{2,3},{4,5},{5,6},{6,7},{8,9},{9,10},{10,11},{12,13},{... | collective-permute-start | bytes 737288 | tf_op jit(solution)/shard_map/ppermute | solution.py:436
  44.7 2.6 %collective-permute-start.4 = (f32[3,384,128]{2,1,0:T(8,128)S(1)}, f32[3,384,128]{2,1,0:T(8,128)S(1)}, u32[]{:S(2)}, u32[]{:S(2)}) collective-permute-start(f32[3,384,128]{2,1,0:T(8,128)S(1)} %pad_maximum_fusion.2), channel_id=1, source_target_pairs={{0,1},{1,2},{2,3},{4,5},{5,6},{6,7},{8,9},{9,10},{10,11},{12,13},{... | collective-permute-start | bytes 1769480 | tf_op jit(solution)/shard_map/ppermute | solution.py:497
  49.6 14.4 %shard_map.95 = (f32[3072,128]{1,0:T(8,128)S(1)}, f32[3072,128]{1,0:T(8,128)S(1)}) custom-call(s32[4112]{0:T(1024)S(1)} %concatenate.59.code, f32[4112]{0:T(1024)S(1)} %concatenate.60.load, f32[4112]{0:T(1024)S(1)} %concatenate.61.value), custom_call_target="tpu_custom_call" | custom-call | flops 20000000 | tf_op jit(solution)/shard_map/pallas_call | solution.py:426
  65.9 20.3 %shard_map.96 = (f32[3,384,128]{2,1,0:T(8,128)}, f32[3,640,128]{2,1,0:T(8,128)S(1)}, f32[8,128]{1,0:T(8,128)S(1)}) custom-call(s32[1]{0:T(128)} %bitcast.5.own_lo, f32[4]{0:T(128)S(1)} %add_convert_fusion.1.flags, f32[3,384,128]{2,1,0:T(8,128)S(1)} %copy-done.3, f32[3,640,128]{2,1,0:T(8,128)} %slice.188.own_m, f32[3,384,128]{2,1,0:T(8,128)S(1)} %copy-done.5, ...), custom_call_target="tpu_custom_call" | custom-call | flops 45000000 | tf_op jit(solution)/shard_map/pallas_call | solution.py:520
  87.2 5.5 %collective-permute-start.11 = (f32[3,384,128]{2,1,0:T(8,128)}, f32[3,384,128]{2,1,0:T(8,128)}, u32[]{:S(2)}, u32[]{:S(2)}) collective-permute-start(f32[3,384,128]{2,1,0:T(8,128)} %get-tuple-element.16.own_e), channel_id=1, source_target_pairs={{0,8},{8,16},{16,24},{12,4},{20,12},{28,20},{1,9},{9,17},{17,25},{... | collective-permute-start | bytes 1769480 | tf_op jit(solution)/shard_map/ppermute | solution.py:493
  94.0 2.0 %collective-permute-start.15 = (f32[8,128]{1,0:T(8,128)S(1)}, f32[8,128]{1,0:T(8,128)S(1)}, u32[]{:S(2)}, u32[]{:S(2)}) collective-permute-start(f32[8,128]{1,0:T(8,128)S(1)} %get-tuple-element.22), channel_id=1, source_target_pairs={{0,4},{4,0},{8,12},{12,8},{16,20},{20,16},{24,28},{28,24},{1,5},{5... | collective-permute-start | bytes 12296 | tf_op jit(solution)/shard_map/ppermute | solution.py:541
  97.0 3.1 %collective-permute-start.12 = (f32[3,640,128]{2,1,0:T(8,128)}, f32[3,640,128]{2,1,0:T(8,128)S(1)}, u32[]{:S(2)}, u32[]{:S(2)}) collective-permute-start(f32[3,640,128]{2,1,0:T(8,128)} %copy-done.8), channel_id=1, source_target_pairs={{0,8},{8,16},{16,24},{12,4},{20,12},{28,20},{1,9},{9,17},{17,25},{... | collective-permute-start | bytes 2949128 | tf_op jit(solution)/shard_map/ppermute | solution.py:495
  100.2 10.0 %collective-permute-done.15 = f32[8,128]{1,0:T(8,128)S(1)} collective-permute-done((f32[8,128]{1,0:T(8,128)S(1)}, f32[8,128]{1,0:T(8,128)S(1)}, u32[]{:S(2)}, u32[]{:S(2)}) %collective-permute-start.15) | collective-permute-done | bytes 4128 | tf_op jit(solution)/shard_map/ppermute | solution.py:541
  110.2 3.5 %collective-permute-start.17 = (f32[2,8,128]{2,1,0:T(8,128)S(1)}, f32[2,8,128]{2,1,0:T(8,128)S(1)}, u32[]{:S(2)}, u32[]{:S(2)}) collective-permute-start(f32[2,8,128]{2,1,0:T(8,128)S(1)} %stack.57), channel_id=1, source_target_pairs={{0,2},{1,3},{2,0},{3,1},{4,6},{5,7},{6,4},{7,5},{8,10},{9,11},{10,... | collective-permute-start | bytes 24584 | tf_op jit(solution)/shard_map/ppermute | solution.py:485
  115.4 2.1 %collective-permute-start.13 = (f32[3,384,128]{2,1,0:T(8,128)S(1)}, f32[3,384,128]{2,1,0:T(8,128)S(1)}, u32[]{:S(2)}, u32[]{:S(2)}) collective-permute-start(f32[3,384,128]{2,1,0:T(8,128)S(1)} %pad_maximum_fusion.4), channel_id=1, source_target_pairs={{0,1},{1,2},{2,3},{4,5},{5,6},{6,7},{8,9},{9,10},{10,11},{12,13},{... | collective-permute-start | bytes 1769480 | tf_op jit(solution)/shard_map/ppermute | solution.py:497
  119.9 13.5 %shard_map.97 = (f32[3072,128]{1,0:T(8,128)S(1)}, f32[3072,128]{1,0:T(8,128)S(1)}) custom-call(s32[4112]{0:T(1024)S(1)} %concatenate.64.code, f32[4112]{0:T(1024)S(1)} %concatenate.65.load, f32[4112]{0:T(1024)S(1)} %concatenate.66.value), custom_call_target="tpu_custom_call" | custom-call | flops 20000000 | tf_op jit(solution)/shard_map/pallas_call | solution.py:426
  133.5 21.3 %shard_map.98 = (f32[3,128,1024]{2,1,0:T(8,128)}, f32[8,128]{1,0:T(8,128)S(1)}) custom-call(s32[1]{0:T(128)} %bitcast.own_lo, f32[4]{0:T(128)S(1)} %add_convert_fusion.flags, f32[3,384,128]{2,1,0:T(8,128)} %get-tuple-element.16.own_e, f32[3,640,128]{2,1,0:T(8,128)S(1)} %copy-done.9, f32[3,384,128]{2,1,0:T(8,128)S(1)} %collective-permute-done.9.mid_e, ...), custom_call_target="tpu_custom_call" | custom-call | flops 45000000 | tf_op jit(solution)/shard_map/pallas_call | solution.py:520
  154.8 2.5 %collective-permute-start.21 = (f32[8,128]{1,0:T(8,128)S(1)}, f32[8,128]{1,0:T(8,128)S(1)}, u32[]{:S(2)}, u32[]{:S(2)}) collective-permute-start(f32[8,128]{1,0:T(8,128)S(1)} %get-tuple-element.23), channel_id=1, source_target_pairs={{0,3},{1,0},{2,1},{3,2},{4,7},{5,4},{6,5},{7,6},{8,11},{9,8},{10,9... | collective-permute-start | bytes 12296 | tf_op jit(solution)/shard_map/ppermute | solution.py:485
  157.3 1.7 %collective-permute-start.20 = (f32[8,128]{1,0:T(8,128)S(1)}, f32[8,128]{1,0:T(8,128)S(1)}, u32[]{:S(2)}, u32[]{:S(2)}) collective-permute-start(f32[8,128]{1,0:T(8,128)S(1)} %get-tuple-element.23), channel_id=1, source_target_pairs={{0,2},{1,3},{2,0},{3,1},{4,6},{5,7},{6,4},{7,5},{8,10},{9,11},{10,... | collective-permute-start | bytes 12296 | tf_op jit(solution)/shard_map/ppermute | solution.py:485
  162.7 1.8 %maximum_multiply_fusion.1 = f32[2,1]{0,1:T(1,128)} fusion(f32[1,1]{0,1:T(1,128)} %bitcast.28, f32[1,1]{0,1:T(1,128)} %bitcast.26), kind=kLoop, calls=%fused_computation.54 | loop fusion | flops 4 | bytes 16 | tf_op jit(solution)/shard_map/mul | solution.py:546
  (124 shorter events, 33.5 us)
Async XLA Ops:
  2.2 29.6 %copy-start.10 = (f32[3,1024,128]{2,1,0:T(8,128)}, f32[3,1024,128]{2,1,0:T(8,128)S(1)}, u32[]{:S(2)}) copy-start(f32[3,1024,128]{2,1,0:T(8,128)S(1)} %reshape_squeeze.3) | copy-start | bytes 4718596
  2.3 37.2 %collective-permute-start.2 = (f32[3,384,128]{2,1,0:T(8,128)S(1)}, f32[3,384,128]{2,1,0:T(8,128)S(1)}, u32[]{:S(2)}, u32[]{:S(2)}) collective-permute-start(f32[3,384,128]{2,1,0:T(8,128)S(1)} %pad_maximum_fusion.1.own_e), channel_id=1, source_target_pairs={{8,0},{16,8},{24,16},{4,12},{12,20},{20,28},{9,1},{17,9},{25,17},{... | collective-permute-start | bytes 1769480 | tf_op jit(solution)/shard_map/ppermute | solution.py:493
  3.7 37.1 %collective-permute-start = (f32[3,384,128]{2,1,0:T(8,128)S(1)}, f32[3,384,128]{2,1,0:T(8,128)S(1)}, u32[]{:S(2)}, u32[]{:S(2)}) collective-permute-start(f32[3,384,128]{2,1,0:T(8,128)S(1)} %pad_maximum_fusion.1.own_e), channel_id=1, source_target_pairs={{0,4},{4,0},{8,12},{12,8},{16,20},{20,16},{24,28},{28,24},{1,5},{5... | collective-permute-start | bytes 1769480 | tf_op jit(solution)/shard_map/ppermute | solution.py:492
  10.0 54.3 %collective-permute-start.3 = (f32[3,640,128]{2,1,0:T(8,128)}, f32[3,640,128]{2,1,0:T(8,128)}, u32[]{:S(2)}, u32[]{:S(2)}) collective-permute-start(f32[3,640,128]{2,1,0:T(8,128)} %slice.188.own_m), channel_id=1, source_target_pairs={{8,0},{16,8},{24,16},{4,12},{12,20},{20,28},{9,1},{17,9},{25,17},{... | collective-permute-start | bytes 2949128 | tf_op jit(solution)/shard_map/ppermute | solution.py:495
  11.3 53.1 %collective-permute-start.1 = (f32[3,640,128]{2,1,0:T(8,128)}, f32[3,640,128]{2,1,0:T(8,128)}, u32[]{:S(2)}, u32[]{:S(2)}) collective-permute-start(f32[3,640,128]{2,1,0:T(8,128)} %slice.188.own_m), channel_id=1, source_target_pairs={{0,4},{4,0},{8,12},{12,8},{16,20},{20,16},{24,28},{28,24},{1,5},{5... | collective-permute-start | bytes 2949128 | tf_op jit(solution)/shard_map/ppermute | solution.py:494
  16.2 28.4 %collective-permute-start.8 = (f32[3,4096]{1,0:T(4,128)}, f32[3,4096]{1,0:T(4,128)}, u32[]{:S(2)}, u32[]{:S(2)}) collective-permute-start(f32[3,4096]{1,0:T(4,128)} %pad_maximum_fusion.8), channel_id=1, source_target_pairs={{0,4},{4,0},{8,12},{12,8},{16,20},{20,16},{24,28},{28,24},{1,5},{5... | collective-permute-start | bytes 147464 | tf_op jit(solution)/shard_map/ppermute | solution.py:397
  39.5 7.8 %collective-permute-start.7 = (f32[480,128]{1,0:T(8,128)S(1)}, f32[480,128]{1,0:T(8,128)S(1)}, u32[]{:S(2)}, u32[]{:S(2)}) collective-permute-start(f32[480,128]{1,0:T(8,128)S(1)} %pad_maximum_fusion.7), channel_id=1, source_target_pairs={{1,0},{2,1},{3,2},{5,4},{6,5},{7,6},{9,8},{10,9},{11,10},{13,12},{... | collective-permute-start | bytes 737288 | tf_op jit(solution)/shard_map/ppermute | solution.py:441
  40.9 23.2 %collective-permute-start.6 = (f32[480,128]{1,0:T(8,128)S(1)}, f32[480,128]{1,0:T(8,128)S(1)}, u32[]{:S(2)}, u32[]{:S(2)}) collective-permute-start(f32[480,128]{1,0:T(8,128)S(1)} %copy-done.14), channel_id=1, source_target_pairs={{0,1},{1,2},{2,3},{4,5},{5,6},{6,7},{8,9},{9,10},{10,11},{12,13},{... | collective-permute-start | bytes 737288 | tf_op jit(solution)/shard_map/ppermute | solution.py:436
  44.7 19.7 %collective-permute-start.4 = (f32[3,384,128]{2,1,0:T(8,128)S(1)}, f32[3,384,128]{2,1,0:T(8,128)S(1)}, u32[]{:S(2)}, u32[]{:S(2)}) collective-permute-start(f32[3,384,128]{2,1,0:T(8,128)S(1)} %pad_maximum_fusion.2), channel_id=1, source_target_pairs={{0,1},{1,2},{2,3},{4,5},{5,6},{6,7},{8,9},{9,10},{10,11},{12,13},{... | collective-permute-start | bytes 1769480 | tf_op jit(solution)/shard_map/ppermute | solution.py:497
  47.3 17.1 %collective-permute-start.5 = (f32[3,384,128]{2,1,0:T(8,128)S(1)}, f32[3,384,128]{2,1,0:T(8,128)S(1)}, u32[]{:S(2)}, u32[]{:S(2)}) collective-permute-start(f32[3,384,128]{2,1,0:T(8,128)S(1)} %pad_maximum_fusion.3), channel_id=1, source_target_pairs={{1,0},{2,1},{3,2},{5,4},{6,5},{7,6},{9,8},{10,9},{11,10},{13,12},{... | collective-permute-start | bytes 1769480 | tf_op jit(solution)/shard_map/ppermute | solution.py:504
  65.9 26.8 %copy-start.20 = (f32[1,4096]{1,0:T(1,128)S(1)}, f32[1,4096]{1,0:T(1,128)}, u32[]{:S(2)}) copy-start(f32[1,4096]{1,0:T(1,128)} %param.15) | copy-start | bytes 49156
  87.2 26.5 %collective-permute-start.11 = (f32[3,384,128]{2,1,0:T(8,128)}, f32[3,384,128]{2,1,0:T(8,128)}, u32[]{:S(2)}, u32[]{:S(2)}) collective-permute-start(f32[3,384,128]{2,1,0:T(8,128)} %get-tuple-element.16.own_e), channel_id=1, source_target_pairs={{0,8},{8,16},{16,24},{12,4},{20,12},{28,20},{1,9},{9,17},{17,25},{... | collective-permute-start | bytes 1769480 | tf_op jit(solution)/shard_map/ppermute | solution.py:493
  94.0 20.7 %collective-permute-start.9 = (f32[3,384,128]{2,1,0:T(8,128)}, f32[3,384,128]{2,1,0:T(8,128)S(1)}, u32[]{:S(2)}, u32[]{:S(2)}) collective-permute-start(f32[3,384,128]{2,1,0:T(8,128)} %get-tuple-element.16.own_e), channel_id=1, source_target_pairs={{0,4},{4,0},{8,12},{12,8},{16,20},{20,16},{24,28},{28,24},{1,5},{5... | collective-permute-start | bytes 1769480 | tf_op jit(solution)/shard_map/ppermute | solution.py:492
  94.0 16.2 %collective-permute-start.15 = (f32[8,128]{1,0:T(8,128)S(1)}, f32[8,128]{1,0:T(8,128)S(1)}, u32[]{:S(2)}, u32[]{:S(2)}) collective-permute-start(f32[8,128]{1,0:T(8,128)S(1)} %get-tuple-element.22), channel_id=1, source_target_pairs={{0,4},{4,0},{8,12},{12,8},{16,20},{20,16},{24,28},{28,24},{1,5},{5... | collective-permute-start | bytes 12296 | tf_op jit(solution)/shard_map/ppermute | solution.py:541
  97.0 36.4 %collective-permute-start.12 = (f32[3,640,128]{2,1,0:T(8,128)}, f32[3,640,128]{2,1,0:T(8,128)S(1)}, u32[]{:S(2)}, u32[]{:S(2)}) collective-permute-start(f32[3,640,128]{2,1,0:T(8,128)} %copy-done.8), channel_id=1, source_target_pairs={{0,8},{8,16},{16,24},{12,4},{20,12},{28,20},{1,9},{9,17},{17,25},{... | collective-permute-start | bytes 2949128 | tf_op jit(solution)/shard_map/ppermute | solution.py:495
  100.1 33.3 %collective-permute-start.10 = (f32[3,640,128]{2,1,0:T(8,128)}, f32[3,640,128]{2,1,0:T(8,128)S(1)}, u32[]{:S(2)}, u32[]{:S(2)}) collective-permute-start(f32[3,640,128]{2,1,0:T(8,128)} %copy-done.8), channel_id=1, source_target_pairs={{0,4},{4,0},{8,12},{12,8},{16,20},{20,16},{24,28},{28,24},{1,5},{5... | collective-permute-start | bytes 2949128 | tf_op jit(solution)/shard_map/ppermute | solution.py:494
  110.2 5.2 %collective-permute-start.17 = (f32[2,8,128]{2,1,0:T(8,128)S(1)}, f32[2,8,128]{2,1,0:T(8,128)S(1)}, u32[]{:S(2)}, u32[]{:S(2)}) collective-permute-start(f32[2,8,128]{2,1,0:T(8,128)S(1)} %stack.57), channel_id=1, source_target_pairs={{0,2},{1,3},{2,0},{3,1},{4,6},{5,7},{6,4},{7,5},{8,10},{9,11},{10,... | collective-permute-start | bytes 24584 | tf_op jit(solution)/shard_map/ppermute | solution.py:485
  113.7 3.9 %collective-permute-start.18 = (f32[2,8,128]{2,1,0:T(8,128)S(1)}, f32[2,8,128]{2,1,0:T(8,128)S(1)}, u32[]{:S(2)}, u32[]{:S(2)}) collective-permute-start(f32[2,8,128]{2,1,0:T(8,128)S(1)} %stack.57), channel_id=1, source_target_pairs={{0,3},{1,0},{2,1},{3,2},{4,7},{5,4},{6,5},{7,6},{8,11},{9,8},{10,9... | collective-permute-start | bytes 24584 | tf_op jit(solution)/shard_map/ppermute | solution.py:485
  114.7 18.7 %collective-permute-start.16 = (f32[2,8,128]{2,1,0:T(8,128)S(1)}, f32[2,8,128]{2,1,0:T(8,128)S(1)}, u32[]{:S(2)}, u32[]{:S(2)}) collective-permute-start(f32[2,8,128]{2,1,0:T(8,128)S(1)} %stack.57), channel_id=1, source_target_pairs={{0,1},{1,2},{2,3},{3,0},{4,5},{5,6},{6,7},{7,4},{8,9},{9,10},{10,1... | collective-permute-start | bytes 24584 | tf_op jit(solution)/shard_map/ppermute | solution.py:485
  115.4 18.0 %collective-permute-start.13 = (f32[3,384,128]{2,1,0:T(8,128)S(1)}, f32[3,384,128]{2,1,0:T(8,128)S(1)}, u32[]{:S(2)}, u32[]{:S(2)}) collective-permute-start(f32[3,384,128]{2,1,0:T(8,128)S(1)} %pad_maximum_fusion.4), channel_id=1, source_target_pairs={{0,1},{1,2},{2,3},{4,5},{5,6},{6,7},{8,9},{9,10},{10,11},{12,13},{... | collective-permute-start | bytes 1769480 | tf_op jit(solution)/shard_map/ppermute | solution.py:497
  117.5 15.9 %collective-permute-start.14 = (f32[3,384,128]{2,1,0:T(8,128)S(1)}, f32[3,384,128]{2,1,0:T(8,128)S(1)}, u32[]{:S(2)}, u32[]{:S(2)}) collective-permute-start(f32[3,384,128]{2,1,0:T(8,128)S(1)} %pad_maximum_fusion.5), channel_id=1, source_target_pairs={{1,0},{2,1},{3,2},{5,4},{6,5},{7,6},{9,8},{10,9},{11,10},{13,12},{... | collective-permute-start | bytes 1769480 | tf_op jit(solution)/shard_map/ppermute | solution.py:504
  154.8 4.9 %collective-permute-start.21 = (f32[8,128]{1,0:T(8,128)S(1)}, f32[8,128]{1,0:T(8,128)S(1)}, u32[]{:S(2)}, u32[]{:S(2)}) collective-permute-start(f32[8,128]{1,0:T(8,128)S(1)} %get-tuple-element.23), channel_id=1, source_target_pairs={{0,3},{1,0},{2,1},{3,2},{4,7},{5,4},{6,5},{7,6},{8,11},{9,8},{10,9... | collective-permute-start | bytes 12296 | tf_op jit(solution)/shard_map/ppermute | solution.py:485
  157.3 3.6 %collective-permute-start.20 = (f32[8,128]{1,0:T(8,128)S(1)}, f32[8,128]{1,0:T(8,128)S(1)}, u32[]{:S(2)}, u32[]{:S(2)}) collective-permute-start(f32[8,128]{1,0:T(8,128)S(1)} %get-tuple-element.23), channel_id=1, source_target_pairs={{0,2},{1,3},{2,0},{3,1},{4,6},{5,7},{6,4},{7,5},{8,10},{9,11},{10,... | collective-permute-start | bytes 12296 | tf_op jit(solution)/shard_map/ppermute | solution.py:485
  159.0 3.0 %collective-permute-start.19 = (f32[8,128]{1,0:T(8,128)S(1)}, f32[8,128]{1,0:T(8,128)S(1)}, u32[]{:S(2)}, u32[]{:S(2)}) collective-permute-start(f32[8,128]{1,0:T(8,128)S(1)} %get-tuple-element.23), channel_id=1, source_target_pairs={{0,1},{1,2},{2,3},{3,0},{4,5},{5,6},{6,7},{7,4},{8,9},{9,10},{10,1... | collective-permute-start | bytes 12296 | tf_op jit(solution)/shard_map/ppermute | solution.py:485
  (19 other events, 180.5 us)

commit v3 on v2

v3 whole, which is shorter than its diff:
```python
import functools
import math

import jax
import jax.numpy as jnp
from jax import lax
from jax.experimental import pallas as pl
from jax.experimental.pallas import tpu as pltpu
from jax.sharding import PartitionSpec as P


STEPS = 6
ITERS = 2
COURANT = 0.35
CORIOLIS_MAX = 0.2
STEP_SIZE = 0.2

SUB = 8
LANE = 128
NEAR = 2 * STEPS
FAR = 4 * STEPS
GROUPS = 4
DEALS = 4
HALF = 0.5 * COURANT
LEAD = 24

EDGE_W = 16


def turned(x):
    return pltpu.roll(x, LANE - 1, 1), pltpu.roll(x, 1, 1)


def raw_lon(pair, first, last):
    ahead, behind = pair
    size = ahead.shape[0]
    ahead = jnp.where(last, pltpu.roll(ahead, size - 1, 0), ahead)
    behind = jnp.where(first, pltpu.roll(behind, 1, 0), behind)
    return ahead - behind


def sweep(state, depth, rate, off, halo, edge_ref, forward):
    count = rate.shape[0] - 2 * off
    north, south = halo - 1, count - halo

    def one(_, carry):
        lane = lax.broadcasted_iota(jnp.int32, depth.shape[1:], 1)
        first, last = lane == 0, lane == LANE - 1
        flows, tops, pairs_a, pairs_b = {}, {}, {}, {}

        def coef(r):
            return depth[off + r]

        def rot(r):
            return rate[pl.ds(off + r, 1), :]

        def masked(r, x):
            if r == north:
                return x * edge_ref[0]
            if r == south:
                return x * edge_ref[1]
            return x

        def prepare(r):
            v = state[1, r]
            flows[r] = coef(r) * v if forward else v

        def lat(values, r):
            return values[min(r + 1, count - 1)] - values[max(r - 1, 0)]

        def open_a(r):
            if forward:
                pairs_a[r] = turned(coef(r) * state[0, r])
            else:
                mix = state[0, r] - rot(r) * state[1, r]
                state[0, r] = mix
                pairs_a[r] = turned(mix)

        def close_a(r):
            if r + 1 < count:
                prepare(r + 1)
            slope = raw_lon(pairs_a.pop(r), first, last) + lat(flows, r)
            old = state[2, r]
            tops[r] = masked(r, old - slope if forward else old + slope)
            state[2, r] = tops[r]
            pairs_b[r] = turned(tops[r])

        def close_b(r):
            u, v = state[0, r], state[1, r]
            slope = raw_lon(pairs_b.pop(r), first, last)
            if r + 1 < count:
                above = state[2, r + 1]
            else:
                above = tops[r]
            rise = above - state[2, max(r - 1, 0)]
            if forward:
                u = u + rot(r) * v - slope
                state[0, r] = u
                state[1, r] = v - rot(r) * u - rise
            else:
                state[0, r] = u + coef(r) * slope
                state[1, r] = v + rot(r) * u + coef(r) * rise

        prepare(0)
        for r in range(-LEAD, count + LEAD):
            if 0 <= r + LEAD < count:
                open_a(r + LEAD)
            if 0 <= r < count:
                close_a(r)
            if 0 <= r - LEAD < count:
                close_b(r - LEAD)
        return carry

    lax.fori_loop(0, STEPS, one, 0)


def over(count, body, block=8):
    trips = count // block

    def step(n, carry):
        body(n * block)
        return carry

    lax.fori_loop(0, trips, step, 0, unroll=2 if trips % 2 == 0 else 1)


def run(copies):
    for c in copies:
        c.start()
    for c in copies:
        c.wait()


def unfold(src, dst, row, sems, slot):
    columns, rows = dst.shape[-2], src.shape[-2]
    lead = (slice(None),) * (len(src.shape) - 2)
    return [
        pltpu.make_async_copy(
            src.at[lead + (slice(None), pl.ds(s * LANE, LANE))],
            dst.at[lead + (pl.ds(row, rows), s)],
            sems.at[slot + s],
        )
        for s in range(columns)
    ]


def pack_kernel(own, mid, far, southward, northward):
    for src, rows, at in ((own, NEAR, 0), (mid, FAR, NEAR), (far, NEAR, NEAR + FAR)):
        last = src.shape[1] - rows
        southward[:, pl.ds(at, rows)] = src[:, pl.ds(last, rows)]
        northward[:, pl.ds(at, rows)] = src[:, pl.ds(0, rows)]


def fixed_kernel(weight, depth, southward, northward, sems):
    parts, rows, _ = weight.shape
    copies = []
    for k, (dst, w, d) in enumerate(((southward, rows - EDGE_W, rows - FAR), (northward, 0, 0))):
        moves = [
            (weight.at[p, pl.ds(w, EDGE_W)], dst.at[pl.ds(p * EDGE_W, EDGE_W)])
            for p in range(parts)
        ]
        moves.append((depth.at[pl.ds(d, FAR)], dst.at[pl.ds(parts * EDGE_W, FAR)]))
        for n, (src, out) in enumerate(moves):
            copies.append(pltpu.make_async_copy(src, out, sems.at[k * (parts + 1) + n]))
    run(copies)


def round_kernel(
    finish,
    own_lo,
    flags,
    own_e,
    own_m,
    mid_e,
    mid_m,
    far_e,
    far_m,
    from_north,
    from_south,
    start,
    depth,
    rate,
    weight,
    fixed_n,
    fixed_s,
    obs_a,
    obs_b,
    *refs,
):
    outs, cost_out = refs[:finish], refs[finish]
    lo, mid, kept, hi, depth_v, rate_v, weight_v, a_v, b_v, cost_v, sems, wide_sems = refs[
        finish + 1 :
    ]
    rows = kept.shape[1]
    inner = rows - 2 * FAR
    columns = kept.shape[2]

    def assemble(dst, halo, e, m, at, slot):
        pieces = [
            (from_north.at[:, pl.ds(at, halo)], 0, halo),
            (e.at[:, pl.ds(0, FAR)], halo, FAR),
            (m, halo + FAR, inner),
            (e.at[:, pl.ds(FAR, FAR)], halo + FAR + inner, FAR),
            (from_south.at[:, pl.ds(at, halo)], halo + rows, halo),
        ]
        return [
            pltpu.make_async_copy(src, dst.at[:, pl.ds(where, length)], sems.at[slot + n])
            for n, (src, where, length) in enumerate(pieces)
        ]

    own_at, mid_at, far_at = 0, NEAR, NEAR + FAR
    is_own_lo = own_lo[0] == 1
    c_rate = pltpu.make_async_copy(rate, rate_v, sems.at[0])
    c_mid = assemble(mid, FAR, mid_e, mid_m, mid_at, 2)
    lo_own = assemble(lo, NEAR, own_e, own_m, own_at, 7)
    lo_far = assemble(lo, NEAR, far_e, far_m, far_at, 7)
    hi_own = assemble(hi, NEAR, own_e, own_m, own_at, 12)
    hi_far = assemble(hi, NEAR, far_e, far_m, far_at, 12)
    c_kept = [
        pltpu.make_async_copy(mid_e.at[:, pl.ds(0, FAR)], kept.at[:, pl.ds(0, FAR)], sems.at[17]),
        pltpu.make_async_copy(mid_m, kept.at[:, pl.ds(FAR, inner)], sems.at[18]),
        pltpu.make_async_copy(
            mid_e.at[:, pl.ds(FAR, FAR)], kept.at[:, pl.ds(FAR + inner, FAR)], sems.at[19]
        ),
    ]
    c_a = pltpu.make_async_copy(obs_a, a_v, sems.at[20])
    c_b = pltpu.make_async_copy(obs_b, b_v, sems.at[21])
    c_depth = unfold(depth, depth_v, FAR, wide_sems, 0)
    c_weight = unfold(weight, weight_v, EDGE_W, wide_sems, columns)
    for n, (fixed, top_d, top_w) in enumerate(
        ((fixed_n, 0, 0), (fixed_s, FAR + rows, EDGE_W + rows))
    ):
        slot = (2 + 4 * n) * columns
        for p in range(3):
            c_weight += unfold(
                fixed.at[pl.ds(p * EDGE_W, EDGE_W)],
                weight_v.at[p],
                top_w,
                wide_sems,
                slot + p * columns,
            )
        c_depth += unfold(
            fixed.at[pl.ds(3 * EDGE_W, FAR)], depth_v, top_d, wide_sems, slot + 3 * columns
        )
    for c in c_depth + [c_rate] + c_mid:
        c.start()

    @pl.when(is_own_lo)
    def _():
        for c in lo_own + hi_far:
            c.start()

    @pl.when(jnp.logical_not(is_own_lo))
    def _():
        for c in lo_far + hi_own:
            c.start()

    for c in c_weight + c_kept + [c_a, c_b]:
        c.start()

    def scale_third(ref, where, length, block):
        def body(n):
            at = pl.ds(where + n, block)
            ref[2, at] = ref[2, at] * HALF

        over(length, body, block)

    for c in c_depth + [c_rate]:
        c.wait()

    def scale_depth(n):
        depth_v[pl.ds(n, 8)] = depth_v[pl.ds(n, 8)] * (HALF * HALF)

    over(depth_v.shape[0], scale_depth)
    for c in c_mid:
        c.wait()

    scale_third(mid, 0, mid.shape[1], 8)
    sweep(mid, depth_v, rate_v, 0, FAR, flags, True)
    for c in lo_own:
        c.wait()

    scale_third(lo, 0, lo.shape[1], 8)
    sweep(lo, depth_v, rate_v, FAR - NEAR, NEAR, flags, True)
    for c in hi_own + c_weight:
        c.wait()

    shift = EDGE_W - NEAR
    for part in range(3):
        back_scale = 1.0 / HALF if part == 2 else 1.0

        def body(n):
            at = pl.ds(n, 8)
            end = mid[part, pl.ds(FAR - NEAR + n, 8)] * back_scale
            lam = weight_v[part, pl.ds(shift + n, 8)] * (hi[part, at] - end)
            hi[part, at] = lam * (flags[2] * back_scale)

        over(hi.shape[1], body)

    for c in c_kept + [c_a, c_b]:
        c.wait()

    @pl.when(flags[3] > 0.5)
    def _():
        run(unfold(start, lo, NEAR, wide_sems, 0))
        scale_third(lo, NEAR, rows, 8)

    cost_v[...] = jnp.zeros_like(cost_v)
    for part in range(3):
        back_scale = 1.0 / HALF if part == 2 else 1.0

        def body(n):
            at = pl.ds(n, 8)
            here = kept[part, at]
            gap = here - lo[part, pl.ds(NEAR + n, 8)] * back_scale
            lam = weight_v[part, pl.ds(EDGE_W + n, 8)] * gap
            pull = a_v[part, at] * here
            kept[part, at] = here - STEP_SIZE * (lam + (pull - b_v[part, at]))
            cost_v[...] += lam * gap + here * (pull - 2.0 * b_v[part, at])

        over(rows, body)

    total = cost_v[0]
    for n in range(1, cost_v.shape[0]):
        total = total + cost_v[n]
    cost_out[...] = total

    sweep(hi, depth_v, rate_v, FAR - NEAR, NEAR, flags, False)
    copies = []
    for part in range(3):
        scale = STEP_SIZE * (HALF if part == 2 else 1.0)

        def add(n):
            at = pl.ds(n, 8)
            kept[part, at] = kept[part, at] + scale * hi[part, pl.ds(NEAR + n, 8)]

        over(rows, add)
        if finish == 2:
            moves = [
                (kept.at[part, pl.ds(0, FAR)], outs[0].at[part, pl.ds(0, FAR)]),
                (kept.at[part, pl.ds(rows - FAR, FAR)], outs[0].at[part, pl.ds(FAR, FAR)]),
                (kept.at[part, pl.ds(FAR, inner)], outs[1].at[part]),
            ]
        else:
            moves = [
                (kept.at[part, :, s], outs[0].at[part, :, pl.ds(s * LANE, LANE)])
                for s in range(columns)
            ]
        for n, (src, dst) in enumerate(moves):
            copies.append(pltpu.make_async_copy(src, dst, wide_sems.at[part * columns + n]))
            copies[-1].start()
    for c in copies:
        c.wait()


def deposit_kernel(plane, place, entries, a_out, b_out, const_out, *refs):
    words_v, words, picked, sems = refs[:4]
    values_v, values = refs[4:6]
    acc = refs[6:]
    a_acc, b_acc = acc[:GROUPS], acc[GROUPS:]
    comps, rows, columns, _ = a_out.shape
    lon = columns * LANE
    shift = lon.bit_length() - 1
    count, lanes = entries.shape[1:]
    spare = comps * rows

    index = entries[0].astype(jnp.int32)
    part = jnp.zeros_like(index)
    for n in range(1, comps):
        part = part + (index >= n * plane).astype(jnp.int32)
    rest = index - part * plane
    local = (rest >> shift) - place[0]
    kept = (index >= 0) & (local >= 0) & (local < rows)
    kept_f = kept.astype(jnp.float32)
    load = entries[2] * kept_f
    pulled = load * entries[1]
    row = lax.broadcasted_iota(jnp.int32, (lanes, lanes), 0)
    col = lax.broadcasted_iota(jnp.int32, (lanes, lanes), 1)
    before = (row < col).astype(jnp.float32)
    row = lax.broadcasted_iota(jnp.int32, (count, count), 0)
    col = lax.broadcasted_iota(jnp.int32, (count, count), 1)
    above = (col < row).astype(jnp.float32)
    dot = functools.partial(jnp.dot, preferred_element_type=jnp.float32)
    found = dot(kept_f, before) + dot(dot(above, kept_f), jnp.ones((lanes, lanes), jnp.float32))
    words_v[0] = found.astype(jnp.int32)
    words_v[1] = jnp.where(kept, ((part * rows + local) << shift) + (rest & (lon - 1)), spare << shift)
    values_v[0] = load
    values_v[1] = pulled
    const_out[...] = jnp.sum(
        (pulled * entries[1]).reshape(count // SUB, SUB, lanes), axis=0
    )
    copies = [
        pltpu.make_async_copy(words_v, words, sems.at[0]),
        pltpu.make_async_copy(values_v, values, sems.at[1]),
    ]
    for c in copies:
        c.start()

    zero = jnp.zeros((8, columns, LANE), jnp.float32)

    def clear(n):
        for ref in acc:
            ref[pl.ds(n, 8)] = zero

    over(spare, clear)
    column = lax.broadcasted_iota(jnp.int32, (columns, LANE), 0) * LANE
    column = column + lax.broadcasted_iota(jnp.int32, (columns, LANE), 1)
    for c in copies:
        c.wait()

    def pick(n, carry):
        for k in range(lanes):
            picked[words[0, n, k]] = n * lanes + k
        return carry

    lax.fori_loop(0, count, pick, 0)
    live = words[0, count - 1, lanes - 1]
    live = live + (words[1, count - 1, lanes - 1] < (spare << shift)).astype(jnp.int32)
    step = GROUPS * DEALS

    def body(n, carry):
        for k in range(DEALS):
            for g in range(GROUPS):
                at = n * step + (k * GROUPS + g)
                i = jnp.where(at < live, picked[at], 0)
                r, c = i >> (lanes.bit_length() - 1), i & (lanes - 1)
                word = jnp.where(at < live, words[1, r, c], spare << shift)
                hit = column == (word & (lon - 1))
                to = word >> shift
                a_acc[g][to] = a_acc[g][to] + jnp.where(hit, values[0, r, c], 0.0)
                b_acc[g][to] = b_acc[g][to] + jnp.where(hit, values[1, r, c], 0.0)
        return carry

    lax.fori_loop(0, (live + step - 1) // step, body, 0)
    copies = []
    for n in range(comps):

        def total(r):
            at = pl.ds(n * rows + r, 8)
            for group in (a_acc, b_acc):
                group[0][at] = (group[0][at] + group[1][at]) + (group[2][at] + group[3][at])

        over(rows, total)
        for k, (out, group) in enumerate(((a_out, a_acc), (b_out, b_acc))):
            copies.append(
                pltpu.make_async_copy(
                    group[0].at[pl.ds(n * rows, rows)], out.at[n], sems.at[2 + 2 * n + k]
                )
            )
            copies[-1].start()
    for c in copies:
        c.wait()


def per_device(
    increments, start_state, depth, error_weight, obs_index, obs_count, obs_value, obs_weight
):
    _, comps, rows, lon = increments.shape
    bands = lax.axis_size("space")
    windows = lax.axis_size("tm")
    band = lax.axis_index("space")
    me = lax.axis_index("tm")
    even = me % 2 == 0
    total_rows = rows * bands
    first_row = band * rows
    columns = lon // LANE
    f32 = jnp.float32
    hbm = pl.BlockSpec(memory_space=pltpu.HBM)
    smem = pl.BlockSpec(memory_space=pltpu.SMEM)
    vmem = pl.BlockSpec(memory_space=pltpu.VMEM)

    swap = [(i, i ^ 1) for i in range(windows)]
    inward = [(i, i - 2) for i in range(2, windows) if i % 2 == 0] + [
        (i, i + 2) for i in range(windows - 2) if i % 2 == 1
    ]
    outward = [(b, a) for a, b in inward]
    southward = [(i, i + 1) for i in range(bands - 1)]
    northward = [(b, a) for a, b in southward]

    own = increments[0].reshape(comps, rows, columns, LANE)
    edge = jnp.concatenate([own[:, :FAR], own[:, rows - FAR :]], 1)
    inner = own[:, FAR : rows - FAR]

    number = obs_index.shape[1]
    index = jnp.where(jnp.arange(number) < obs_count[0], obs_index[0], -1).astype(f32)
    own_list = jnp.stack([index, obs_value[0], obs_weight[0]])
    own_list = own_list.reshape(3, number // LANE, LANE)
    other_list = lax.ppermute(own_list, "tm", swap)

    def kernel(body, in_specs, out_specs, outs, scratch, flops):
        return pl.pallas_call(
            body,
            in_specs=in_specs,
            out_specs=out_specs,
            out_shape=outs,
            scratch_shapes=scratch,
            cost_estimate=pl.CostEstimate(flops=flops, bytes_accessed=0, transcendentals=0),
        )

    def field(*shape):
        return jax.ShapeDtypeStruct(shape + (columns, LANE), f32)

    def held(*shape):
        return pltpu.VMEM(shape + (columns, LANE), f32)

    tile = jax.ShapeDtypeStruct((SUB, LANE), f32)
    list_shape = own_list.shape[1:]
    deposit = kernel(
        functools.partial(deposit_kernel, total_rows * lon),
        [smem, vmem],
        [hbm, hbm, vmem],
        [field(comps, rows), field(comps, rows), tile],
        [
            pltpu.VMEM((2,) + list_shape, jnp.int32),
            pltpu.SMEM((2,) + list_shape, jnp.int32),
            pltpu.SMEM((number + GROUPS * DEALS,), jnp.int32),
            pltpu.SemaphoreType.DMA((2 + 2 * comps,)),
            pltpu.VMEM((2,) + list_shape, f32),
            pltpu.SMEM((2,) + list_shape, f32),
        ]
        + [held(comps * rows + 1)] * (2 * GROUPS),
        20_000_000,
    )
    place = jnp.reshape(first_row, (1,)).astype(jnp.int32)

    latitude = (
        (first_row - FAR + jnp.arange(rows + 2 * FAR)).astype(f32) + 0.5
    ) / total_rows * math.pi - math.pi / 2
    rate_wide = jnp.broadcast_to(
        (CORIOLIS_MAX * jnp.sin(latitude))[:, None], (rows + 2 * FAR, LANE)
    )

    small = pltpu.CompilerParams(vmem_limit_bytes=12 << 20)
    pack = pl.pallas_call(
        pack_kernel,
        in_specs=[vmem] * 3,
        out_specs=[vmem] * 2,
        out_shape=[field(comps, 2 * NEAR + FAR)] * 2,
        compiler_params=small,
        name="pack",
    )
    fixed = pl.pallas_call(
        fixed_kernel,
        in_specs=[hbm] * 2,
        out_specs=[vmem] * 2,
        out_shape=[jax.ShapeDtypeStruct((comps * EDGE_W + FAR, lon), f32)] * 2,
        scratch_shapes=[pltpu.SemaphoreType.DMA((2 * (comps + 1),))],
        compiler_params=small,
        name="fixed",
    )
    to_south, to_north = fixed(error_weight, depth)
    fixed_n = lax.ppermute(to_south, "space", southward)
    fixed_s = lax.ppermute(to_north, "space", northward)

    def round_call(finish, outs):
        return kernel(
            functools.partial(round_kernel, finish),
            [smem, smem] + [hbm] * 16,
            [hbm] * finish + [vmem],
            outs + [tile],
            [
                held(comps, rows + 2 * NEAR),
                held(comps, rows + 2 * FAR),
                held(comps, rows),
                held(comps, rows + 2 * NEAR),
                held(rows + 2 * FAR),
                pltpu.VMEM((rows + 2 * FAR, LANE), f32),
                held(comps, rows + 2 * EDGE_W),
                held(comps, rows),
                held(comps, rows),
                held(8),
                pltpu.SemaphoreType.DMA((22,)),
                pltpu.SemaphoreType.DMA((10 * columns,)),
            ],
            45_000_000,
        )

    def ring_sum(x):
        total = x
        for turn in range(1, bands):
            ring = [(i, (i + turn) % bands) for i in range(bands)]
            total = total + lax.ppermute(x, "space", ring)
        return total

    for turn in range(ITERS):
        away = turn % 2 == 0
        target = (me ^ 1) if away else me
        shift = inward if away else outward
        mid_e = lax.ppermute(edge, "tm", swap)
        far_e = lax.ppermute(edge, "tm", shift)
        mid_m = lax.ppermute(inner, "tm", swap)
        far_m = lax.ppermute(inner, "tm", shift)
        if away:
            _, mid_e = lax.optimization_barrier((to_south, mid_e))
        to_south, to_north = pack(edge, mid_e, far_e)
        entries = other_list if away else own_list
        to_south, entries = lax.optimization_barrier((to_south, entries))
        obs_a, obs_b, const = deposit(place, entries)
        from_north = lax.ppermute(to_south, "space", southward)
        from_south = lax.ppermute(to_north, "space", northward)
        own_lo = (even if away else ~even).astype(jnp.int32).reshape(1)
        flags = jnp.stack(
            [band > 0, band < bands - 1, target < windows - 1, target == 0]
        ).astype(f32)
        if turn < ITERS - 1:
            outs = [field(comps, 2 * FAR), field(comps, rows - 2 * FAR)]
        else:
            outs = [jax.ShapeDtypeStruct((comps, rows, lon), f32)]
        *state, cost = round_call(len(outs), outs)(
            own_lo,
            flags,
            edge,
            inner,
            mid_e,
            mid_m,
            far_e,
            far_m,
            from_north,
            from_south,
            start_state,
            depth,
            rate_wide,
            error_weight,
            fixed_n,
            fixed_s,
            obs_a,
            obs_b,
        )
        if turn == 0:
            edge, inner = state
            early = lax.ppermute(cost + const, "tm", swap)
    early, cost = lax.optimization_barrier((early, cost))
    sums = ring_sum(jnp.stack([early, cost + const]))
    cells = comps * total_rows * lon
    return state[0][None], (0.5 / cells) * jnp.sum(sums, (1, 2))[:, None]


def solution(mesh):
    placed = (
        P("tm", None, "space", None),
        P(None, "space", None),
        P("space", None),
        P(None, "space", None),
        P("tm", None),
        P("tm"),
        P("tm", None),
        P("tm", None),
    )

    return jax.shard_map(
        per_device,
        mesh=mesh,
        in_specs=placed,
        out_specs=(P("tm", None, "space", None), P(None, "tm")),
        check_vma=False,
    )
```

time: 166 us -> 164 us (0.988)
  waiting for transfers between devices: 12.9 us -> 42.8 us
  local copies, waits for them, and re-layouts: 27.8 us -> 5.1 us
  other arithmetic: 9.8 us -> 2.76 us
  starting transfers between devices: 41.8 us -> 37.1 us
  Pallas kernels: 69.5 us -> 72.2 us
    ppermute x1, waiting for transfers between devices: 0.54 us -> 19.6 us  [per_device(): other_list = lax.ppermute(own_list, 'tm', swap)]
    slice x22 -> x2, local copies, waits for them, and re-layouts: 17.7 us -> 1.06 us  [the longest x1 1.01 us: per_device(): inner = own[:, FAR:rows - FAR]]
    ppermute x7, waiting for transfers between devices: 10 us -> 0.02 us  [the longest x2 0.01 us: per_device(): from_south = lax.ppermute(to_north, 'space', northward)]
    ppermute x2, waiting for transfers between devices: 0.01 us -> 9.09 us  [per_device(): mid_e = lax.ppermute(edge, 'tm', swap)]
    ppermute x2, waiting for transfers between devices: 0.01 us -> 8.91 us  [per_device(): far_e = lax.ppermute(edge, 'tm', shift)]
    ppermute x6 -> x3, starting transfers between devices: 8.38 us -> 1.69 us  [ring_sum(): total = total + lax.ppermute(x, 'space', ring)]
    reshape x3 -> x0, local copies, waits for them, and re-layouts: 6.06 us -> none  [folded(): return x.reshape(x.shape[:-2] + (x.shape[-2] * size, LANE))]
    pallas_call x2, Pallas kernels: 41.6 us -> 46.2 us  [per_device(): round_call(len(outs), outs)]
  transfers between devices with their start and end apart: 22 -> 19, of which waited for: 4 -> 7; matrix products, arithmetic and copies ran while one was open for 19% -> 2% of each run, Pallas kernels for 17% -> 31%
where the time goes in v3:
time: 164 us; the launch traced here: 162 us
  Pallas kernels  72.2 us (44%)
  waiting for transfers between devices  42.8 us (26%)
  starting transfers between devices  37.1 us (23%)
  local copies, waits for them, and re-layouts  5.1 us (3%)
  other arithmetic  2.76 us (2%)
  between operations  1.8 us (1%)
    pallas_call x2, Pallas kernels, per_device(): round_call(len(outs), outs)  46.2 us
    pallas_call x2, Pallas kernels, per_device(): obs_a, obs_b, const = deposit(place, entries)  24.3 us
    ppermute x1, waiting for transfers between devices, per_device(): other_list = lax.ppermute(own_list, 'tm', swap)  19.6 us
    ppermute x2, waiting for transfers between devices, per_device(): mid_e = lax.ppermute(edge, 'tm', swap)  9.09 us
    ppermute x2, waiting for transfers between devices, per_device(): far_e = lax.ppermute(edge, 'tm', shift)  8.91 us
    ppermute x2, starting transfers between devices, per_device(): far_e = lax.ppermute(edge, 'tm', shift)  6.96 us
    ppermute x2, starting transfers between devices, per_device(): far_m = lax.ppermute(inner, 'tm', shift)  5.44 us
    ppermute x2, starting transfers between devices, per_device(): mid_e = lax.ppermute(edge, 'tm', swap)  5.36 us
  transfers between devices with their start and end apart: 19, of which 7 were waited for; matrix products, arithmetic and copies ran while one was open for 2% of the time, Pallas kernels for 31%

profile of v3, /device:TPU:0, one launch (start us, length us, event | category | flops | bytes accessed | tf_op | source)
XLA Modules:
  0.0 161.8 jit_solution(15984462905676301083)
XLA Ops:
  0.6 1.7 %copy.10 = f32[48,8,8,128]{3,2,1,0:T(8,128)S(1)} copy(f32[48,8,8,128]{3,1,2,0:T(8,128)} %bitcast.27) | data formatting | bytes 3145728
  2.5 1.4 collective-permute-start.2
  4.0 5.3 %collective-permute-start = (f32[3,48,8,128]{3,2,1,0:T(8,128)S(1)}, f32[3,48,8,128]{3,2,1,0:T(8,128)S(1)}, u32[]{:S(2)}, u32[]{:S(2)}) collective-permute-start(f32[3,48,8,128]{3,2,1,0:T(8,128)S(1)} %pad_maximum_fusion.own.own_e), channel_id=1, source_target_pairs={{0,4},{4,0},{8,12},{12,8},{16,20},{20,16},{24,28},{28,24},{1,5},{5... | collective-permute-start | bytes 1769480 | tf_op jit(solution)/shard_map/ppermute | solution.py:589
  10.3 1.3 collective-permute-start.3
  11.6 3.2 %collective-permute-start.1 = (f32[3,80,8,128]{3,2,1,0:T(8,128)}, f32[3,80,8,128]{3,2,1,0:T(8,128)}, u32[]{:S(2)}, u32[]{:S(2)}) collective-permute-start(f32[3,80,8,128]{3,2,1,0:T(8,128)} %slice.14.own_m), channel_id=1, source_target_pairs={{0,4},{4,0},{8,12},{12,8},{16,20},{20,16},{24,28},{28,24},{1,5},{5... | collective-permute-start | bytes 2949128 | tf_op jit(solution)/shard_map/ppermute | solution.py:591
  15.5 1.6 fixed.1
  17.1 6.3 %collective-permute-done.mid.mid_e = f32[3,48,8,128]{3,2,1,0:T(8,128)S(1)} collective-permute-done((f32[3,48,8,128]{3,2,1,0:T(8,128)S(1)}, f32[3,48,8,128]{3,2,1,0:T(8,128)S(1)}, u32[]{:S(2)}, u32[]{:S(2)}) %collective-permute-start) | collective-permute-done | bytes 589856 | tf_op jit(solution)/shard_map/ppermute | solution.py:589
  23.4 1.3 collective-permute-start.8
  24.9 19.6 %collective-permute-done.4.entries = f32[3,32,128]{2,1,0:T(8,128)S(1)} collective-permute-done((f32[3,32,128]{2,1,0:T(8,128)S(1)}, f32[3,32,128]{2,1,0:T(8,128)S(1)}, u32[]{:S(2)}, u32[]{:S(2)}) %collective-permute-start.4) | collective-permute-done | bytes 49184 | tf_op jit(solution)/shard_map/ppermute | solution.py:488
  44.4 1.3 collective-permute-start.5
  45.8 1.3 collective-permute-start.6
  47.1 4.7 %collective-permute-start.7 = (f32[72,1024]{1,0:T(8,128)}, f32[72,1024]{1,0:T(8,128)S(1)}, u32[]{:S(2)}, u32[]{:S(2)}) collective-permute-start(f32[72,1024]{1,0:T(8,128)} %get-tuple-element.26), channel_id=1, source_target_pairs={{0,1},{1,2},{2,3},{4,5},{5,6},{6,7},{8,9},{9,10},{10,11},{12,13},{... | collective-permute-start | bytes 884744 | tf_op jit(solution)/shard_map/ppermute | solution.py:552
  52.6 12.9 %shard_map.95 = (f32[3,128,8,128]{3,2,1,0:T(8,128)}, f32[3,128,8,128]{3,2,1,0:T(8,128)}, f32[8,128]{1,0:T(8,128)}) custom-call(s32[1]{0:T(128)} %bitcast.12.place, f32[3,32,128]{2,1,0:T(8,128)} %copy-done.20), custom_call_target="tpu_custom_call" | custom-call | flops 20000000 | tf_op jit(solution)/shard_map/pallas_call | solution.py:598
  66.7 22.4 %shard_map.96 = (f32[3,48,8,128]{3,2,1,0:T(8,128)}, f32[3,80,8,128]{3,2,1,0:T(8,128)}, f32[8,128]{1,0:T(8,128)}) custom-call(s32[1]{0:T(128)} %bitcast.5.own_lo, f32[4]{0:T(128)} %add_convert_fusion.1.flags, f32[3,48,8,128]{3,2,1,0:T(8,128)} %copy-done.1, f32[3,80,8,128]{3,2,1,0:T(8,128)} %slice.14.own_m, f32[3,48,8,128]{3,2,1,0:T(8,128)} %copy-done.4, ...), custom_call_target="tpu_custom_call" | custom-call | flops 45000000 | tf_op jit(solution)/shard_map/pallas_call | solution.py:609
  89.1 5.5 %collective-permute-start.11 = (f32[3,48,8,128]{3,2,1,0:T(8,128)}, f32[3,48,8,128]{3,2,1,0:T(8,128)S(1)}, u32[]{:S(2)}, u32[]{:S(2)}) collective-permute-start(f32[3,48,8,128]{3,2,1,0:T(8,128)} %get-tuple-element.35.own.own_e), channel_id=1, source_target_pairs={{0,8},{8,16},{16,24},{12,4},{20,12},{28,20},{1,9},{9,17},{17,25},{... | collective-permute-start | bytes 1769480 | tf_op jit(solution)/shard_map/ppermute | solution.py:590
  94.8 4.2 %collective-permute-start.12 = (f32[3,80,8,128]{3,2,1,0:T(8,128)}, f32[3,80,8,128]{3,2,1,0:T(8,128)S(1)}, u32[]{:S(2)}, u32[]{:S(2)}) collective-permute-start(f32[3,80,8,128]{3,2,1,0:T(8,128)} %get-tuple-element.36.own_m), channel_id=1, source_target_pairs={{0,8},{8,16},{16,24},{12,4},{20,12},{28,20},{1,9},{9,17},{17,25},{... | collective-permute-start | bytes 2949128 | tf_op jit(solution)/shard_map/ppermute | solution.py:592
  99.0 8.9 %collective-permute-done.11.far.far_e = f32[3,48,8,128]{3,2,1,0:T(8,128)S(1)} collective-permute-done((f32[3,48,8,128]{3,2,1,0:T(8,128)}, f32[3,48,8,128]{3,2,1,0:T(8,128)S(1)}, u32[]{:S(2)}, u32[]{:S(2)}) %collective-permute-start.11) | collective-permute-done | bytes 589856 | tf_op jit(solution)/shard_map/ppermute | solution.py:590
  107.9 2.8 %collective-permute-done.9.mid.mid_e = f32[3,48,8,128]{3,2,1,0:T(8,128)S(1)} collective-permute-done((f32[3,48,8,128]{3,2,1,0:T(8,128)}, f32[3,48,8,128]{3,2,1,0:T(8,128)S(1)}, u32[]{:S(2)}, u32[]{:S(2)}) %collective-permute-start.9) | collective-permute-done | bytes 589856 | tf_op jit(solution)/shard_map/ppermute | solution.py:589
  111.8 3.9 %collective-permute-start.13 = (f32[3,48,8,128]{3,2,1,0:T(8,128)S(1)}, f32[3,48,8,128]{3,2,1,0:T(8,128)}, u32[]{:S(2)}, u32[]{:S(2)}) collective-permute-start(f32[3,48,8,128]{3,2,1,0:T(8,128)S(1)} %get-tuple-element.38), channel_id=1, source_target_pairs={{0,1},{1,2},{2,3},{4,5},{5,6},{6,7},{8,9},{9,10},{10,11},{12,13},{... | collective-permute-start | bytes 1769480 | tf_op jit(solution)/shard_map/ppermute | solution.py:599
  115.8 1.3 collective-permute-start.14
  118.3 11.4 %shard_map.97 = (f32[3,128,8,128]{3,2,1,0:T(8,128)}, f32[3,128,8,128]{3,2,1,0:T(8,128)}, f32[8,128]{1,0:T(8,128)}) custom-call(s32[1]{0:T(128)} %bitcast.12.place, f32[3,32,128]{2,1,0:T(8,128)} %copy-done.13), custom_call_target="tpu_custom_call" | custom-call | flops 20000000 | tf_op jit(solution)/shard_map/pallas_call | solution.py:598
  129.7 2.2 %collective-permute-done.10.mid_m = f32[3,80,8,128]{3,2,1,0:T(8,128)} collective-permute-done((f32[3,80,8,128]{3,2,1,0:T(8,128)}, f32[3,80,8,128]{3,2,1,0:T(8,128)}, u32[]{:S(2)}, u32[]{:S(2)}) %collective-permute-start.10) | collective-permute-done | bytes 983072 | tf_op jit(solution)/shard_map/ppermute | solution.py:591
  131.9 23.8 %shard_map.98 = (f32[3,128,1024]{2,1,0:T(8,128)}, f32[8,128]{1,0:T(8,128)}) custom-call(s32[1]{0:T(128)} %bitcast.own_lo, f32[4]{0:T(128)} %add_convert_fusion.flags, f32[3,48,8,128]{3,2,1,0:T(8,128)} %get-tuple-element.35.own.own_e, f32[3,80,8,128]{3,2,1,0:T(8,128)} %get-tuple-element.36.own_m, f32[3,48,8,128]{3,2,1,0:T(8,128)} %copy-done.7, ...), custom_call_target="tpu_custom_call" | custom-call | flops 45000000 | tf_op jit(solution)/shard_map/pallas_call | solution.py:609
  158.1 2.0 %collective-permute-done.17 = f32[2,8,128]{2,1,0:T(8,128)S(1)} collective-permute-done((f32[2,8,128]{2,1,0:T(8,128)S(1)}, f32[2,8,128]{2,1,0:T(8,128)S(1)}, u32[]{:S(2)}, u32[]{:S(2)}) %collective-permute-start.17) | collective-permute-done | bytes 8224 | tf_op jit(solution)/shard_map/ppermute | solution.py:582
  (78 shorter events, 9.9 us)
Async XLA Ops:
  2.5 22.2 %copy-start.1 = (f32[3,48,8,128]{3,2,1,0:T(8,128)}, f32[3,48,8,128]{3,2,1,0:T(8,128)S(1)}, u32[]{:S(2)}) copy-start(f32[3,48,8,128]{3,2,1,0:T(8,128)S(1)} %pad_maximum_fusion.own.own_e) | copy-start | bytes 1769476
  2.5 22.2 %collective-permute-start.2 = (f32[3,48,8,128]{3,2,1,0:T(8,128)S(1)}, f32[3,48,8,128]{3,2,1,0:T(8,128)S(1)}, u32[]{:S(2)}, u32[]{:S(2)}) collective-permute-start(f32[3,48,8,128]{3,2,1,0:T(8,128)S(1)} %pad_maximum_fusion.own.own_e), channel_id=1, source_target_pairs={{8,0},{16,8},{24,16},{4,12},{12,20},{20,28},{9,1},{17,9},{25,17},{... | collective-permute-start | bytes 1769480 | tf_op jit(solution)/shard_map/ppermute | solution.py:590
  4.0 19.5 %collective-permute-start = (f32[3,48,8,128]{3,2,1,0:T(8,128)S(1)}, f32[3,48,8,128]{3,2,1,0:T(8,128)S(1)}, u32[]{:S(2)}, u32[]{:S(2)}) collective-permute-start(f32[3,48,8,128]{3,2,1,0:T(8,128)S(1)} %pad_maximum_fusion.own.own_e), channel_id=1, source_target_pairs={{0,4},{4,0},{8,12},{12,8},{16,20},{20,16},{24,28},{28,24},{1,5},{5... | collective-permute-start | bytes 1769480 | tf_op jit(solution)/shard_map/ppermute | solution.py:589
  10.3 55.2 %collective-permute-start.3 = (f32[3,80,8,128]{3,2,1,0:T(8,128)}, f32[3,80,8,128]{3,2,1,0:T(8,128)}, u32[]{:S(2)}, u32[]{:S(2)}) collective-permute-start(f32[3,80,8,128]{3,2,1,0:T(8,128)} %slice.14.own_m), channel_id=1, source_target_pairs={{8,0},{16,8},{24,16},{4,12},{12,20},{20,28},{9,1},{17,9},{25,17},{... | collective-permute-start | bytes 2949128 | tf_op jit(solution)/shard_map/ppermute | solution.py:592
  11.6 53.9 %collective-permute-start.1 = (f32[3,80,8,128]{3,2,1,0:T(8,128)}, f32[3,80,8,128]{3,2,1,0:T(8,128)}, u32[]{:S(2)}, u32[]{:S(2)}) collective-permute-start(f32[3,80,8,128]{3,2,1,0:T(8,128)} %slice.14.own_m), channel_id=1, source_target_pairs={{0,4},{4,0},{8,12},{12,8},{16,20},{20,16},{24,28},{28,24},{1,5},{5... | collective-permute-start | bytes 2949128 | tf_op jit(solution)/shard_map/ppermute | solution.py:591
  15.4 29.0 %collective-permute-start.4 = (f32[3,32,128]{2,1,0:T(8,128)S(1)}, f32[3,32,128]{2,1,0:T(8,128)S(1)}, u32[]{:S(2)}, u32[]{:S(2)}) collective-permute-start(f32[3,32,128]{2,1,0:T(8,128)S(1)} %pad_maximum_fusion.1.entries), channel_id=1, source_target_pairs={{0,4},{4,0},{8,12},{12,8},{16,20},{20,16},{24,28},{28,24},{1,5},{5... | collective-permute-start | bytes 147464 | tf_op jit(solution)/shard_map/ppermute | solution.py:488
  23.4 23.6 %collective-permute-start.8 = (f32[72,1024]{1,0:T(8,128)S(1)}, f32[72,1024]{1,0:T(8,128)S(1)}, u32[]{:S(2)}, u32[]{:S(2)}) collective-permute-start(f32[72,1024]{1,0:T(8,128)S(1)} %get-tuple-element.31), channel_id=1, source_target_pairs={{1,0},{2,1},{3,2},{5,4},{6,5},{7,6},{9,8},{10,9},{11,10},{13,12},{... | collective-permute-start | bytes 884744 | tf_op jit(solution)/shard_map/ppermute | solution.py:553
  24.7 41.7 %copy-start.3 = (f32[3,48,8,128]{3,2,1,0:T(8,128)}, f32[3,48,8,128]{3,2,1,0:T(8,128)S(1)}, u32[]{:S(2)}) copy-start(f32[3,48,8,128]{3,2,1,0:T(8,128)S(1)} %collective-permute-done.2.far.far_e) | copy-start | bytes 1769476
  44.4 21.1 %collective-permute-start.5 = (f32[3,48,8,128]{3,2,1,0:T(8,128)S(1)}, f32[3,48,8,128]{3,2,1,0:T(8,128)S(1)}, u32[]{:S(2)}, u32[]{:S(2)}) collective-permute-start(f32[3,48,8,128]{3,2,1,0:T(8,128)S(1)} %get-tuple-element.29), channel_id=1, source_target_pairs={{0,1},{1,2},{2,3},{4,5},{5,6},{6,7},{8,9},{9,10},{10,11},{12,13},{... | collective-permute-start | bytes 1769480 | tf_op jit(solution)/shard_map/ppermute | solution.py:599
  45.8 19.8 %collective-permute-start.6 = (f32[3,48,8,128]{3,2,1,0:T(8,128)S(1)}, f32[3,48,8,128]{3,2,1,0:T(8,128)S(1)}, u32[]{:S(2)}, u32[]{:S(2)}) collective-permute-start(f32[3,48,8,128]{3,2,1,0:T(8,128)S(1)} %get-tuple-element.30), channel_id=1, source_target_pairs={{1,0},{2,1},{3,2},{5,4},{6,5},{7,6},{9,8},{10,9},{11,10},{13,12},{... | collective-permute-start | bytes 1769480 | tf_op jit(solution)/shard_map/ppermute | solution.py:600
  47.1 18.4 %collective-permute-start.7 = (f32[72,1024]{1,0:T(8,128)}, f32[72,1024]{1,0:T(8,128)S(1)}, u32[]{:S(2)}, u32[]{:S(2)}) collective-permute-start(f32[72,1024]{1,0:T(8,128)} %get-tuple-element.26), channel_id=1, source_target_pairs={{0,1},{1,2},{2,3},{4,5},{5,6},{6,7},{8,9},{9,10},{10,11},{12,13},{... | collective-permute-start | bytes 884744 | tf_op jit(solution)/shard_map/ppermute | solution.py:552
  66.7 51.0 %copy-start.17 = (f32[8,128]{1,0:T(8,128)S(1)}, f32[8,128]{1,0:T(8,128)}, u32[]{:S(2)}) copy-start(f32[8,128]{1,0:T(8,128)} %get-tuple-element.45) | copy-start | bytes 12292
  89.1 18.8 %collective-permute-start.11 = (f32[3,48,8,128]{3,2,1,0:T(8,128)}, f32[3,48,8,128]{3,2,1,0:T(8,128)S(1)}, u32[]{:S(2)}, u32[]{:S(2)}) collective-permute-start(f32[3,48,8,128]{3,2,1,0:T(8,128)} %get-tuple-element.35.own.own_e), channel_id=1, source_target_pairs={{0,8},{8,16},{16,24},{12,4},{20,12},{28,20},{1,9},{9,17},{17,25},{... | collective-permute-start | bytes 1769480 | tf_op jit(solution)/shard_map/ppermute | solution.py:590
  94.7 16.0 %collective-permute-start.9 = (f32[3,48,8,128]{3,2,1,0:T(8,128)}, f32[3,48,8,128]{3,2,1,0:T(8,128)S(1)}, u32[]{:S(2)}, u32[]{:S(2)}) collective-permute-start(f32[3,48,8,128]{3,2,1,0:T(8,128)} %get-tuple-element.35.own.own_e), channel_id=1, source_target_pairs={{0,4},{4,0},{8,12},{12,8},{16,20},{20,16},{24,28},{28,24},{1,5},{5... | collective-permute-start | bytes 1769480 | tf_op jit(solution)/shard_map/ppermute | solution.py:589
  94.8 34.9 %collective-permute-start.12 = (f32[3,80,8,128]{3,2,1,0:T(8,128)}, f32[3,80,8,128]{3,2,1,0:T(8,128)S(1)}, u32[]{:S(2)}, u32[]{:S(2)}) collective-permute-start(f32[3,80,8,128]{3,2,1,0:T(8,128)} %get-tuple-element.36.own_m), channel_id=1, source_target_pairs={{0,8},{8,16},{16,24},{12,4},{20,12},{28,20},{1,9},{9,17},{17,25},{... | collective-permute-start | bytes 2949128 | tf_op jit(solution)/shard_map/ppermute | solution.py:592
  98.9 32.9 %collective-permute-start.10 = (f32[3,80,8,128]{3,2,1,0:T(8,128)}, f32[3,80,8,128]{3,2,1,0:T(8,128)}, u32[]{:S(2)}, u32[]{:S(2)}) collective-permute-start(f32[3,80,8,128]{3,2,1,0:T(8,128)} %get-tuple-element.36.own_m), channel_id=1, source_target_pairs={{0,4},{4,0},{8,12},{12,8},{16,20},{20,16},{24,28},{28,24},{1,5},{5... | collective-permute-start | bytes 2949128 | tf_op jit(solution)/shard_map/ppermute | solution.py:591
  107.9 24.0 %copy-start.6 = (f32[3,48,8,128]{3,2,1,0:T(8,128)}, f32[3,48,8,128]{3,2,1,0:T(8,128)S(1)}, u32[]{:S(2)}) copy-start(f32[3,48,8,128]{3,2,1,0:T(8,128)S(1)} %collective-permute-done.11.far.far_e) | copy-start | bytes 1769476
  111.8 20.0 %collective-permute-start.13 = (f32[3,48,8,128]{3,2,1,0:T(8,128)S(1)}, f32[3,48,8,128]{3,2,1,0:T(8,128)}, u32[]{:S(2)}, u32[]{:S(2)}) collective-permute-start(f32[3,48,8,128]{3,2,1,0:T(8,128)S(1)} %get-tuple-element.38), channel_id=1, source_target_pairs={{0,1},{1,2},{2,3},{4,5},{5,6},{6,7},{8,9},{9,10},{10,11},{12,13},{... | collective-permute-start | bytes 1769480 | tf_op jit(solution)/shard_map/ppermute | solution.py:599
  115.8 16.1 %collective-permute-start.14 = (f32[3,48,8,128]{3,2,1,0:T(8,128)S(1)}, f32[3,48,8,128]{3,2,1,0:T(8,128)}, u32[]{:S(2)}, u32[]{:S(2)}) collective-permute-start(f32[3,48,8,128]{3,2,1,0:T(8,128)S(1)} %get-tuple-element.39), channel_id=1, source_target_pairs={{1,0},{2,1},{3,2},{5,4},{6,5},{7,6},{9,8},{10,9},{11,10},{13,12},{... | collective-permute-start | bytes 1769480 | tf_op jit(solution)/shard_map/ppermute | solution.py:600
  117.8 37.9 %collective-permute-start.15 = (f32[8,128]{1,0:T(8,128)S(1)}, f32[8,128]{1,0:T(8,128)S(1)}, u32[]{:S(2)}, u32[]{:S(2)}) collective-permute-start(f32[8,128]{1,0:T(8,128)S(1)} %add.50), channel_id=1, source_target_pairs={{0,4},{4,0},{8,12},{12,8},{16,20},{20,16},{24,28},{28,24},{1,5},{5... | collective-permute-start | bytes 12296 | tf_op jit(solution)/shard_map/ppermute | solution.py:631
  131.9 23.8 %copy-start.19 = (f32[8,128]{1,0:T(8,128)S(1)}, f32[8,128]{1,0:T(8,128)}, u32[]{:S(2)}) copy-start(f32[8,128]{1,0:T(8,128)} %get-tuple-element.49) | copy-start | bytes 12292
  156.4 3.7 %collective-permute-start.17 = (f32[2,8,128]{2,1,0:T(8,128)S(1)}, f32[2,8,128]{2,1,0:T(8,128)S(1)}, u32[]{:S(2)}, u32[]{:S(2)}) collective-permute-start(f32[2,8,128]{2,1,0:T(8,128)S(1)} %pad_maximum_fusion.2), channel_id=1, source_target_pairs={{0,2},{1,3},{2,0},{3,1},{4,6},{5,7},{6,4},{7,5},{8,10},{9,11},{10,... | collective-permute-start | bytes 24584 | tf_op jit(solution)/shard_map/ppermute | solution.py:582
  157.2 2.8 %collective-permute-start.18 = (f32[2,8,128]{2,1,0:T(8,128)S(1)}, f32[2,8,128]{2,1,0:T(8,128)S(1)}, u32[]{:S(2)}, u32[]{:S(2)}) collective-permute-start(f32[2,8,128]{2,1,0:T(8,128)S(1)} %pad_maximum_fusion.2), channel_id=1, source_target_pairs={{0,3},{1,0},{2,1},{3,2},{4,7},{5,4},{6,5},{7,6},{8,11},{9,8},{10,9... | collective-permute-start | bytes 24584 | tf_op jit(solution)/shard_map/ppermute | solution.py:582
  158.1 3.1 %collective-permute-start.16 = (f32[2,8,128]{2,1,0:T(8,128)S(1)}, f32[2,8,128]{2,1,0:T(8,128)S(1)}, u32[]{:S(2)}, u32[]{:S(2)}) collective-permute-start(f32[2,8,128]{2,1,0:T(8,128)S(1)} %pad_maximum_fusion.2), channel_id=1, source_target_pairs={{0,1},{1,2},{2,3},{3,0},{4,5},{5,6},{6,7},{7,4},{8,9},{9,10},{10,1... | collective-permute-start | bytes 24584 | tf_op jit(solution)/shard_map/ppermute | solution.py:582
  (16 other events, 130.4 us)

commit v4 on v3

--- a/solution.py
+++ b/solution.py
@@ -390,8 +390,8 @@
         (pulled * entries[1]).reshape(count // SUB, SUB, lanes), axis=0
     )
     copies = [
-        pltpu.make_async_copy(words_v, words, sems.at[0]),
-        pltpu.make_async_copy(values_v, values, sems.at[1]),
+        pltpu.make_async_copy(words_v, words.at[:, pl.ds(0, count)], sems.at[0]),
+        pltpu.make_async_copy(values_v, values.at[:, pl.ds(0, count)], sems.at[1]),
     ]
     for c in copies:
         c.start()
@@ -417,14 +417,18 @@
     live = words[0, count - 1, lanes - 1]
     live = live + (words[1, count - 1, lanes - 1] < (spare << shift)).astype(jnp.int32)
     step = GROUPS * DEALS
+    words[1, count, 0] = spare << shift
+    values[0, count, 0] = 0.0
+    values[1, count, 0] = 0.0
+    for k in range(step):
+        picked[live + k] = count * lanes
 
     def body(n, carry):
         for k in range(DEALS):
             for g in range(GROUPS):
-                at = n * step + (k * GROUPS + g)
-                i = jnp.where(at < live, picked[at], 0)
+                i = picked[n * step + (k * GROUPS + g)]
                 r, c = i >> (lanes.bit_length() - 1), i & (lanes - 1)
-                word = jnp.where(at < live, words[1, r, c], spare << shift)
+                word = words[1, r, c]
                 hit = column == (word & (lon - 1))
                 to = word >> shift
                 a_acc[g][to] = a_acc[g][to] + jnp.where(hit, values[0, r, c], 0.0)
@@ -512,11 +516,11 @@
         [field(comps, rows), field(comps, rows), tile],
         [
             pltpu.VMEM((2,) + list_shape, jnp.int32),
-            pltpu.SMEM((2,) + list_shape, jnp.int32),
+            pltpu.SMEM((2, list_shape[0] + SUB, LANE), jnp.int32),
             pltpu.SMEM((number + GROUPS * DEALS,), jnp.int32),
             pltpu.SemaphoreType.DMA((2 + 2 * comps,)),
             pltpu.VMEM((2,) + list_shape, f32),
-            pltpu.SMEM((2,) + list_shape, f32),
+            pltpu.SMEM((2, list_shape[0] + SUB, LANE), f32),
         ]
         + [held(comps * rows + 1)] * (2 * GROUPS),
         20_000_000,
@@ -592,10 +596,14 @@
         far_m = lax.ppermute(inner, "tm", shift)
         if away:
             _, mid_e = lax.optimization_barrier((to_south, mid_e))
-        to_south, to_north = pack(edge, mid_e, far_e)
-        entries = other_list if away else own_list
-        to_south, entries = lax.optimization_barrier((to_south, entries))
-        obs_a, obs_b, const = deposit(place, entries)
+            to_south, to_north = pack(edge, mid_e, far_e)
+            to_south, other_list = lax.optimization_barrier((to_south, other_list))
+            obs_a, obs_b, const = deposit(place, other_list)
+        else:
+            _, own_list = lax.optimization_barrier((edge, own_list))
+            obs_a, obs_b, const = deposit(place, own_list)
+            const, mid_e = lax.optimization_barrier((const, mid_e))
+            to_south, to_north = pack(edge, mid_e, far_e)
         from_north = lax.ppermute(to_south, "space", southward)
         from_south = lax.ppermute(to_north, "space", northward)
         own_lo = (even if away else ~even).astype(jnp.int32).reshape(1)

time: 164 us -> 162 us (0.988); the launches traced: 162 us -> 162 us
  waiting for transfers between devices: 42.8 us -> 40.4 us
  starting transfers between devices: 37.1 us -> 39.3 us
    ppermute x2, waiting for transfers between devices: 0.01 us -> 11.1 us  [per_device(): far_m = lax.ppermute(inner, 'tm', shift)]
    ppermute x2, waiting for transfers between devices: 8.91 us -> 0.3 us  [per_device(): far_e = lax.ppermute(edge, 'tm', shift)]
    ppermute x2, waiting for transfers between devices: 9.09 us -> 6.32 us  [per_device(): mid_e = lax.ppermute(edge, 'tm', swap)]
    ppermute x1, starting transfers between devices: 0.56 us -> 2.84 us  [per_device(): early = lax.ppermute(cost + const, 'tm', swap)]
    ppermute x2, waiting for transfers between devices: 2.15 us -> 0.01 us  [per_device(): mid_m = lax.ppermute(inner, 'tm', swap)]
    ppermute x2, starting transfers between devices: 5.44 us -> 3.4 us  [per_device(): far_m = lax.ppermute(inner, 'tm', shift)]
    ppermute x2, starting transfers between devices: 5.36 us -> 7.37 us  [per_device(): mid_e = lax.ppermute(edge, 'tm', swap)]
  transfers between devices with their start and end apart: 19 -> 19, of which waited for: 7 -> 6; matrix products, arithmetic and copies ran while one was open for 2% -> 1% of each run, Pallas kernels for 31% -> 30%
where the time goes in v4:
time: 162 us
  Pallas kernels  71.5 us (44%)
  waiting for transfers between devices  40.4 us (25%)
  starting transfers between devices  39.3 us (24%)
  local copies, waits for them, and re-layouts  6.04 us (4%)
  other arithmetic  2.59 us (2%)
  between operations  1.8 us (1%)
    pallas_call x2, Pallas kernels, per_device(): round_call(len(outs), outs)  46.2 us
    ppermute x1, waiting for transfers between devices, per_device(): other_list = lax.ppermute(own_list, 'tm', swap)  19.6 us
    pallas_call x1, Pallas kernels, per_device(): obs_a, obs_b, const = deposit(place, other_list)  12.5 us
    pallas_call x1, Pallas kernels, per_device(): obs_a, obs_b, const = deposit(place, own_list)  11.1 us
    ppermute x2, waiting for transfers between devices, per_device(): far_m = lax.ppermute(inner, 'tm', shift)  11.1 us
    ppermute x2, starting transfers between devices, per_device(): mid_e = lax.ppermute(edge, 'tm', swap)  7.37 us
    ppermute x2, starting transfers between devices, per_device(): far_e = lax.ppermute(edge, 'tm', shift)  6.63 us
    ppermute x2, waiting for transfers between devices, per_device(): mid_e = lax.ppermute(edge, 'tm', swap)  6.32 us
  transfers between devices with their start and end apart: 19, of which 6 were waited for; matrix products, arithmetic and copies ran while one was open for 1% of the time, Pallas kernels for 30%

profile of v4, /device:TPU:0, one launch (start us, length us, event | category | flops | bytes accessed | tf_op | source)
XLA Modules:
  0.0 161.6 jit_solution(17539794782673149105)
XLA Ops:
  0.6 1.7 %copy.10 = f32[48,8,8,128]{3,2,1,0:T(8,128)S(1)} copy(f32[48,8,8,128]{3,1,2,0:T(8,128)} %bitcast.27) | data formatting | bytes 3145728
  2.5 1.4 collective-permute-start.2
  4.0 5.3 %collective-permute-start = (f32[3,48,8,128]{3,2,1,0:T(8,128)S(1)}, f32[3,48,8,128]{3,2,1,0:T(8,128)S(1)}, u32[]{:S(2)}, u32[]{:S(2)}) collective-permute-start(f32[3,48,8,128]{3,2,1,0:T(8,128)S(1)} %pad_maximum_fusion.own.own_e), channel_id=1, source_target_pairs={{0,4},{4,0},{8,12},{12,8},{16,20},{20,16},{24,28},{28,24},{1,5},{5... | collective-permute-start | bytes 1769480 | tf_op jit(solution)/shard_map/ppermute | solution.py:593
  10.3 1.3 collective-permute-start.3
  11.6 3.2 %collective-permute-start.1 = (f32[3,80,8,128]{3,2,1,0:T(8,128)}, f32[3,80,8,128]{3,2,1,0:T(8,128)}, u32[]{:S(2)}, u32[]{:S(2)}) collective-permute-start(f32[3,80,8,128]{3,2,1,0:T(8,128)} %slice.14.own_m), channel_id=1, source_target_pairs={{0,4},{4,0},{8,12},{12,8},{16,20},{20,16},{24,28},{28,24},{1,5},{5... | collective-permute-start | bytes 2949128 | tf_op jit(solution)/shard_map/ppermute | solution.py:595
  15.5 1.6 fixed.1
  17.1 6.3 %collective-permute-done.mid.mid_e = f32[3,48,8,128]{3,2,1,0:T(8,128)S(1)} collective-permute-done((f32[3,48,8,128]{3,2,1,0:T(8,128)S(1)}, f32[3,48,8,128]{3,2,1,0:T(8,128)S(1)}, u32[]{:S(2)}, u32[]{:S(2)}) %collective-permute-start) | collective-permute-done | bytes 589856 | tf_op jit(solution)/shard_map/ppermute | solution.py:593
  23.4 1.3 collective-permute-start.8
  24.9 19.6 %collective-permute-done.4.entries = f32[3,32,128]{2,1,0:T(8,128)S(1)} collective-permute-done((f32[3,32,128]{2,1,0:T(8,128)S(1)}, f32[3,32,128]{2,1,0:T(8,128)S(1)}, u32[]{:S(2)}, u32[]{:S(2)}) %collective-permute-start.4) | collective-permute-done | bytes 49184 | tf_op jit(solution)/shard_map/ppermute | solution.py:492
  44.4 1.3 collective-permute-start.5
  45.8 1.3 collective-permute-start.6
  47.1 4.7 %collective-permute-start.7 = (f32[72,1024]{1,0:T(8,128)}, f32[72,1024]{1,0:T(8,128)S(1)}, u32[]{:S(2)}, u32[]{:S(2)}) collective-permute-start(f32[72,1024]{1,0:T(8,128)} %get-tuple-element.27), channel_id=1, source_target_pairs={{0,1},{1,2},{2,3},{4,5},{5,6},{6,7},{8,9},{9,10},{10,11},{12,13},{... | collective-permute-start | bytes 884744 | tf_op jit(solution)/shard_map/ppermute | solution.py:556
  52.5 12.5 %shard_map.95 = (f32[3,128,8,128]{3,2,1,0:T(8,128)}, f32[3,128,8,128]{3,2,1,0:T(8,128)}, f32[8,128]{1,0:T(8,128)}) custom-call(s32[1]{0:T(128)} %bitcast.12.place, f32[3,32,128]{2,1,0:T(8,128)} %copy-done.20), custom_call_target="tpu_custom_call" | custom-call | flops 20000000 | tf_op jit(solution)/shard_map/pallas_call | solution.py:601
  66.2 22.3 %shard_map.96 = (f32[3,48,8,128]{3,2,1,0:T(8,128)}, f32[3,80,8,128]{3,2,1,0:T(8,128)}, f32[8,128]{1,0:T(8,128)}) custom-call(s32[1]{0:T(128)} %bitcast.5.own_lo, f32[4]{0:T(128)} %add_convert_fusion.1.flags, f32[3,48,8,128]{3,2,1,0:T(8,128)} %copy-done.1, f32[3,80,8,128]{3,2,1,0:T(8,128)} %slice.14.own_m, f32[3,48,8,128]{3,2,1,0:T(8,128)} %copy-done.4, ...), custom_call_target="tpu_custom_call" | custom-call | flops 45000000 | tf_op jit(solution)/shard_map/pallas_call | solution.py:617
  88.5 2.1 %collective-permute-start.9 = (f32[3,48,8,128]{3,2,1,0:T(8,128)}, f32[3,48,8,128]{3,2,1,0:T(8,128)S(1)}, u32[]{:S(2)}, u32[]{:S(2)}) collective-permute-start(f32[3,48,8,128]{3,2,1,0:T(8,128)} %get-tuple-element.36.own.own_e), channel_id=1, source_target_pairs={{0,4},{4,0},{8,12},{12,8},{16,20},{20,16},{24,28},{28,24},{1,5},{5... | collective-permute-start | bytes 1769480 | tf_op jit(solution)/shard_map/ppermute | solution.py:593
  90.6 5.2 %collective-permute-start.11 = (f32[3,48,8,128]{3,2,1,0:T(8,128)}, f32[3,48,8,128]{3,2,1,0:T(8,128)S(1)}, u32[]{:S(2)}, u32[]{:S(2)}) collective-permute-start(f32[3,48,8,128]{3,2,1,0:T(8,128)} %get-tuple-element.36.own.own_e), channel_id=1, source_target_pairs={{0,8},{8,16},{16,24},{12,4},{20,12},{28,20},{1,9},{9,17},{17,25},{... | collective-permute-start | bytes 1769480 | tf_op jit(solution)/shard_map/ppermute | solution.py:594
  95.8 2.1 %collective-permute-start.12 = (f32[3,80,8,128]{3,2,1,0:T(8,128)}, f32[3,80,8,128]{3,2,1,0:T(8,128)S(1)}, u32[]{:S(2)}, u32[]{:S(2)}) collective-permute-start(f32[3,80,8,128]{3,2,1,0:T(8,128)} %get-tuple-element.37.own_m), channel_id=1, source_target_pairs={{0,8},{8,16},{16,24},{12,4},{20,12},{28,20},{1,9},{9,17},{17,25},{... | collective-permute-start | bytes 2949128 | tf_op jit(solution)/shard_map/ppermute | solution.py:596
  98.1 11.1 %shard_map.97 = (f32[3,128,8,128]{3,2,1,0:T(8,128)}, f32[3,128,8,128]{3,2,1,0:T(8,128)}, f32[8,128]{1,0:T(8,128)}) custom-call(s32[1]{0:T(128)} %bitcast.12.place, f32[3,32,128]{2,1,0:T(8,128)} %copy-done.13), custom_call_target="tpu_custom_call" | custom-call | flops 20000000 | tf_op jit(solution)/shard_map/pallas_call | solution.py:604
  110.7 4.1 %collective-permute-start.13 = (f32[3,48,8,128]{3,2,1,0:T(8,128)S(1)}, f32[3,48,8,128]{3,2,1,0:T(8,128)}, u32[]{:S(2)}, u32[]{:S(2)}) collective-permute-start(f32[3,48,8,128]{3,2,1,0:T(8,128)S(1)} %get-tuple-element.41), channel_id=1, source_target_pairs={{0,1},{1,2},{2,3},{4,5},{5,6},{6,7},{8,9},{9,10},{10,11},{12,13},{... | collective-permute-start | bytes 1769480 | tf_op jit(solution)/shard_map/ppermute | solution.py:607
  116.7 2.8 %collective-permute-start.15 = (f32[8,128]{1,0:T(8,128)S(1)}, f32[8,128]{1,0:T(8,128)S(1)}, u32[]{:S(2)}, u32[]{:S(2)}) collective-permute-start(f32[8,128]{1,0:T(8,128)S(1)} %add.50), channel_id=1, source_target_pairs={{0,4},{4,0},{8,12},{12,8},{16,20},{20,16},{24,28},{28,24},{1,5},{5... | collective-permute-start | bytes 12296 | tf_op jit(solution)/shard_map/ppermute | solution.py:639
  119.5 11.1 %collective-permute-done.12.far_m = f32[3,80,8,128]{3,2,1,0:T(8,128)S(1)} collective-permute-done((f32[3,80,8,128]{3,2,1,0:T(8,128)}, f32[3,80,8,128]{3,2,1,0:T(8,128)S(1)}, u32[]{:S(2)}, u32[]{:S(2)}) %collective-permute-start.12) | collective-permute-done | bytes 983072 | tf_op jit(solution)/shard_map/ppermute | solution.py:596
  131.6 23.9 %shard_map.98 = (f32[3,128,1024]{2,1,0:T(8,128)}, f32[8,128]{1,0:T(8,128)}) custom-call(s32[1]{0:T(128)} %bitcast.own_lo, f32[4]{0:T(128)} %add_convert_fusion.flags, f32[3,48,8,128]{3,2,1,0:T(8,128)} %get-tuple-element.36.own.own_e, f32[3,80,8,128]{3,2,1,0:T(8,128)} %get-tuple-element.37.own_m, f32[3,48,8,128]{3,2,1,0:T(8,128)} %copy-done.6, ...), custom_call_target="tpu_custom_call" | custom-call | flops 45000000 | tf_op jit(solution)/shard_map/pallas_call | solution.py:617
  156.2 1.8 %collective-permute-start.18 = (f32[2,8,128]{2,1,0:T(8,128)S(1)}, f32[2,8,128]{2,1,0:T(8,128)S(1)}, u32[]{:S(2)}, u32[]{:S(2)}) collective-permute-start(f32[2,8,128]{2,1,0:T(8,128)S(1)} %pad_maximum_fusion.2), channel_id=1, source_target_pairs={{0,3},{1,0},{2,1},{3,2},{4,7},{5,4},{6,5},{7,6},{8,11},{9,8},{10,9... | collective-permute-start | bytes 24584 | tf_op jit(solution)/shard_map/ppermute | solution.py:586
  157.9 1.9 %collective-permute-done.17 = f32[2,8,128]{2,1,0:T(8,128)S(1)} collective-permute-done((f32[2,8,128]{2,1,0:T(8,128)S(1)}, f32[2,8,128]{2,1,0:T(8,128)S(1)}, u32[]{:S(2)}, u32[]{:S(2)}) %collective-permute-start.17) | collective-permute-done | bytes 8224 | tf_op jit(solution)/shard_map/ppermute | solution.py:586
  (78 shorter events, 10.0 us)
Async XLA Ops:
  2.5 22.2 %copy-start.1 = (f32[3,48,8,128]{3,2,1,0:T(8,128)}, f32[3,48,8,128]{3,2,1,0:T(8,128)S(1)}, u32[]{:S(2)}) copy-start(f32[3,48,8,128]{3,2,1,0:T(8,128)S(1)} %pad_maximum_fusion.own.own_e) | copy-start | bytes 1769476
  2.5 22.2 %collective-permute-start.2 = (f32[3,48,8,128]{3,2,1,0:T(8,128)S(1)}, f32[3,48,8,128]{3,2,1,0:T(8,128)S(1)}, u32[]{:S(2)}, u32[]{:S(2)}) collective-permute-start(f32[3,48,8,128]{3,2,1,0:T(8,128)S(1)} %pad_maximum_fusion.own.own_e), channel_id=1, source_target_pairs={{8,0},{16,8},{24,16},{4,12},{12,20},{20,28},{9,1},{17,9},{25,17},{... | collective-permute-start | bytes 1769480 | tf_op jit(solution)/shard_map/ppermute | solution.py:594
  4.0 19.5 %collective-permute-start = (f32[3,48,8,128]{3,2,1,0:T(8,128)S(1)}, f32[3,48,8,128]{3,2,1,0:T(8,128)S(1)}, u32[]{:S(2)}, u32[]{:S(2)}) collective-permute-start(f32[3,48,8,128]{3,2,1,0:T(8,128)S(1)} %pad_maximum_fusion.own.own_e), channel_id=1, source_target_pairs={{0,4},{4,0},{8,12},{12,8},{16,20},{20,16},{24,28},{28,24},{1,5},{5... | collective-permute-start | bytes 1769480 | tf_op jit(solution)/shard_map/ppermute | solution.py:593
  10.3 54.7 %collective-permute-start.3 = (f32[3,80,8,128]{3,2,1,0:T(8,128)}, f32[3,80,8,128]{3,2,1,0:T(8,128)}, u32[]{:S(2)}, u32[]{:S(2)}) collective-permute-start(f32[3,80,8,128]{3,2,1,0:T(8,128)} %slice.14.own_m), channel_id=1, source_target_pairs={{8,0},{16,8},{24,16},{4,12},{12,20},{20,28},{9,1},{17,9},{25,17},{... | collective-permute-start | bytes 2949128 | tf_op jit(solution)/shard_map/ppermute | solution.py:596
  11.6 53.5 %collective-permute-start.1 = (f32[3,80,8,128]{3,2,1,0:T(8,128)}, f32[3,80,8,128]{3,2,1,0:T(8,128)}, u32[]{:S(2)}, u32[]{:S(2)}) collective-permute-start(f32[3,80,8,128]{3,2,1,0:T(8,128)} %slice.14.own_m), channel_id=1, source_target_pairs={{0,4},{4,0},{8,12},{12,8},{16,20},{20,16},{24,28},{28,24},{1,5},{5... | collective-permute-start | bytes 2949128 | tf_op jit(solution)/shard_map/ppermute | solution.py:595
  15.4 29.0 %collective-permute-start.4 = (f32[3,32,128]{2,1,0:T(8,128)S(1)}, f32[3,32,128]{2,1,0:T(8,128)S(1)}, u32[]{:S(2)}, u32[]{:S(2)}) collective-permute-start(f32[3,32,128]{2,1,0:T(8,128)S(1)} %pad_maximum_fusion.1.entries), channel_id=1, source_target_pairs={{0,4},{4,0},{8,12},{12,8},{16,20},{20,16},{24,28},{28,24},{1,5},{5... | collective-permute-start | bytes 147464 | tf_op jit(solution)/shard_map/ppermute | solution.py:492
  23.4 23.6 %collective-permute-start.8 = (f32[72,1024]{1,0:T(8,128)S(1)}, f32[72,1024]{1,0:T(8,128)S(1)}, u32[]{:S(2)}, u32[]{:S(2)}) collective-permute-start(f32[72,1024]{1,0:T(8,128)S(1)} %get-tuple-element.32), channel_id=1, source_target_pairs={{1,0},{2,1},{3,2},{5,4},{6,5},{7,6},{9,8},{10,9},{11,10},{13,12},{... | collective-permute-start | bytes 884744 | tf_op jit(solution)/shard_map/ppermute | solution.py:557
  24.7 41.2 %copy-start.3 = (f32[3,48,8,128]{3,2,1,0:T(8,128)}, f32[3,48,8,128]{3,2,1,0:T(8,128)S(1)}, u32[]{:S(2)}) copy-start(f32[3,48,8,128]{3,2,1,0:T(8,128)S(1)} %collective-permute-done.2.far.far_e) | copy-start | bytes 1769476
  44.4 20.6 %collective-permute-start.5 = (f32[3,48,8,128]{3,2,1,0:T(8,128)S(1)}, f32[3,48,8,128]{3,2,1,0:T(8,128)S(1)}, u32[]{:S(2)}, u32[]{:S(2)}) collective-permute-start(f32[3,48,8,128]{3,2,1,0:T(8,128)S(1)} %get-tuple-element.30), channel_id=1, source_target_pairs={{0,1},{1,2},{2,3},{4,5},{5,6},{6,7},{8,9},{9,10},{10,11},{12,13},{... | collective-permute-start | bytes 1769480 | tf_op jit(solution)/shard_map/ppermute | solution.py:607
  45.8 19.3 %collective-permute-start.6 = (f32[3,48,8,128]{3,2,1,0:T(8,128)S(1)}, f32[3,48,8,128]{3,2,1,0:T(8,128)S(1)}, u32[]{:S(2)}, u32[]{:S(2)}) collective-permute-start(f32[3,48,8,128]{3,2,1,0:T(8,128)S(1)} %get-tuple-element.31), channel_id=1, source_target_pairs={{1,0},{2,1},{3,2},{5,4},{6,5},{7,6},{9,8},{10,9},{11,10},{13,12},{... | collective-permute-start | bytes 1769480 | tf_op jit(solution)/shard_map/ppermute | solution.py:608
  47.1 17.9 %collective-permute-start.7 = (f32[72,1024]{1,0:T(8,128)}, f32[72,1024]{1,0:T(8,128)S(1)}, u32[]{:S(2)}, u32[]{:S(2)}) collective-permute-start(f32[72,1024]{1,0:T(8,128)} %get-tuple-element.27), channel_id=1, source_target_pairs={{0,1},{1,2},{2,3},{4,5},{5,6},{6,7},{8,9},{9,10},{10,11},{12,13},{... | collective-permute-start | bytes 884744 | tf_op jit(solution)/shard_map/ppermute | solution.py:556
  88.5 28.1 %copy-start.17 = (f32[8,128]{1,0:T(8,128)S(1)}, f32[8,128]{1,0:T(8,128)}, u32[]{:S(2)}) copy-start(f32[8,128]{1,0:T(8,128)} %get-tuple-element.47) | copy-start | bytes 12292
  88.5 28.1 %copy-start.19 = (f32[8,128]{1,0:T(8,128)S(1)}, f32[8,128]{1,0:T(8,128)}, u32[]{:S(2)}) copy-start(f32[8,128]{1,0:T(8,128)} %get-tuple-element.46) | copy-start | bytes 12292
  88.5 20.7 %collective-permute-start.9 = (f32[3,48,8,128]{3,2,1,0:T(8,128)}, f32[3,48,8,128]{3,2,1,0:T(8,128)S(1)}, u32[]{:S(2)}, u32[]{:S(2)}) collective-permute-start(f32[3,48,8,128]{3,2,1,0:T(8,128)} %get-tuple-element.36.own.own_e), channel_id=1, source_target_pairs={{0,4},{4,0},{8,12},{12,8},{16,20},{20,16},{24,28},{28,24},{1,5},{5... | collective-permute-start | bytes 1769480 | tf_op jit(solution)/shard_map/ppermute | solution.py:593
  90.6 18.9 %collective-permute-start.11 = (f32[3,48,8,128]{3,2,1,0:T(8,128)}, f32[3,48,8,128]{3,2,1,0:T(8,128)S(1)}, u32[]{:S(2)}, u32[]{:S(2)}) collective-permute-start(f32[3,48,8,128]{3,2,1,0:T(8,128)} %get-tuple-element.36.own.own_e), channel_id=1, source_target_pairs={{0,8},{8,16},{16,24},{12,4},{20,12},{28,20},{1,9},{9,17},{17,25},{... | collective-permute-start | bytes 1769480 | tf_op jit(solution)/shard_map/ppermute | solution.py:594
  95.8 34.7 %collective-permute-start.12 = (f32[3,80,8,128]{3,2,1,0:T(8,128)}, f32[3,80,8,128]{3,2,1,0:T(8,128)S(1)}, u32[]{:S(2)}, u32[]{:S(2)}) collective-permute-start(f32[3,80,8,128]{3,2,1,0:T(8,128)} %get-tuple-element.37.own_m), channel_id=1, source_target_pairs={{0,8},{8,16},{16,24},{12,4},{20,12},{28,20},{1,9},{9,17},{17,25},{... | collective-permute-start | bytes 2949128 | tf_op jit(solution)/shard_map/ppermute | solution.py:596
  98.0 32.6 %collective-permute-start.10 = (f32[3,80,8,128]{3,2,1,0:T(8,128)}, f32[3,80,8,128]{3,2,1,0:T(8,128)}, u32[]{:S(2)}, u32[]{:S(2)}) collective-permute-start(f32[3,80,8,128]{3,2,1,0:T(8,128)} %get-tuple-element.37.own_m), channel_id=1, source_target_pairs={{0,4},{4,0},{8,12},{12,8},{16,20},{20,16},{24,28},{28,24},{1,5},{5... | collective-permute-start | bytes 2949128 | tf_op jit(solution)/shard_map/ppermute | solution.py:595
  110.7 19.9 %collective-permute-start.13 = (f32[3,48,8,128]{3,2,1,0:T(8,128)S(1)}, f32[3,48,8,128]{3,2,1,0:T(8,128)}, u32[]{:S(2)}, u32[]{:S(2)}) collective-permute-start(f32[3,48,8,128]{3,2,1,0:T(8,128)S(1)} %get-tuple-element.41), channel_id=1, source_target_pairs={{0,1},{1,2},{2,3},{4,5},{5,6},{6,7},{8,9},{9,10},{10,11},{12,13},{... | collective-permute-start | bytes 1769480 | tf_op jit(solution)/shard_map/ppermute | solution.py:607
  114.8 15.8 %collective-permute-start.14 = (f32[3,48,8,128]{3,2,1,0:T(8,128)S(1)}, f32[3,48,8,128]{3,2,1,0:T(8,128)}, u32[]{:S(2)}, u32[]{:S(2)}) collective-permute-start(f32[3,48,8,128]{3,2,1,0:T(8,128)S(1)} %get-tuple-element.42), channel_id=1, source_target_pairs={{1,0},{2,1},{3,2},{5,4},{6,5},{7,6},{9,8},{10,9},{11,10},{13,12},{... | collective-permute-start | bytes 1769480 | tf_op jit(solution)/shard_map/ppermute | solution.py:608
  116.7 38.8 %collective-permute-start.15 = (f32[8,128]{1,0:T(8,128)S(1)}, f32[8,128]{1,0:T(8,128)S(1)}, u32[]{:S(2)}, u32[]{:S(2)}) collective-permute-start(f32[8,128]{1,0:T(8,128)S(1)} %add.50), channel_id=1, source_target_pairs={{0,4},{4,0},{8,12},{12,8},{16,20},{20,16},{24,28},{28,24},{1,5},{5... | collective-permute-start | bytes 12296 | tf_op jit(solution)/shard_map/ppermute | solution.py:639
  131.6 23.9 %copy-start.18 = (f32[8,128]{1,0:T(8,128)S(1)}, f32[8,128]{1,0:T(8,128)}, u32[]{:S(2)}) copy-start(f32[8,128]{1,0:T(8,128)} %get-tuple-element.51) | copy-start | bytes 12292
  156.2 3.7 %collective-permute-start.17 = (f32[2,8,128]{2,1,0:T(8,128)S(1)}, f32[2,8,128]{2,1,0:T(8,128)S(1)}, u32[]{:S(2)}, u32[]{:S(2)}) collective-permute-start(f32[2,8,128]{2,1,0:T(8,128)S(1)} %pad_maximum_fusion.2), channel_id=1, source_target_pairs={{0,2},{1,3},{2,0},{3,1},{4,6},{5,7},{6,4},{7,5},{8,10},{9,11},{10,... | collective-permute-start | bytes 24584 | tf_op jit(solution)/shard_map/ppermute | solution.py:586
  156.2 3.7 %collective-permute-start.18 = (f32[2,8,128]{2,1,0:T(8,128)S(1)}, f32[2,8,128]{2,1,0:T(8,128)S(1)}, u32[]{:S(2)}, u32[]{:S(2)}) collective-permute-start(f32[2,8,128]{2,1,0:T(8,128)S(1)} %pad_maximum_fusion.2), channel_id=1, source_target_pairs={{0,3},{1,0},{2,1},{3,2},{4,7},{5,4},{6,5},{7,6},{8,11},{9,8},{10,9... | collective-permute-start | bytes 24584 | tf_op jit(solution)/shard_map/ppermute | solution.py:586
  157.9 3.1 %collective-permute-start.16 = (f32[2,8,128]{2,1,0:T(8,128)S(1)}, f32[2,8,128]{2,1,0:T(8,128)S(1)}, u32[]{:S(2)}, u32[]{:S(2)}) collective-permute-start(f32[2,8,128]{2,1,0:T(8,128)S(1)} %pad_maximum_fusion.2), channel_id=1, source_target_pairs={{0,1},{1,2},{2,3},{3,0},{4,5},{5,6},{6,7},{7,4},{8,9},{9,10},{10,1... | collective-permute-start | bytes 24584 | tf_op jit(solution)/shard_map/ppermute | solution.py:586
  (16 other events, 144.0 us)

commit v5 on v4

--- a/solution.py
+++ b/solution.py
@@ -19,10 +19,11 @@
 LANE = 128
 NEAR = 2 * STEPS
 FAR = 4 * STEPS
-GROUPS = 4
-DEALS = 4
+GROUPS = 2
+DEALS = 8
 HALF = 0.5 * COURANT
-LEAD = 24
+LEAD = 32
+AT_ONCE = 2
 
 EDGE_W = 16
 
@@ -43,7 +44,7 @@
     count = rate.shape[0] - 2 * off
     north, south = halo - 1, count - halo
 
-    def one(_, carry):
+    def one(begin, end, _, carry):
         lane = lax.broadcasted_iota(jnp.int32, depth.shape[1:], 1)
         first, last = lane == 0, lane == LANE - 1
         flows, tops, pairs_a, pairs_b = {}, {}, {}, {}
@@ -66,18 +67,16 @@
             flows[r] = coef(r) * v if forward else v
 
         def lat(values, r):
-            return values[min(r + 1, count - 1)] - values[max(r - 1, 0)]
+            return values[min(r + 1, end - 1)] - values[max(r - 1, begin)]
 
         def open_a(r):
             if forward:
                 pairs_a[r] = turned(coef(r) * state[0, r])
             else:
-                mix = state[0, r] - rot(r) * state[1, r]
-                state[0, r] = mix
-                pairs_a[r] = turned(mix)
+                pairs_a[r] = turned(state[0, r] - rot(r) * state[1, r])
 
         def close_a(r):
-            if r + 1 < count:
+            if r + 1 < end:
                 prepare(r + 1)
             slope = raw_lon(pairs_a.pop(r), first, last) + lat(flows, r)
             old = state[2, r]
@@ -88,30 +87,33 @@
         def close_b(r):
             u, v = state[0, r], state[1, r]
             slope = raw_lon(pairs_b.pop(r), first, last)
-            if r + 1 < count:
+            if r + 1 < end:
                 above = state[2, r + 1]
             else:
                 above = tops[r]
-            rise = above - state[2, max(r - 1, 0)]
+            rise = above - state[2, max(r - 1, begin)]
             if forward:
                 u = u + rot(r) * v - slope
                 state[0, r] = u
                 state[1, r] = v - rot(r) * u - rise
             else:
+                u = u - rot(r) * v
                 state[0, r] = u + coef(r) * slope
                 state[1, r] = v + rot(r) * u + coef(r) * rise
 
-        prepare(0)
-        for r in range(-LEAD, count + LEAD):
-            if 0 <= r + LEAD < count:
+        prepare(begin)
+        for r in range(begin - LEAD, end + LEAD):
+            if begin <= r + LEAD < end:
                 open_a(r + LEAD)
-            if 0 <= r < count:
+            if begin <= r < end:
                 close_a(r)
-            if 0 <= r - LEAD < count:
+            if begin <= r - LEAD < end:
                 close_b(r - LEAD)
         return carry
 
-    lax.fori_loop(0, STEPS, one, 0)
+    for n in range(0, STEPS, AT_ONCE):
+        trips = min(AT_ONCE, STEPS - n)
+        lax.fori_loop(0, trips, functools.partial(one, 2 * n, count - 2 * n), 0)
 
 
 def over(count, body, block=8):
@@ -442,7 +444,7 @@
         def total(r):
             at = pl.ds(n * rows + r, 8)
             for group in (a_acc, b_acc):
-                group[0][at] = (group[0][at] + group[1][at]) + (group[2][at] + group[3][at])
+                group[0][at] = group[0][at] + group[1][at]
 
         over(rows, total)
         for k, (out, group) in enumerate(((a_out, a_acc), (b_out, b_acc))):
@@ -595,7 +597,7 @@
         mid_m = lax.ppermute(inner, "tm", swap)
         far_m = lax.ppermute(inner, "tm", shift)
         if away:
-            _, mid_e = lax.optimization_barrier((to_south, mid_e))
+            fixed_n, fixed_s, mid_e = lax.optimization_barrier((fixed_n, fixed_s, mid_e))
             to_south, to_north = pack(edge, mid_e, far_e)
             to_south, other_list = lax.optimization_barrier((to_south, other_list))
             obs_a, obs_b, const = deposit(place, other_list)

time: 162 us -> 160 us (0.988)
  starting transfers between devices: 39.3 us -> 36.1 us
  waiting for transfers between devices: 40.4 us -> 43.5 us
  Pallas kernels: 71.5 us -> 68.6 us
    ppermute x2, waiting for transfers between devices: 6.32 us -> 3.09 us  [per_device(): mid_e = lax.ppermute(edge, 'tm', swap)]
    ppermute x1, waiting for transfers between devices: 0.01 us -> 2.51 us  [per_device(): fixed_s = lax.ppermute(to_north, 'space', northward)]
    ppermute x1, waiting for transfers between devices: 19.6 us -> 22 us  [per_device(): other_list = lax.ppermute(own_list, 'tm', swap)]
    ppermute x1, starting transfers between devices: 4.74 us -> 2.41 us  [per_device(): fixed_n = lax.ppermute(to_south, 'space', southward)]
    pallas_call x2, Pallas kernels: 46.2 us -> 44.2 us  [per_device(): round_call(len(outs), outs)]
  transfers between devices with their start and end apart: 19 -> 19, of which waited for: 6 -> 7; matrix products, arithmetic and copies ran while one was open for 1% -> 2% of each run, Pallas kernels for 30% -> 29%
where the time goes in v5:
time: 160 us; the launch traced here: 159 us
  Pallas kernels  68.6 us (43%)
  waiting for transfers between devices  43.5 us (27%)
  starting transfers between devices  36.1 us (23%)
  local copies, waits for them, and re-layouts  6.77 us (4%)
  other arithmetic  2.59 us (2%)
  between operations  1.74 us (1%)
    pallas_call x2, Pallas kernels, per_device(): round_call(len(outs), outs)  44.2 us
    ppermute x1, waiting for transfers between devices, per_device(): other_list = lax.ppermute(own_list, 'tm', swap)  22 us
    pallas_call x1, Pallas kernels, per_device(): obs_a, obs_b, const = deposit(place, other_list)  12.4 us
    ppermute x2, waiting for transfers between devices, per_device(): far_m = lax.ppermute(inner, 'tm', shift)  11.9 us
    pallas_call x1, Pallas kernels, per_device(): obs_a, obs_b, const = deposit(place, own_list)  11 us
    ppermute x2, starting transfers between devices, per_device(): mid_e = lax.ppermute(edge, 'tm', swap)  6.99 us
    ppermute x2, starting transfers between devices, per_device(): far_e = lax.ppermute(edge, 'tm', shift)  6.5 us
    ppermute x2, starting transfers between devices, per_device(): from_north = lax.ppermute(to_south, 'space', southward)  5.36 us
  transfers between devices with their start and end apart: 19, of which 7 were waited for; matrix products, arithmetic and copies ran while one was open for 2% of the time, Pallas kernels for 29%

profile of v5, /device:TPU:0, one launch (start us, length us, event | category | flops | bytes accessed | tf_op | source)
XLA Modules:
  0.0 159.3 jit_solution(3972082572619105058)
XLA Ops:
  0.6 1.4 copy-done
  3.9 2.4 %collective-permute-start = (f32[72,1024]{1,0:T(8,128)S(1)}, f32[72,1024]{1,0:T(8,128)S(1)}, u32[]{:S(2)}, u32[]{:S(2)}) collective-permute-start(f32[72,1024]{1,0:T(8,128)S(1)} %get-tuple-element.29), channel_id=1, source_target_pairs={{0,1},{1,2},{2,3},{4,5},{5,6},{6,7},{8,9},{9,10},{10,11},{12,13},{... | collective-permute-start | bytes 884744 | tf_op jit(solution)/shard_map/ppermute | solution.py:558
  6.8 1.3 collective-permute-start.4
  8.1 4.6 %collective-permute-start.2 = (f32[3,48,8,128]{3,2,1,0:T(8,128)S(1)}, f32[3,48,8,128]{3,2,1,0:T(8,128)S(1)}, u32[]{:S(2)}, u32[]{:S(2)}) collective-permute-start(f32[3,48,8,128]{3,2,1,0:T(8,128)S(1)} %pad_maximum_fusion.own.own_e), channel_id=1, source_target_pairs={{0,4},{4,0},{8,12},{12,8},{16,20},{20,16},{24,28},{28,24},{1,5},{5... | collective-permute-start | bytes 1769480 | tf_op jit(solution)/shard_map/ppermute | solution.py:595
  13.8 1.3 collective-permute-start.5
  15.1 3.2 %collective-permute-start.3 = (f32[3,80,8,128]{3,2,1,0:T(8,128)}, f32[3,80,8,128]{3,2,1,0:T(8,128)}, u32[]{:S(2)}, u32[]{:S(2)}) collective-permute-start(f32[3,80,8,128]{3,2,1,0:T(8,128)} %slice.14.own_m), channel_id=1, source_target_pairs={{0,4},{4,0},{8,12},{12,8},{16,20},{20,16},{24,28},{28,24},{1,5},{5... | collective-permute-start | bytes 2949128 | tf_op jit(solution)/shard_map/ppermute | solution.py:597
  18.9 1.3 collective-permute-start.1
  20.3 2.5 %collective-permute-done.1.fixed_s = f32[72,1024]{1,0:T(8,128)S(1)} collective-permute-done((f32[72,1024]{1,0:T(8,128)S(1)}, f32[72,1024]{1,0:T(8,128)S(1)}, u32[]{:S(2)}, u32[]{:S(2)}) %collective-permute-start.1) | collective-permute-done | bytes 294944 | tf_op jit(solution)/shard_map/ppermute | solution.py:559
  23.1 3.1 %collective-permute-done.2.mid.mid_e = f32[3,48,8,128]{3,2,1,0:T(8,128)S(1)} collective-permute-done((f32[3,48,8,128]{3,2,1,0:T(8,128)S(1)}, f32[3,48,8,128]{3,2,1,0:T(8,128)S(1)}, u32[]{:S(2)}, u32[]{:S(2)}) %collective-permute-start.2) | collective-permute-done | bytes 589856 | tf_op jit(solution)/shard_map/ppermute | solution.py:595
  26.2 22.0 %collective-permute-done.6.entries = f32[3,32,128]{2,1,0:T(8,128)S(1)} collective-permute-done((f32[3,32,128]{2,1,0:T(8,128)S(1)}, f32[3,32,128]{2,1,0:T(8,128)S(1)}, u32[]{:S(2)}, u32[]{:S(2)}) %collective-permute-start.6) | collective-permute-done | bytes 49184 | tf_op jit(solution)/shard_map/ppermute | solution.py:494
  48.3 2.5 %collective-permute-start.7 = (f32[3,48,8,128]{3,2,1,0:T(8,128)S(1)}, f32[3,48,8,128]{3,2,1,0:T(8,128)S(1)}, u32[]{:S(2)}, u32[]{:S(2)}) collective-permute-start(f32[3,48,8,128]{3,2,1,0:T(8,128)S(1)} %get-tuple-element.33), channel_id=1, source_target_pairs={{0,1},{1,2},{2,3},{4,5},{5,6},{6,7},{8,9},{9,10},{10,11},{12,13},{... | collective-permute-start | bytes 1769480 | tf_op jit(solution)/shard_map/ppermute | solution.py:609
  50.8 1.3 collective-permute-start.8
  52.8 12.4 %shard_map.95 = (f32[3,128,8,128]{3,2,1,0:T(8,128)}, f32[3,128,8,128]{3,2,1,0:T(8,128)}, f32[8,128]{1,0:T(8,128)}) custom-call(s32[1]{0:T(128)} %bitcast.12.place, f32[3,32,128]{2,1,0:T(8,128)} %copy-done.20), custom_call_target="tpu_custom_call" | custom-call | flops 20000000 | tf_op jit(solution)/shard_map/pallas_call | solution.py:603
  66.1 21.3 %shard_map.96 = (f32[3,48,8,128]{3,2,1,0:T(8,128)}, f32[3,80,8,128]{3,2,1,0:T(8,128)}, f32[8,128]{1,0:T(8,128)}) custom-call(s32[1]{0:T(128)} %bitcast.5.own_lo, f32[4]{0:T(128)} %add_convert_fusion.1.flags, f32[3,48,8,128]{3,2,1,0:T(8,128)} %copy-done.1, f32[3,80,8,128]{3,2,1,0:T(8,128)} %slice.14.own_m, f32[3,48,8,128]{3,2,1,0:T(8,128)} %copy-done.4, ...), custom_call_target="tpu_custom_call" | custom-call | flops 45000000 | tf_op jit(solution)/shard_map/pallas_call | solution.py:619
  87.5 2.4 %collective-permute-start.9 = (f32[3,48,8,128]{3,2,1,0:T(8,128)}, f32[3,48,8,128]{3,2,1,0:T(8,128)S(1)}, u32[]{:S(2)}, u32[]{:S(2)}) collective-permute-start(f32[3,48,8,128]{3,2,1,0:T(8,128)} %get-tuple-element.40.own.own_e), channel_id=1, source_target_pairs={{0,4},{4,0},{8,12},{12,8},{16,20},{20,16},{24,28},{28,24},{1,5},{5... | collective-permute-start | bytes 1769480 | tf_op jit(solution)/shard_map/ppermute | solution.py:595
  89.8 5.2 %collective-permute-start.11 = (f32[3,48,8,128]{3,2,1,0:T(8,128)}, f32[3,48,8,128]{3,2,1,0:T(8,128)S(1)}, u32[]{:S(2)}, u32[]{:S(2)}) collective-permute-start(f32[3,48,8,128]{3,2,1,0:T(8,128)} %get-tuple-element.40.own.own_e), channel_id=1, source_target_pairs={{0,8},{8,16},{16,24},{12,4},{20,12},{28,20},{1,9},{9,17},{17,25},{... | collective-permute-start | bytes 1769480 | tf_op jit(solution)/shard_map/ppermute | solution.py:596
  95.1 1.9 %collective-permute-start.12 = (f32[3,80,8,128]{3,2,1,0:T(8,128)}, f32[3,80,8,128]{3,2,1,0:T(8,128)S(1)}, u32[]{:S(2)}, u32[]{:S(2)}) collective-permute-start(f32[3,80,8,128]{3,2,1,0:T(8,128)} %get-tuple-element.41.own_m), channel_id=1, source_target_pairs={{0,8},{8,16},{16,24},{12,4},{20,12},{28,20},{1,9},{9,17},{17,25},{... | collective-permute-start | bytes 2949128 | tf_op jit(solution)/shard_map/ppermute | solution.py:598
  97.1 11.0 %shard_map.97 = (f32[3,128,8,128]{3,2,1,0:T(8,128)}, f32[3,128,8,128]{3,2,1,0:T(8,128)}, f32[8,128]{1,0:T(8,128)}) custom-call(s32[1]{0:T(128)} %bitcast.12.place, f32[3,32,128]{2,1,0:T(8,128)} %copy-done.13), custom_call_target="tpu_custom_call" | custom-call | flops 20000000 | tf_op jit(solution)/shard_map/pallas_call | solution.py:606
  110.2 2.8 %collective-permute-start.13 = (f32[3,48,8,128]{3,2,1,0:T(8,128)S(1)}, f32[3,48,8,128]{3,2,1,0:T(8,128)}, u32[]{:S(2)}, u32[]{:S(2)}) collective-permute-start(f32[3,48,8,128]{3,2,1,0:T(8,128)S(1)} %get-tuple-element.45), channel_id=1, source_target_pairs={{0,1},{1,2},{2,3},{4,5},{5,6},{6,7},{8,9},{9,10},{10,11},{12,13},{... | collective-permute-start | bytes 1769480 | tf_op jit(solution)/shard_map/ppermute | solution.py:609
  113.0 1.5 collective-permute-start.14
  115.1 2.8 %collective-permute-start.15 = (f32[8,128]{1,0:T(8,128)S(1)}, f32[8,128]{1,0:T(8,128)S(1)}, u32[]{:S(2)}, u32[]{:S(2)}) collective-permute-start(f32[8,128]{1,0:T(8,128)S(1)} %add.50), channel_id=1, source_target_pairs={{0,4},{4,0},{8,12},{12,8},{16,20},{20,16},{24,28},{28,24},{1,5},{5... | collective-permute-start | bytes 12296 | tf_op jit(solution)/shard_map/ppermute | solution.py:641
  117.9 11.9 %collective-permute-done.12.far_m = f32[3,80,8,128]{3,2,1,0:T(8,128)S(1)} collective-permute-done((f32[3,80,8,128]{3,2,1,0:T(8,128)}, f32[3,80,8,128]{3,2,1,0:T(8,128)S(1)}, u32[]{:S(2)}, u32[]{:S(2)}) %collective-permute-start.12) | collective-permute-done | bytes 983072 | tf_op jit(solution)/shard_map/ppermute | solution.py:598
  130.8 22.9 %shard_map.98 = (f32[3,128,1024]{2,1,0:T(8,128)}, f32[8,128]{1,0:T(8,128)}) custom-call(s32[1]{0:T(128)} %bitcast.own_lo, f32[4]{0:T(128)} %add_convert_fusion.flags, f32[3,48,8,128]{3,2,1,0:T(8,128)} %get-tuple-element.40.own.own_e, f32[3,80,8,128]{3,2,1,0:T(8,128)} %get-tuple-element.41.own_m, f32[3,48,8,128]{3,2,1,0:T(8,128)} %copy-done.6, ...), custom_call_target="tpu_custom_call" | custom-call | flops 45000000 | tf_op jit(solution)/shard_map/pallas_call | solution.py:619
  155.6 2.5 %collective-permute-done.17 = f32[2,8,128]{2,1,0:T(8,128)S(1)} collective-permute-done((f32[2,8,128]{2,1,0:T(8,128)S(1)}, f32[2,8,128]{2,1,0:T(8,128)S(1)}, u32[]{:S(2)}, u32[]{:S(2)}) %collective-permute-start.17) | collective-permute-done | bytes 8224 | tf_op jit(solution)/shard_map/ppermute | solution.py:588
  (78 shorter events, 12.0 us)
Async XLA Ops:
  3.9 15.0 %collective-permute-start = (f32[72,1024]{1,0:T(8,128)S(1)}, f32[72,1024]{1,0:T(8,128)S(1)}, u32[]{:S(2)}, u32[]{:S(2)}) collective-permute-start(f32[72,1024]{1,0:T(8,128)S(1)} %get-tuple-element.29), channel_id=1, source_target_pairs={{0,1},{1,2},{2,3},{4,5},{5,6},{6,7},{8,9},{9,10},{10,11},{12,13},{... | collective-permute-start | bytes 884744 | tf_op jit(solution)/shard_map/ppermute | solution.py:558
  6.8 19.3 %collective-permute-start.4 = (f32[3,48,8,128]{3,2,1,0:T(8,128)S(1)}, f32[3,48,8,128]{3,2,1,0:T(8,128)S(1)}, u32[]{:S(2)}, u32[]{:S(2)}) collective-permute-start(f32[3,48,8,128]{3,2,1,0:T(8,128)S(1)} %pad_maximum_fusion.own.own_e), channel_id=1, source_target_pairs={{8,0},{16,8},{24,16},{4,12},{12,20},{20,28},{9,1},{17,9},{25,17},{... | collective-permute-start | bytes 1769480 | tf_op jit(solution)/shard_map/ppermute | solution.py:596
  8.1 18.0 %collective-permute-start.2 = (f32[3,48,8,128]{3,2,1,0:T(8,128)S(1)}, f32[3,48,8,128]{3,2,1,0:T(8,128)S(1)}, u32[]{:S(2)}, u32[]{:S(2)}) collective-permute-start(f32[3,48,8,128]{3,2,1,0:T(8,128)S(1)} %pad_maximum_fusion.own.own_e), channel_id=1, source_target_pairs={{0,4},{4,0},{8,12},{12,8},{16,20},{20,16},{24,28},{28,24},{1,5},{5... | collective-permute-start | bytes 1769480 | tf_op jit(solution)/shard_map/ppermute | solution.py:595
  13.8 51.4 %collective-permute-start.5 = (f32[3,80,8,128]{3,2,1,0:T(8,128)}, f32[3,80,8,128]{3,2,1,0:T(8,128)}, u32[]{:S(2)}, u32[]{:S(2)}) collective-permute-start(f32[3,80,8,128]{3,2,1,0:T(8,128)} %slice.14.own_m), channel_id=1, source_target_pairs={{8,0},{16,8},{24,16},{4,12},{12,20},{20,28},{9,1},{17,9},{25,17},{... | collective-permute-start | bytes 2949128 | tf_op jit(solution)/shard_map/ppermute | solution.py:598
  15.1 50.1 %collective-permute-start.3 = (f32[3,80,8,128]{3,2,1,0:T(8,128)}, f32[3,80,8,128]{3,2,1,0:T(8,128)}, u32[]{:S(2)}, u32[]{:S(2)}) collective-permute-start(f32[3,80,8,128]{3,2,1,0:T(8,128)} %slice.14.own_m), channel_id=1, source_target_pairs={{0,4},{4,0},{8,12},{12,8},{16,20},{20,16},{24,28},{28,24},{1,5},{5... | collective-permute-start | bytes 2949128 | tf_op jit(solution)/shard_map/ppermute | solution.py:597
  18.9 47.2 %copy-start.9 = (f32[72,1024]{1,0:T(8,128)}, f32[72,1024]{1,0:T(8,128)S(1)}, u32[]{:S(2)}) copy-start(f32[72,1024]{1,0:T(8,128)S(1)} %collective-permute-done.fixed_n) | copy-start | bytes 884740
  18.9 3.9 %collective-permute-start.1 = (f32[72,1024]{1,0:T(8,128)S(1)}, f32[72,1024]{1,0:T(8,128)S(1)}, u32[]{:S(2)}, u32[]{:S(2)}) collective-permute-start(f32[72,1024]{1,0:T(8,128)S(1)} %get-tuple-element.30), channel_id=1, source_target_pairs={{1,0},{2,1},{3,2},{5,4},{6,5},{7,6},{9,8},{10,9},{11,10},{13,12},{... | collective-permute-start | bytes 884744 | tf_op jit(solution)/shard_map/ppermute | solution.py:559
  20.3 31.9 %copy-start.13 = (f32[3,32,128]{2,1,0:T(8,128)}, f32[3,32,128]{2,1,0:T(8,128)S(1)}, u32[]{:S(2)}) copy-start(f32[3,32,128]{2,1,0:T(8,128)S(1)} %pad_maximum_fusion.1.entries) | copy-start | bytes 147460
  22.8 43.3 %copy-start.10 = (f32[72,1024]{1,0:T(8,128)}, f32[72,1024]{1,0:T(8,128)S(1)}, u32[]{:S(2)}) copy-start(f32[72,1024]{1,0:T(8,128)S(1)} %collective-permute-done.1.fixed_s) | copy-start | bytes 884740
  22.8 25.5 %collective-permute-start.6 = (f32[3,32,128]{2,1,0:T(8,128)S(1)}, f32[3,32,128]{2,1,0:T(8,128)S(1)}, u32[]{:S(2)}, u32[]{:S(2)}) collective-permute-start(f32[3,32,128]{2,1,0:T(8,128)S(1)} %pad_maximum_fusion.1.entries), channel_id=1, source_target_pairs={{0,4},{4,0},{8,12},{12,8},{16,20},{20,16},{24,28},{28,24},{1,5},{5... | collective-permute-start | bytes 147464 | tf_op jit(solution)/shard_map/ppermute | solution.py:494
  26.1 39.9 %copy-start.4 = (f32[3,48,8,128]{3,2,1,0:T(8,128)}, f32[3,48,8,128]{3,2,1,0:T(8,128)S(1)}, u32[]{:S(2)}) copy-start(f32[3,48,8,128]{3,2,1,0:T(8,128)S(1)} %collective-permute-done.2.mid.mid_e) | copy-start | bytes 1769476
  26.2 39.9 %copy-start.3 = (f32[3,48,8,128]{3,2,1,0:T(8,128)}, f32[3,48,8,128]{3,2,1,0:T(8,128)S(1)}, u32[]{:S(2)}) copy-start(f32[3,48,8,128]{3,2,1,0:T(8,128)S(1)} %collective-permute-done.4.far.far_e) | copy-start | bytes 1769476
  48.3 16.9 %collective-permute-start.7 = (f32[3,48,8,128]{3,2,1,0:T(8,128)S(1)}, f32[3,48,8,128]{3,2,1,0:T(8,128)S(1)}, u32[]{:S(2)}, u32[]{:S(2)}) collective-permute-start(f32[3,48,8,128]{3,2,1,0:T(8,128)S(1)} %get-tuple-element.33), channel_id=1, source_target_pairs={{0,1},{1,2},{2,3},{4,5},{5,6},{6,7},{8,9},{9,10},{10,11},{12,13},{... | collective-permute-start | bytes 1769480 | tf_op jit(solution)/shard_map/ppermute | solution.py:609
  50.8 14.4 %collective-permute-start.8 = (f32[3,48,8,128]{3,2,1,0:T(8,128)S(1)}, f32[3,48,8,128]{3,2,1,0:T(8,128)}, u32[]{:S(2)}, u32[]{:S(2)}) collective-permute-start(f32[3,48,8,128]{3,2,1,0:T(8,128)S(1)} %get-tuple-element.34), channel_id=1, source_target_pairs={{1,0},{2,1},{3,2},{5,4},{6,5},{7,6},{9,8},{10,9},{11,10},{13,12},{... | collective-permute-start | bytes 1769480 | tf_op jit(solution)/shard_map/ppermute | solution.py:610
  87.5 20.6 %collective-permute-start.9 = (f32[3,48,8,128]{3,2,1,0:T(8,128)}, f32[3,48,8,128]{3,2,1,0:T(8,128)S(1)}, u32[]{:S(2)}, u32[]{:S(2)}) collective-permute-start(f32[3,48,8,128]{3,2,1,0:T(8,128)} %get-tuple-element.40.own.own_e), channel_id=1, source_target_pairs={{0,4},{4,0},{8,12},{12,8},{16,20},{20,16},{24,28},{28,24},{1,5},{5... | collective-permute-start | bytes 1769480 | tf_op jit(solution)/shard_map/ppermute | solution.py:595
  89.8 19.2 %collective-permute-start.11 = (f32[3,48,8,128]{3,2,1,0:T(8,128)}, f32[3,48,8,128]{3,2,1,0:T(8,128)S(1)}, u32[]{:S(2)}, u32[]{:S(2)}) collective-permute-start(f32[3,48,8,128]{3,2,1,0:T(8,128)} %get-tuple-element.40.own.own_e), channel_id=1, source_target_pairs={{0,8},{8,16},{16,24},{12,4},{20,12},{28,20},{1,9},{9,17},{17,25},{... | collective-permute-start | bytes 1769480 | tf_op jit(solution)/shard_map/ppermute | solution.py:596
  95.1 34.8 %collective-permute-start.12 = (f32[3,80,8,128]{3,2,1,0:T(8,128)}, f32[3,80,8,128]{3,2,1,0:T(8,128)S(1)}, u32[]{:S(2)}, u32[]{:S(2)}) collective-permute-start(f32[3,80,8,128]{3,2,1,0:T(8,128)} %get-tuple-element.41.own_m), channel_id=1, source_target_pairs={{0,8},{8,16},{16,24},{12,4},{20,12},{28,20},{1,9},{9,17},{17,25},{... | collective-permute-start | bytes 2949128 | tf_op jit(solution)/shard_map/ppermute | solution.py:598
  97.0 32.8 %collective-permute-start.10 = (f32[3,80,8,128]{3,2,1,0:T(8,128)}, f32[3,80,8,128]{3,2,1,0:T(8,128)}, u32[]{:S(2)}, u32[]{:S(2)}) collective-permute-start(f32[3,80,8,128]{3,2,1,0:T(8,128)} %get-tuple-element.41.own_m), channel_id=1, source_target_pairs={{0,4},{4,0},{8,12},{12,8},{16,20},{20,16},{24,28},{28,24},{1,5},{5... | collective-permute-start | bytes 2949128 | tf_op jit(solution)/shard_map/ppermute | solution.py:597
  110.2 19.6 %collective-permute-start.13 = (f32[3,48,8,128]{3,2,1,0:T(8,128)S(1)}, f32[3,48,8,128]{3,2,1,0:T(8,128)}, u32[]{:S(2)}, u32[]{:S(2)}) collective-permute-start(f32[3,48,8,128]{3,2,1,0:T(8,128)S(1)} %get-tuple-element.45), channel_id=1, source_target_pairs={{0,1},{1,2},{2,3},{4,5},{5,6},{6,7},{8,9},{9,10},{10,11},{12,13},{... | collective-permute-start | bytes 1769480 | tf_op jit(solution)/shard_map/ppermute | solution.py:609
  113.0 16.8 %collective-permute-start.14 = (f32[3,48,8,128]{3,2,1,0:T(8,128)S(1)}, f32[3,48,8,128]{3,2,1,0:T(8,128)}, u32[]{:S(2)}, u32[]{:S(2)}) collective-permute-start(f32[3,48,8,128]{3,2,1,0:T(8,128)S(1)} %get-tuple-element.46), channel_id=1, source_target_pairs={{1,0},{2,1},{3,2},{5,4},{6,5},{7,6},{9,8},{10,9},{11,10},{13,12},{... | collective-permute-start | bytes 1769480 | tf_op jit(solution)/shard_map/ppermute | solution.py:610
  115.1 38.7 %collective-permute-start.15 = (f32[8,128]{1,0:T(8,128)S(1)}, f32[8,128]{1,0:T(8,128)S(1)}, u32[]{:S(2)}, u32[]{:S(2)}) collective-permute-start(f32[8,128]{1,0:T(8,128)S(1)} %add.50), channel_id=1, source_target_pairs={{0,4},{4,0},{8,12},{12,8},{16,20},{20,16},{24,28},{28,24},{1,5},{5... | collective-permute-start | bytes 12296 | tf_op jit(solution)/shard_map/ppermute | solution.py:641
  154.4 3.7 %collective-permute-start.17 = (f32[2,8,128]{2,1,0:T(8,128)S(1)}, f32[2,8,128]{2,1,0:T(8,128)S(1)}, u32[]{:S(2)}, u32[]{:S(2)}) collective-permute-start(f32[2,8,128]{2,1,0:T(8,128)S(1)} %pad_maximum_fusion.2), channel_id=1, source_target_pairs={{0,2},{1,3},{2,0},{3,1},{4,6},{5,7},{6,4},{7,5},{8,10},{9,11},{10,... | collective-permute-start | bytes 24584 | tf_op jit(solution)/shard_map/ppermute | solution.py:588
  155.0 3.1 %collective-permute-start.18 = (f32[2,8,128]{2,1,0:T(8,128)S(1)}, f32[2,8,128]{2,1,0:T(8,128)S(1)}, u32[]{:S(2)}, u32[]{:S(2)}) collective-permute-start(f32[2,8,128]{2,1,0:T(8,128)S(1)} %pad_maximum_fusion.2), channel_id=1, source_target_pairs={{0,3},{1,0},{2,1},{3,2},{4,7},{5,4},{6,5},{7,6},{8,11},{9,8},{10,9... | collective-permute-start | bytes 24584 | tf_op jit(solution)/shard_map/ppermute | solution.py:588
  155.6 3.1 %collective-permute-start.16 = (f32[2,8,128]{2,1,0:T(8,128)S(1)}, f32[2,8,128]{2,1,0:T(8,128)S(1)}, u32[]{:S(2)}, u32[]{:S(2)}) collective-permute-start(f32[2,8,128]{2,1,0:T(8,128)S(1)} %pad_maximum_fusion.2), channel_id=1, source_target_pairs={{0,1},{1,2},{2,3},{3,0},{4,5},{5,6},{6,7},{7,4},{8,9},{9,10},{10,1... | collective-permute-start | bytes 24584 | tf_op jit(solution)/shard_map/ppermute | solution.py:588
  (16 other events, 191.9 us)
